TPU v7x, 32 devices: a whole 2x2x4 slice. The times are simulated.
32 devices in a mesh: dp: 16 (over z, y, x), rep: 2 (over core).
Axes of the slice: x: 2, y: 2, z: 4, core: 2. Of those that a mesh axis runs over, the one named last changes fastest.
Arguments:
- ids: int32 [8192], P(('dp', 'rep')), may hold values from 0 to 65520
- counts: int32 [32], P(('dp', 'rep')), may hold values from 1 to 256, as said below
- hash_scale: int32 [512], replicated, may hold values from 1 to 32767
- hash_shift: int32 [512], replicated, may hold values from 0 to 65520
- w_code: bfloat16 [512, 1024], replicated, may hold values from -0.25 to 0.25
- norm_gain: float32 [1024], replicated, may hold values from 0.5 to 1.5
- norm_bias: float32 [1024], replicated, may hold values from -3 to 3
- w_out: bfloat16 [1024, 128], replicated, may hold values from -0.1875 to 0.1875
- out_bias: float32 [128], replicated, may hold values from -3 to 3
- cotangent: bfloat16 [8192, 128], P(('dp', 'rep')), may hold values from -6 to 6
Outputs:
- embeddings: bfloat16 [8192, 128], P(('dp', 'rep'))
- grad_code_t: float32 [1024, 512], P(('dp', 'rep'))
- grad_out: float32 [1024, 128], P(('dp', 'rep'))
- grad_gain: float32 [1024], replicated
- grad_bias: float32 [1024], replicated
Inputs may be any that keep to these rules, and one draw needn't show every extreme that they name: Each device has 1 to 256 live slots, the first ones of its slots; the counts of the devices of one rep index sum to exactly 1024, and in each such group one device has exactly 256.
All inputs are finite; a program needn't handle non-finite values.
Results may differ from a plain program's by a relative error of at most 0.006.
Values may be sent and summed in bfloat16 or wider, within the bound.
No kernel may reach another device: no remote copies, remote signals or barrier semaphores. Data moves between devices by JAX's collectives and lax.ppermute only.
A program may use at most 64 MiB of HBM per device.

v0:
```python
import math

import jax
import jax.numpy as jnp
from jax import lax
from jax.sharding import PartitionSpec as P

BLOCK = 256


modulus = 65521
epsilon = 1e-05


def hashed(ident, hash_scale, hash_shift):
    resid = ident % modulus
    bucket = (hash_scale[None, :] * resid[:, None] + hash_shift[None, :]) % modulus
    return (bucket.astype(jnp.float32) * (2.0 / (modulus - 1)) - 1.0).astype(jnp.bfloat16)


def mish_parts(gated):
    softer = jax.nn.softplus(gated)
    tangent = jnp.tanh(softer)
    return (gated * tangent, tangent + gated * (1.0 - tangent * tangent) * jax.nn.sigmoid(gated))


def owner_rows(dpre_rows, row_ids, hash_scale, hash_shift):
    dp_count = lax.axis_size("dp")
    rep_count = lax.axis_size("rep")
    device_count = dp_count * rep_count
    row_count = dpre_rows.shape[0]
    columns = lax.all_to_all(
        lax.all_to_all(dpre_rows, "dp", split_axis=1, concat_axis=0, tiled=True),
        "rep",
        split_axis=1,
        concat_axis=0,
        tiled=True,
    )
    everyone = lax.all_gather(row_ids, ("dp", "rep"), axis=0, tiled=True)
    everyone = everyone.reshape(dp_count, rep_count, row_count).transpose(1, 0, 2).reshape(-1)
    group = math.gcd(device_count, max(1, 8192 // row_count))
    step_rows = group * row_count

    def accumulate(index, grad_rows):
        start = index * step_rows
        id_block = lax.dynamic_slice_in_dim(everyone, start, step_rows, 0)
        col_block = lax.dynamic_slice_in_dim(columns, start, step_rows, 0)
        code_block = hashed(id_block, hash_scale, hash_shift)
        return grad_rows + lax.dot_general(
            col_block, code_block, (((0,), (0,)), ((), ())), preferred_element_type=jnp.float32
        )

    start_rows = jnp.zeros((columns.shape[1], hash_scale.shape[0]), jnp.float32)
    return lax.fori_loop(0, device_count // group, accumulate, start_rows)


def train_rows(
    code_rows,
    cot_rows,
    live_count,
    row_ids,
    hash_scale,
    hash_shift,
    w_code,
    norm_gain,
    norm_bias,
    w_out,
    out_bias,
):
    row_count = code_rows.shape[0]
    hidden = w_code.shape[1]
    width = w_out.shape[1]
    live_flags = jnp.arange(row_count, dtype=jnp.int32) < live_count
    block_total = (live_count + BLOCK - 1) // BLOCK
    zero_row = jnp.zeros((hidden,), jnp.float32)

    def first_pass(block_index, state_carry):
        stored, sum_hidden, sum_square = state_carry
        keep_rows = live_flags[:, None]
        preact = jnp.dot(code_rows, w_code, preferred_element_type=jnp.float32)
        masked = jnp.where(keep_rows, preact, 0.0)
        stored = preact
        return (stored, sum_hidden + masked.sum(0), sum_square + (masked * masked).sum(0))

    stored, sum_hidden, sum_square = lax.fori_loop(
        0,
        block_total,
        first_pass,
        (jnp.zeros((row_count, hidden), jnp.float32), zero_row, zero_row),
    )
    sum_hidden, sum_square, total = lax.psum(
        (sum_hidden, sum_square, live_count.astype(jnp.float32)), ("dp", "rep")
    )
    feature_mean = sum_hidden / total
    inv_std = lax.rsqrt(sum_square / total - feature_mean * feature_mean + epsilon)
    loss_scale = lax.rsqrt(total)

    def second_pass(block_index, state_carry):
        stored, dvalue_rows, embedded, grad_gain, grad_bias, grad_out = state_carry
        keep_rows = live_flags[:, None]
        normed = (stored - feature_mean) * inv_std
        act_full, mish_slope = mish_parts(normed * norm_gain + norm_bias)
        activation = act_full.astype(jnp.bfloat16)
        out_rows = jnp.dot(activation, w_out, preferred_element_type=jnp.float32) + out_bias
        out_rows = jnp.where(keep_rows, out_rows, 0.0).astype(jnp.bfloat16)
        delta_rows = jnp.where(keep_rows, cot_rows.astype(jnp.float32) * loss_scale, 0.0).astype(
            jnp.bfloat16
        )
        grad_act = lax.dot_general(
            delta_rows, w_out, (((1,), (1,)), ((), ())), preferred_element_type=jnp.float32
        )
        dvalue = grad_act * mish_slope
        stored = normed
        dvalue_rows = dvalue
        embedded = out_rows
        out_part = lax.dot_general(
            activation, delta_rows, (((0,), (0,)), ((), ())), preferred_element_type=jnp.float32
        )
        return (
            stored,
            dvalue_rows,
            embedded,
            grad_gain + (dvalue * normed).sum(0),
            grad_bias + dvalue.sum(0),
            grad_out + out_part,
        )

    start_state = (
        stored,
        jnp.zeros((row_count, hidden), jnp.float32),
        jnp.zeros((row_count, width), jnp.bfloat16),
        zero_row,
        zero_row,
        jnp.zeros((hidden, width), jnp.float32),
    )
    stored, dvalue_rows, embedded, grad_gain, grad_bias, grad_out = lax.fori_loop(
        0, block_total, second_pass, start_state
    )
    grad_gain, grad_bias = lax.psum((grad_gain, grad_bias), ("dp", "rep"))

    def signal_block():
        keep_rows = live_flags[:, None]
        dpre = norm_gain * inv_std * (dvalue_rows - grad_bias / total - stored * grad_gain / total)
        return jnp.where(keep_rows, dpre, 0.0).astype(jnp.bfloat16)

    def store_pass(block_index, dpre_rows):
        return signal_block()

    dpre_rows = lax.fori_loop(
        0, block_total, store_pass, jnp.zeros((row_count, hidden), jnp.bfloat16)
    )
    out_share = lax.psum_scatter(grad_out, ("dp", "rep"), scatter_dimension=0, tiled=True)
    code_share = owner_rows(dpre_rows, row_ids, hash_scale, hash_shift)
    return (embedded, code_share, out_share, grad_gain, grad_bias)


def per_device(
    ids, counts, hash_scale, hash_shift, w_code, norm_gain, norm_bias, w_out, out_bias, cotangent
):
    live_count = counts[0]
    weights = (w_code, norm_gain, norm_bias, w_out, out_bias)
    code_rows = hashed(ids, hash_scale, hash_shift)
    embedded, code_share, out_share, grad_gain, grad_bias = train_rows(
        code_rows, cotangent, live_count, ids, hash_scale, hash_shift, *weights
    )
    return (embedded, code_share, out_share, grad_gain, grad_bias)


def solution(mesh):
    return jax.shard_map(
        per_device,
        mesh=mesh,
        in_specs=(
            P(("dp", "rep")),
            P(("dp", "rep")),
            P(),
            P(),
            P(),
            P(),
            P(),
            P(),
            P(),
            P(("dp", "rep"), None),
        ),
        out_specs=(
            P(("dp", "rep"), None),
            P(("dp", "rep"), None),
            P(("dp", "rep"), None),
            P(),
            P(),
        ),
        check_vma=False,
    )
```

profile of v0, /device:TPU:0, one launch (start us, length us, event | category | flops | bytes accessed | tf_op | source)
XLA Modules:
  0.0 264.1 jit_solution(4582363690425462505)
XLA Ops:
  7.9 0.7 and_select_fusion
  8.6 1.4 multiply_reduce_fusion.1
  10.1 1.1 broadcast.69.clone
  11.2 1.0 while.57
  11.2 1.0 copy.38
  12.3 42.2 %all-reduce.1 = (f32[1024]{0:T(1024)S(1)}, f32[]{:T(128)}, f32[1024]{0:T(1024)S(1)}) all-reduce(f32[1024]{0:T(1024)S(1)} %get-tuple-element.387, f32[]{:T(128)S(6)} %convert_element_type.36, f32[1024]{0:T(1024)S(1)} %get-tuple-element.388), channel_id=1, replica_groups=mesh['dp'=16,'rep'=2] {'dp','rep'}, use_global_device_ids=true, to_apply=%region_4.5 | all-reduce | flops 2049 | bytes 16392 | tf_op jit(solution)/shard_map/psum | solution.py:91
  55.2 0.7 fusion.43
  55.8 1.1 broadcast.69
  57.0 0.6 broadcast_in_dim.81
  57.6 5.0 %while.58 = (s32[]{:T(128)}, f32[256,1024]{1,0:T(8,128)S(1)}, f32[256,1024]{1,0:T(8,128)}, bf16[256,128]{1,0:T(8,128)(2,1)}, f32[1024]{0:T(1024)S(1)}, /*index=5...) while((s32[]{:T(128)}, f32[256,1024]{1,0:T(8,128)S(1)}, ...), condition=%wide.region_10.11_spmd.clone, body=%wide.region_7.10_spmd.clone.sunk | while | flops 210206976 | bytes 7595697 | solution.py:136
  57.7 0.8 multiply_convert_fusion.2
  58.4 0.7 iota_compare_fusion.5
  59.1 2.2 fusion.60
  61.3 0.4 convolution_add_fusion.3
  61.7 0.9 fusion.61
  62.7 40.3 %all-reduce = (f32[1024]{0:T(1024)S(1)}, f32[1024]{0:T(1024)S(1)}) all-reduce(f32[1024]{0:T(1024)S(1)} %get-tuple-element.390, f32[1024]{0:T(1024)S(1)} %get-tuple-element.392), channel_id=1, replica_groups=mesh['dp'=16,'rep'=2] {'dp','rep'}, use_global_device_ids=true, to_apply=%region_11.12 | all-reduce | flops 2048 | bytes 16384 | tf_op jit(solution)/shard_map/psum | solution.py:139
  103.0 0.8 broadcast_in_dim.83
  103.9 4.2 %while.59 = (s32[]{:T(128)}, bf16[256,1024]{1,0:T(8,128)(2,1)}, s32[]{:T(128)}, f32[1,1024]{1,0:T(1,128)S(1)}, f32[]{:T(128)}, /*index=5*/f32[1024]{0:T(1024)S(1...) while((s32[]{:T(128)}, bf16[256,1024]{1,0:T(8,128)(2,1)}, ...), condition=%wide.region_14.15_spmd.clone, body=%wide.region_13.14_spmd.clone.sunk | while | flops 1836290 | bytes 2642553 | solution.py:149
  103.9 0.6 broadcast_divide_fusion.3
  104.5 0.7 iota_compare_fusion.6
  105.2 2.9 %select_convert_fusion.7 = bf16[256,1024]{1,0:T(8,128)(2,1)} fusion(f32[256,1024]{1,0:T(8,128)S(1)} %get-tuple-element.870, f32[256,1024]{1,0:T(8,128)} %get-tuple-element.868, f32[]{:T(128)} %get-tuple-element.866, f32[1024]{0:T(1024)S(1)} %get-tuple-element.869, f32[1024]{0:T(1024)S(1)} %broadcast_divide_fusion.3, f32[1024]{0:T(1024)S(1)} %bitcast.37, ...), kind=kLoop, calls=%fused_computation.18.clone.1 | loop fusion | flops 1835008 | bytes 2633988 | tf_op jit(solution)/shard_map/while/body/convert_element_type | solution.py:144
  108.1 2.0 copy.22
  110.1 6.4 %all-to-all-start = ((bf16[256,16,64]{0,2,1:T(8,128)(2,1)}), bf16[256,16,64]{0,2,1:T(8,128)(2,1)S(1)}, u32[]{:S(2)}, u32[]{:S(2)}) async-start(bf16[256,16,64]{0,2,1:T(8,128)(2,1)} %bitcast.2), calls=%async_computation | async-start | bytes 1048576 | tf_op jit(solution)/shard_map/all_to_all | solution.py:33
  116.5 0.0 reduce-scatter.2.cloned.1.call-start
  116.6 0.7 reduce-scatter.2.cloned.1.call-update
  117.3 41.9 %all-gather = s32[32,1,256]{2,1,0:T(1,128)S(1)} all-gather(s32[1,1,256]{2,1,0:T(1,128)S(1)} %bitcast.41), channel_id=1, replica_groups=mesh['dp'=16,'rep'=2] {'dp','rep'}, dimensions={0}, use_global_device_ids=true | all-gather | bytes 33792 | tf_op jit(solution)/shard_map/all_gather | solution.py:39
  159.2 0.2 remainder_reduce_fusion
  159.4 0.3 copy.23
  159.7 0.2 all_to_all.29
  160.0 4.2 %all_to_all.35 = bf16[4096,2,32]{0,2,1:T(8,128)(2,1)S(1)} all-to-all(bf16[4096,2,32]{0,2,1:T(8,128)(2,1)S(1)} %all_to_all.29), channel_id=1, replica_groups=mesh['dp'=16,'rep'=2] {'rep'}, dimensions={1} | all-to-all | bytes 1048576 | tf_op jit(solution)/shard_map/all_to_all | solution.py:32
  164.2 11.9 %fusion.16 = f32[32,512]{1,0:T(8,128)} fusion(bf16[8192,32]{0,1:T(8,128)(2,1)S(1)} %bitcast.35, s32[512]{0:T(512)S(1)} %copy-done.11, s32[8192]{0:T(1024)S(1)} %add_select_fusion.2, s32[512]{0:T(512)S(1)} %copy-done.12), kind=kOutput, calls=%fused_computation.30 | convolution fusion | flops 318767104 | bytes 626688 | tf_op jit(solution)/shard_map/while/body/eval_jaxpr/dot_general | solution.py:49
  176.1 81.1 %reduce-scatter.2.cloned.1.call-done = f32[32,128]{1,0:T(8,128)} async-done(((f32[1024,128]{1,0:T(8,128)}), f32[32,128]{1,0:T(8,128)}) %reduce-scatter.2.cloned.1.call-update) | async-done | bytes 16400 | tf_op jit(solution)/shard_map/reduce_scatter | solution.py:152
  (42 shorter events, 0.2 us)
Async XLA Ops:
  7.2 1.5 copy-start
  11.2 43.9 %copy-start.5 = (f32[1024]{0:T(1024)S(1)}, f32[1024]{0:T(1024)}, u32[]{:S(2)}) copy-start(f32[1024]{0:T(1024)} %param.21) | copy-start | bytes 12292
  12.2 45.4 %copy-start.1 = (f32[256,1024]{1,0:T(8,128)S(1)}, f32[256,1024]{1,0:T(8,128)}, u32[]{:S(2)}) copy-start(f32[256,1024]{1,0:T(8,128)} %get-tuple-element.787) | copy-start | bytes 3145732
  12.2 45.4 %copy-start.3 = (bf16[1024,128]{1,0:T(8,128)(2,1)S(1)}, bf16[1024,128]{1,0:T(8,128)(2,1)}, u32[]{:S(2)}) copy-start(bf16[1024,128]{1,0:T(8,128)(2,1)} %param.23) | copy-start | bytes 786436
  12.3 45.3 %copy-start.4 = (bf16[256,128]{1,0:T(8,128)(2,1)S(1)}, bf16[256,128]{1,0:T(8,128)(2,1)}, u32[]{:S(2)}) copy-start(bf16[256,128]{1,0:T(8,128)(2,1)} %param.25) | copy-start | bytes 196612
  12.3 45.3 %copy-start.6 = (f32[1024]{0:T(1024)S(1)}, f32[1024]{0:T(1024)}, u32[]{:S(2)}) copy-start(f32[1024]{0:T(1024)} %param.22) | copy-start | bytes 12292
  12.3 45.3 %copy-start.9 = (f32[128]{0:T(128)S(1)}, f32[128]{0:T(128)}, u32[]{:S(2)}) copy-start(f32[128]{0:T(128)} %param.24) | copy-start | bytes 1540
  62.7 41.2 %copy-start.2 = (f32[1024,128]{1,0:T(8,128)}, f32[1024,128]{1,0:T(8,128)S(1)}, u32[]{:S(2)}) copy-start(f32[1024,128]{1,0:T(8,128)S(1)} %get-tuple-element.395) | copy-start | bytes 1572868
  108.1 2.0 copy-start.7
  108.1 2.1 copy-start.8
  110.1 7.1 %copy-start.10 = (s32[256]{0:T(256)S(1)}, s32[256]{0:T(256)}, u32[]{:S(2)}) copy-start(s32[256]{0:T(256)} %param.16) | copy-start | bytes 3076
  110.1 49.3 %all-to-all-start = ((bf16[256,16,64]{0,2,1:T(8,128)(2,1)}), bf16[256,16,64]{0,2,1:T(8,128)(2,1)S(1)}, u32[]{:S(2)}, u32[]{:S(2)}) async-start(bf16[256,16,64]{0,2,1:T(8,128)(2,1)} %bitcast.2), calls=%async_computation | async-start | bytes 1048576 | tf_op jit(solution)/shard_map/all_to_all | solution.py:33
  116.5 140.7 %reduce-scatter.2.cloned.1.call-start = ((), (), s32[]{:S(2)}) async-start(), calls=%async_computation.3 | async-start | bytes 540672 | tf_op jit(solution)/shard_map/reduce_scatter | solution.py:152
  160.0 4.2 %copy-start.11 = (s32[512]{0:T(512)S(1)}, s32[512]{0:T(512)}, u32[]{:S(2)}) copy-start(s32[512]{0:T(512)} %param.19) | copy-start | bytes 6148
  160.0 4.2 %copy-start.12 = (s32[512]{0:T(512)S(1)}, s32[512]{0:T(512)}, u32[]{:S(2)}) copy-start(s32[512]{0:T(512)} %param.18) | copy-start | bytes 6148
Sparse Core Ops, SparseCore 0:
  120.1 137.0 reduce-scatter.1
where the time goes:
time: 265 us; the launch traced here: 264 us
  blocking collectives  129 us (49%)
  waiting for transfers between devices  81.8 us (31%)
  matrix products  16.9 us (6%)
  between operations  15.7 us (6%)
  local copies, waits for them, and re-layouts  7.5 us (3%)
  other arithmetic  7.18 us (3%)
  starting transfers between devices  6.41 us (2%)
    reduce_scatter x1, waiting for transfers between devices, train_rows(): lax.psum_scatter(grad_out, ('dp', 'rep'), scatter_dimension=0, tiled=True)  81.1 us
    psum x1, blocking collectives, train_rows(): lax.psum((sum_hidden, sum_square, live_count.astype(jnp.float32)), ('dp',...  42.2 us
    all_gather x1, blocking collectives, owner_rows(): everyone = lax.all_gather(row_ids, ('dp', 'rep'), axis=0, tiled=True)  41.9 us
    psum x1, blocking collectives, train_rows(): grad_gain, grad_bias = lax.psum((grad_gain, grad_bias), ('dp', 'rep'))  40.3 us
    dot_general x1, matrix products, accumulate(): lax.dot_general(col_block, code_block, (((0,), (0,)), ((), ())), preferre...  11.9 us
    all_to_all x1, starting transfers between devices, owner_rows(): lax.all_to_all(dpre_rows, 'dp', split_axis=1, concat_axis=0, tiled=True)  6.37 us
  transfers between devices with their start and end apart: 2, of which 1 were waited for; matrix products, arithmetic and copies ran while one was open for 5% of the time, Pallas kernels for 0%

commit v1 on v0

v1 whole, which is shorter than its diff:
```python
import math

import jax
import jax.numpy as jnp
from jax import lax
from jax.sharding import PartitionSpec as P

LANES = 128
modulus = 65521
epsilon = 1e-05
AXES = ("dp", "rep")


def hashed(ident, hash_scale, hash_shift):
    resid = ident % modulus
    bucket = (hash_scale[None, :] * resid[:, None] + hash_shift[None, :]) % modulus
    return (bucket.astype(jnp.float32) * (2.0 / (modulus - 1)) - 1.0).astype(jnp.bfloat16)


def mish_parts(gated):
    softer = jax.nn.softplus(gated)
    tangent = jnp.tanh(softer)
    return (gated * tangent, tangent + gated * (1.0 - tangent * tangent) * jax.nn.sigmoid(gated))


def exchange(blocks):
    return lax.all_to_all(blocks, AXES, split_axis=0, concat_axis=0, tiled=True)


def lane_rows(flat):
    pad = -flat.shape[-1] % (8 * LANES)
    flat = jnp.pad(flat, [(0, 0)] * (flat.ndim - 1) + [(0, pad)])
    return flat.reshape(flat.shape[:-1] + (-1, LANES))


def per_device(
    ids, counts, hash_scale, hash_shift, w_code, norm_gain, norm_bias, w_out, out_bias, cotangent
):
    devices = lax.axis_size("dp") * lax.axis_size("rep")
    me = lax.axis_index("dp") * lax.axis_size("rep") + lax.axis_index("rep")
    slots = ids.shape[0]
    codes, hidden = w_code.shape
    width = w_out.shape[1]
    share = hidden // devices
    keep = (jnp.arange(slots, dtype=jnp.int32) < counts[0])[:, None]

    preact = jnp.dot(
        hashed(ids, hash_scale, hash_shift), w_code, preferred_element_type=jnp.float32
    )
    masked = jnp.where(keep, preact, 0.0)
    row = lane_rows(
        jnp.concatenate(
            [
                masked.sum(0),
                (masked * masked).sum(0),
                ids.astype(jnp.float32),
                counts.astype(jnp.float32),
            ]
        )
    )
    table = exchange(jnp.broadcast_to(row, (devices,) + row.shape)).reshape(devices, -1)
    sums = table[:, : 2 * hidden].sum(0)
    all_ids = table[:, 2 * hidden : 2 * hidden + slots].astype(jnp.int32)
    all_counts = table[:, 2 * hidden + slots].astype(jnp.int32)
    total = all_counts.sum().astype(jnp.float32)
    mean = sums[:hidden] / total
    inv_std = lax.rsqrt(sums[hidden:] / total - mean * mean + epsilon)

    normed = (preact - mean) * inv_std
    act_full, slope = mish_parts(normed * norm_gain + norm_bias)
    act = act_full.astype(jnp.bfloat16)
    delta = jnp.where(keep, cotangent.astype(jnp.float32) * lax.rsqrt(total), 0.0).astype(
        jnp.bfloat16
    )
    dval = (
        lax.dot_general(delta, w_out, (((1,), (1,)), ((), ())), preferred_element_type=jnp.float32)
        * slope
    )
    grad_out = lax.dot_general(
        act, delta, (((0,), (0,)), ((), ())), preferred_element_type=jnp.float32
    )
    columns = exchange(dval.astype(jnp.bfloat16).T.reshape(devices, share, slots))
    pair = jnp.concatenate([(dval * normed).sum(0), dval.sum(0)])
    grads = exchange(
        lane_rows(
            jnp.concatenate(
                [
                    grad_out.reshape(devices, share * width),
                    jnp.broadcast_to(pair, (devices, 2 * hidden)),
                ],
                axis=1,
            )
        )
    )
    grads = grads.reshape(devices, -1)[:, : share * width + 2 * hidden].sum(0)
    out_share = grads[: share * width].reshape(share, width)
    grad_gain = grads[share * width : share * width + hidden]
    grad_bias = grads[share * width + hidden :]

    embedded = jnp.dot(act, w_out, preferred_element_type=jnp.float32) + out_bias
    embedded = jnp.where(keep, embedded, 0.0).astype(jnp.bfloat16)

    def own(vector):
        return lax.dynamic_slice_in_dim(vector, me * share, share, vector.ndim - 1)

    w_own = own(w_code)
    mean_own, inv_own = own(mean), own(inv_std)
    shift_own, tilt_own = own(grad_bias) / total, own(grad_gain) / total
    scale_own = own(norm_gain) * inv_own
    group = math.gcd(devices, max(1, 8192 // slots))

    def accumulate(index, grad_rows):
        start = index * group
        block_ids = lax.dynamic_slice_in_dim(all_ids, start, group, 0).reshape(-1)
        block_counts = lax.dynamic_slice_in_dim(all_counts, start, group, 0)
        block = lax.dynamic_slice_in_dim(columns, start, group, 0)
        code = hashed(block_ids, hash_scale, hash_shift)
        pre = lax.dot_general(
            w_own, code, (((0,), (1,)), ((), ())), preferred_element_type=jnp.float32
        )
        seen = (pre - mean_own[:, None]) * inv_own[:, None]
        dval_own = block.transpose(1, 0, 2).reshape(share, -1).astype(jnp.float32)
        dpre = scale_own[:, None] * (dval_own - shift_own[:, None] - seen * tilt_own[:, None])
        live = jnp.arange(slots, dtype=jnp.int32)[None, :] < block_counts[:, None]
        dpre = jnp.where(live.reshape(1, -1), dpre, 0.0).astype(jnp.bfloat16)
        return grad_rows + jnp.dot(dpre, code, preferred_element_type=jnp.float32)

    code_share = lax.fori_loop(
        0, devices // group, accumulate, jnp.zeros((share, codes), jnp.float32)
    )
    return embedded, code_share, out_share, grad_gain, grad_bias


def solution(mesh):
    rows = P(AXES)
    return jax.shard_map(
        per_device,
        mesh=mesh,
        in_specs=(rows, rows, P(), P(), P(), P(), P(), P(), P(), P(AXES, None)),
        out_specs=(P(AXES, None), P(AXES, None), P(AXES, None), P(), P()),
        check_vma=False,
    )
```

time: 265 us -> 97.1 us (0.37)
  blocking collectives: 129 us -> 20.4 us
  waiting for transfers between devices: 81.8 us -> 24.7 us
  matrix products: 16.9 us -> 31.3 us
  between operations: 15.7 us -> 2.37 us
    psum x2 -> x0, blocking collectives: 82.5 us -> none  [the longest x1 42.2 us: train_rows(): lax.psum((sum_hidden, sum_square, live_count.astype(jnp.float32)), ('dp',...]
    reduce_scatter x1 -> x0, waiting for transfers between devices: 81.1 us -> none  [train_rows(): lax.psum_scatter(grad_out, ('dp', 'rep'), scatter_dimension=0, tiled=True)]
    all_gather x1 -> x0, blocking collectives: 41.9 us -> none  [owner_rows(): everyone = lax.all_gather(row_ids, ('dp', 'rep'), axis=0, tiled=True)]
    all_to_all x1 -> x2, waiting for transfers between devices: 0.01 us -> 24.7 us  [exchange(): return lax.all_to_all(blocks, AXES, split_axis=0, concat_axis=0, tiled=True)]
    all_to_all x1, blocking collectives: 4.18 us -> 20.4 us  [exchange(): return lax.all_to_all(blocks, AXES, split_axis=0, concat_axis=0, tiled=True)]
    dot_general x5 -> x6, matrix products: 16.9 us -> 31.3 us  [the longest x1 12.2 us: accumulate(): lax.dot_general(w_own, code, (((0,), (1,)), ((), ())), preferred_element_...]
    while x2 -> x0, local copies, waits for them, and re-layouts: 3.06 us -> none  [the longest x1 2.04 us: train_rows(): lax.fori_loop(0, block_total, store_pass, jnp.zeros((row_count, hidden),...]
    all_to_all x1 -> x2, starting transfers between devices: 6.37 us -> 5.69 us  [exchange(): return lax.all_to_all(blocks, AXES, split_axis=0, concat_axis=0, tiled=True)]
  transfers between devices with their start and end apart: 2 -> 2, of which waited for: 1 -> 2; matrix products, arithmetic and copies ran while one was open for 5% -> 12% of each run, Pallas kernels for 0% -> 0%
where the time goes in v1:
time: 97.1 us; the launch traced here: 96.5 us
  matrix products  31.3 us (32%)
  waiting for transfers between devices  24.7 us (25%)
  blocking collectives  20.4 us (21%)
  other arithmetic  6.5 us (7%)
  starting transfers between devices  5.69 us (6%)
  local copies, waits for them, and re-layouts  5.56 us (6%)
  between operations  2.37 us (2%)
    all_to_all x2, waiting for transfers between devices, exchange(): return lax.all_to_all(blocks, AXES, split_axis=0, concat_axis=0, tiled=True)  24.7 us
    all_to_all x1, blocking collectives, exchange(): return lax.all_to_all(blocks, AXES, split_axis=0, concat_axis=0, tiled=True)  20.4 us
    dot_general x1, matrix products, accumulate(): lax.dot_general(w_own, code, (((0,), (1,)), ((), ())), preferred_element_...  12.2 us
    dot_general x1, matrix products, accumulate(): return grad_rows + jnp.dot(dpre, code, preferred_element_type=jnp.float32)  11.9 us
    all_to_all x2, starting transfers between devices, exchange(): return lax.all_to_all(blocks, AXES, split_axis=0, concat_axis=0, tiled=True)  5.69 us
    dot_general x1, matrix products, per_device(): lax.dot_general(delta, w_out, (((1,), (1,)), ((), ())), preferred_element...  2.22 us
    dot_general x1, matrix products, per_device(): lax.dot_general(act, delta, (((0,), (0,)), ((), ())), preferred_element_t...  2.03 us
  transfers between devices with their start and end apart: 2, of which 2 were waited for; matrix products, arithmetic and copies ran while one was open for 12% of the time, Pallas kernels for 0%

profile of v1, /device:TPU:0, one launch (start us, length us, event | category | flops | bytes accessed | tf_op | source)
XLA Modules:
  0.0 96.5 jit_solution(10607334301454308005)
XLA Ops:
  0.6 0.0 copy-start
  1.4 0.0 copy-start.11
  1.4 0.8 fusion.85
  2.2 1.4 %select_reduce_fusion = (f32[1024]{0:T(1024)S(1)}, f32[1024]{0:T(1024)S(1)}, f32[256,1024]{1,0:T(8,128)S(1)}) fusion(pred[256]{0:T(512)(128)(4,1)S(1)} %iota_compare_fusion.2, bf16[512,1024]{1,0:T(8,128)(2,1)S(1)} %copy-done, s32[512]{0:T(512)} %param.13, s32[256]{0:T(256)S(1)} %get-tuple-element.62, s32[512]{0:T(512)} %param.12), kind=kOutput, calls=%fused_computation.48 | convolution fusion | flops 271054848 | bytes 2110720 | tf_op jit(solution)/shard_map/dot_general | solution.py:47
  3.7 20.4 %all_to_all.15 = f32[32,24,128]{2,1,0:T(8,128)S(1)} all-to-all(f32[32,24,128]{2,1,0:T(8,128)S(1)} %broadcast_in_dim.85), channel_id=1, replica_groups=mesh['dp'=16,'rep'=2] {'dp','rep'}, dimensions={0} | all-to-all | bytes 786432 | tf_op jit(solution)/shard_map/all_to_all | solution.py:27
  24.1 0.1 copy.24
  24.2 0.6 fusion.64
  25.6 2.2 %add_multiply_fusion = (f32[256,1024]{1,0:T(8,128)}, bf16[256,1024]{1,0:T(8,128)(2,1)S(1)}, f32[256,1024]{1,0:T(8,128)S(1)}) fusion(f32[256,1024]{1,0:T(8,128)S(1)} %get-tuple-element.63, f32[1024]{0:T(1024)S(1)} %copy-done.10, f32[1024]{0:T(1024)S(1)} %copy-done.7, f32[1024]{0:T(1024)S(1)} %get-tuple-element.60, f32[1024]{0:T(1024)S(1)} %get-tuple-element.59, ...), kind=kOutput, calls=%fused_computation.40 | convolution fusion | flops 72744960 | bytes 4014340 | tf_op jit(solution)/shard_map/dot_general | solution.py:76
  27.8 1.1 %fusion.32 = bf16[1024,256]{0,1:T(8,128)(2,1)S(1)} fusion(f32[256,1024]{1,0:T(8,128)S(1)} %get-tuple-element.64, f32[256,1024]{1,0:T(8,128)S(1)} %get-tuple-element.63, f32[1024]{0:T(1024)S(1)} %copy-done.10, f32[1024]{0:T(1024)S(1)} %copy-done.7, f32[1024]{0:T(1024)S(1)} %get-tuple-element.60, f32[1024]{0:T(1024)S(1)} %get-tuple-element.59), kind=kLoop, calls=%fused_computation.47 | loop fusion | flops 5242880 | bytes 2637824 | tf_op jit(solution)/shard_map/convert_element_type | solution.py:82
  28.9 1.0 %copy.17 = bf16[1024,256]{1,0:T(8,128)(2,1)} copy(bf16[1024,256]{0,1:T(8,128)(2,1)S(1)} %fusion.32) | data formatting | bytes 1048576 | tf_op jit(solution)/shard_map/convert_element_type | solution.py:82
  29.9 2.6 %all-to-all-start.1 = ((bf16[32,32,256]{2,1,0:T(8,128)(2,1)}), bf16[32,32,256]{2,1,0:T(8,128)(2,1)S(1)}, u32[]{:S(2)}, u32[]{:S(2)}) async-start(bf16[32,32,256]{2,1,0:T(8,128)(2,1)} %bitcast.69), calls=%async_computation.1 | async-start | bytes 1048576 | tf_op jit(solution)/shard_map/all_to_all | solution.py:27
  32.5 2.0 %fusion.62 = f32[1024,128]{1,0:T(8,128)} fusion(bf16[256,1024]{1,0:T(8,128)(2,1)S(1)} %get-tuple-element.56, bf16[256,128]{1,0:T(8,128)(2,1)} %param.19, f32[]{:T(128)S(6)} %rsqrt.7, pred[256]{0:T(512)(128)(4,1)S(1)} %copy-done.12), kind=kOutput, calls=%fused_computation.84 | convolution fusion | flops 67239936 | bytes 1114372 | tf_op jit(solution)/shard_map/dot_general | solution.py:79
  34.6 1.9 %reshape.88 = f32[32,4096]{1,0:T(8,128)} reshape(f32[1024,128]{1,0:T(8,128)} %fusion.62) | data formatting | bytes 1048576 | tf_op jit(solution)/shard_map/reshape | solution.py:88
  36.5 1.5 %multiply_reduce_fusion = (f32[1024]{0:T(1024)S(1)}, f32[1024]{0:T(1024)S(1)}) fusion(f32[256,1024]{1,0:T(8,128)} %get-tuple-element.41, f32[256,1024]{1,0:T(8,128)S(1)} %get-tuple-element.63, f32[1024]{0:T(1024)S(1)} %get-tuple-element.60, f32[1024]{0:T(1024)S(1)} %get-tuple-element.59), kind=kLoop, calls=%fused_computation.39 | loop fusion | flops 1308672 | bytes 2113536 | tf_op jit(solution)/shard_map/reduce_sum | solution.py:83
  38.0 0.1 maximum_bitcast_fusion
  38.1 1.0 %copy.21 = f32[4,8,48,128]{3,2,1,0:T(8,128)} copy(f32[4,8,48,128]{3,1,2,0:T(8,128)S(1)} %maximum_bitcast_fusion) | data formatting | bytes 1572864
  39.1 9.0 %all-to-all-done.1 = bf16[32,32,256]{2,1,0:T(8,128)(2,1)S(1)} async-done(((bf16[32,32,256]{2,1,0:T(8,128)(2,1)}), bf16[32,32,256]{2,1,0:T(8,128)(2,1)S(1)}, u32[]{:S(2)}, u32[]{:S(2)}) %all-to-all-start.1) | async-done | bytes 524320 | tf_op jit(solution)/shard_map/all_to_all | solution.py:27
  48.1 3.1 %all-to-all-start.2 = ((f32[32,48,128]{2,1,0:T(8,128)}), f32[32,48,128]{2,1,0:T(8,128)S(1)}, u32[]{:S(2)}, u32[]{:S(2)}) async-start(f32[32,48,128]{2,1,0:T(8,128)} %bitcast.13), calls=%async_computation.2 | async-start | bytes 1572864 | tf_op jit(solution)/shard_map/all_to_all | solution.py:27
  51.2 0.7 iota_compare_fusion
  52.0 0.6 lt.87
  52.6 0.1 dynamic_slice.28
  52.7 0.8 dynamic-slice_multiply_fusion
  53.5 0.6 add_select_fusion.2
  54.1 1.6 %fusion.17 = bf16[256,128]{1,0:T(8,128)(2,1)} fusion(bf16[256,1024]{1,0:T(8,128)(2,1)S(1)} %get-tuple-element.56, bf16[1024,128]{1,0:T(8,128)(2,1)S(1)} %copy-done.3, f32[128]{0:T(128)} %param.18, pred[256]{0:T(512)(128)(4,1)} %copy-done.11), kind=kOutput, calls=%fused_computation.21 | convolution fusion | flops 67207168 | bytes 852736 | tf_op jit(solution)/shard_map/dot_general | solution.py:100
  55.7 0.1 convert_bitcast_fusion
  55.9 0.1 copy.19
  56.0 15.7 %all-to-all-done.2 = f32[32,48,128]{2,1,0:T(8,128)S(1)} async-done(((f32[32,48,128]{2,1,0:T(8,128)}), f32[32,48,128]{2,1,0:T(8,128)S(1)}, u32[]{:S(2)}, u32[]{:S(2)}) %all-to-all-start.2) | async-done | bytes 786464 | tf_op jit(solution)/shard_map/all_to_all | solution.py:27
  71.6 0.1 reduce_sum.69
  71.7 0.6 slice.49
  72.3 0.1 dynamic-slice_divide_fusion
  72.4 12.2 %fusion.12.clone.5 = bf16[32,8192]{1,0:T(8,128)(2,1)S(1)} fusion(s32[512]{0:T(512)S(1)} %copy-done.13, s32[8192]{0:T(1024)S(1)} %copy-done.5, s32[512]{0:T(512)S(1)} %copy-done.14, f32[32,8192]{1,0:T(8,128)S(1)} %bitcast.74, f32[32]{0:T(128)S(1)} %get-tuple-element.65, f32[32]{0:T(128)S(1)} %get-tuple-element.40, ...), kind=kOutput, calls=%fused_computation.15.clone.clone.clone.2 | convolution fusion | flops 320864256 | bytes 1751556 | tf_op jit(solution)/shard_map/while/body/eval_jaxpr/dot_general | solution.py:118
  84.6 11.9 %fusion.13 = f32[32,512]{1,0:T(8,128)} fusion(s32[512]{0:T(512)S(1)} %copy-done.13, s32[8192]{0:T(1024)S(1)} %copy-done.5, s32[512]{0:T(512)S(1)} %copy-done.14, bf16[32,8192]{1,0:T(8,128)(2,1)S(1)} %fusion.12.clone.5), kind=kOutput, calls=%fused_computation.16 | convolution fusion | flops 318767104 | bytes 626688 | tf_op jit(solution)/shard_map/while/body/eval_jaxpr/dot_general | solution.py:126
  (37 shorter events, 0.2 us)
Async XLA Ops:
  0.6 1.5 %copy-start = (bf16[512,1024]{1,0:T(8,128)(2,1)S(1)}, bf16[512,1024]{1,0:T(8,128)(2,1)}, u32[]{:S(2)}) copy-start(bf16[512,1024]{1,0:T(8,128)(2,1)} %param.14) | copy-start | bytes 3145732
  1.4 24.2 %copy-start.11 = (pred[256]{0:T(512)(128)(4,1)}, pred[256]{0:T(512)(128)(4,1)S(1)}, u32[]{:S(2)}) copy-start(pred[256]{0:T(512)(128)(4,1)S(1)} %iota_compare_fusion.2) | copy-start | bytes 772
  3.6 21.9 %copy-start.2 = (bf16[1024,128]{1,0:T(8,128)(2,1)S(1)}, bf16[1024,128]{1,0:T(8,128)(2,1)}, u32[]{:S(2)}) copy-start(bf16[1024,128]{1,0:T(8,128)(2,1)} %param.17) | copy-start | bytes 786436
  3.6 21.9 %copy-start.4 = (bf16[256,128]{1,0:T(8,128)(2,1)S(1)}, bf16[256,128]{1,0:T(8,128)(2,1)}, u32[]{:S(2)}) copy-start(bf16[256,128]{1,0:T(8,128)(2,1)} %param.19) | copy-start | bytes 196612
  3.7 21.9 %copy-start.7 = (f32[1024]{0:T(1024)S(1)}, f32[1024]{0:T(1024)}, u32[]{:S(2)}) copy-start(f32[1024]{0:T(1024)} %param.15) | copy-start | bytes 12292
  3.7 21.9 %copy-start.10 = (f32[1024]{0:T(1024)S(1)}, f32[1024]{0:T(1024)}, u32[]{:S(2)}) copy-start(f32[1024]{0:T(1024)} %param.16) | copy-start | bytes 12292
  28.9 3.6 %copy-start.12 = (pred[256]{0:T(512)(128)(4,1)S(1)}, pred[256]{0:T(512)(128)(4,1)}, u32[]{:S(2)}) copy-start(pred[256]{0:T(512)(128)(4,1)} %copy-done.11) | copy-start | bytes 772
  29.9 18.2 %all-to-all-start.1 = ((bf16[32,32,256]{2,1,0:T(8,128)(2,1)}), bf16[32,32,256]{2,1,0:T(8,128)(2,1)S(1)}, u32[]{:S(2)}, u32[]{:S(2)}) async-start(bf16[32,32,256]{2,1,0:T(8,128)(2,1)} %bitcast.69), calls=%async_computation.1 | async-start | bytes 1048576 | tf_op jit(solution)/shard_map/all_to_all | solution.py:27
  36.5 1.5 %copy-start.1 = (f32[32,4096]{1,0:T(8,128)S(1)}, f32[32,4096]{1,0:T(8,128)}, u32[]{:S(2)}) copy-start(f32[32,4096]{1,0:T(8,128)} %reshape.88) | copy-start | bytes 1572868
  39.1 15.0 %copy-start.3 = (bf16[1024,128]{1,0:T(8,128)(2,1)S(1)}, bf16[1024,128]{1,0:T(8,128)(2,1)}, u32[]{:S(2)}) copy-start(bf16[1024,128]{1,0:T(8,128)(2,1)} %param.17) | copy-start | bytes 786436
  48.1 23.5 %all-to-all-start.2 = ((f32[32,48,128]{2,1,0:T(8,128)}), f32[32,48,128]{2,1,0:T(8,128)S(1)}, u32[]{:S(2)}, u32[]{:S(2)}) async-start(f32[32,48,128]{2,1,0:T(8,128)} %bitcast.13), calls=%async_computation.2 | async-start | bytes 1572864 | tf_op jit(solution)/shard_map/all_to_all | solution.py:27
  55.8 16.6 %copy-start.5 = (s32[8192]{0:T(1024)S(1)}, s32[8192]{0:T(1024)}, u32[]{:S(2)}) copy-start(s32[8192]{0:T(1024)} %add_select_fusion.2) | copy-start | bytes 98308
  55.8 16.6 %copy-start.6 = (pred[8192]{0:T(1024)(128)(4,1)S(1)}, pred[8192]{0:T(1024)(128)(4,1)}, u32[]{:S(2)}) copy-start(pred[8192]{0:T(1024)(128)(4,1)} %lt.87) | copy-start | bytes 24580
  55.8 16.6 %copy-start.13 = (s32[512]{0:T(512)S(1)}, s32[512]{0:T(512)}, u32[]{:S(2)}) copy-start(s32[512]{0:T(512)} %param.13) | copy-start | bytes 6148
  55.8 16.6 %copy-start.14 = (s32[512]{0:T(512)S(1)}, s32[512]{0:T(512)}, u32[]{:S(2)}) copy-start(s32[512]{0:T(512)} %param.12) | copy-start | bytes 6148
  71.7 12.9 %copy-start.8 = (f32[1024]{0:T(1024)}, f32[1024]{0:T(1024)S(1)}, u32[]{:S(2)}) copy-start(f32[1024]{0:T(1024)S(1)} %get-tuple-element.57) | copy-start | bytes 12292
  71.7 12.9 %copy-start.9 = (f32[1024]{0:T(1024)}, f32[1024]{0:T(1024)S(1)}, u32[]{:S(2)}) copy-start(f32[1024]{0:T(1024)S(1)} %get-tuple-element.58) | copy-start | bytes 12292

commit v2 on v1

--- a/solution.py
+++ b/solution.py
@@ -1,8 +1,11 @@
+import functools
 import math
 
 import jax
 import jax.numpy as jnp
 from jax import lax
+from jax.experimental import pallas as pl
+from jax.experimental.pallas import tpu as pltpu
 from jax.sharding import PartitionSpec as P
 
 LANES = 128
@@ -33,7 +36,7 @@
     return flat.reshape(flat.shape[:-1] + (-1, LANES))
 
 
-def per_device(
+def general_device(
     ids, counts, hash_scale, hash_shift, w_code, norm_gain, norm_bias, w_out, out_bias, cotangent
 ):
     devices = lax.axis_size("dp") * lax.axis_size("rep")
@@ -131,8 +134,414 @@
     return embedded, code_share, out_share, grad_gain, grad_bias
 
 
+def row_of(tiles):
+    return jnp.concatenate(tiles, axis=1)
+
+
+def place_block(tile, source, target, block):
+    shift = ((target - source) * block) % LANES
+    return pltpu.roll(tile, shift, 1) if shift else tile
+
+
+def pick_blocks(x, chosen, block):
+    per_tile = LANES // block
+    lane = lax.broadcasted_iota(jnp.int32, (x.shape[0], LANES), 1) // block
+    tiles = []
+    for first in range(0, len(chosen), per_tile):
+        tile = None
+        for place, b in enumerate(chosen[first : first + per_tile]):
+            start = b // per_tile * LANES
+            piece = place_block(x[:, start : start + LANES], b % per_tile, place, block)
+            tile = piece if tile is None else jnp.where(lane == place, piece, tile)
+        tiles.append(tile)
+    return tiles
+
+
+def split_pair(x):
+    high = x.astype(jnp.bfloat16).astype(jnp.float32)
+    return high, (x - high).astype(jnp.bfloat16).astype(jnp.float32)
+
+
+def codes_of(id_column, scale_row, shift_row):
+    raw = scale_row * id_column + shift_row
+    once = lax.shift_right_logical(raw, 16) * 15 + lax.bitwise_and(raw, 65535)
+    twice = lax.shift_right_logical(once, 16) * 15 + lax.bitwise_and(once, 65535)
+    bucket = jnp.where(twice >= modulus, twice - modulus, twice)
+    return (bucket.astype(jnp.float32) * (2.0 / (modulus - 1)) - 1.0).astype(jnp.bfloat16)
+
+
+def mish_of(val):
+    grown = jnp.exp(jnp.minimum(val, 20.0))
+    n = grown * (grown + 2.0)
+    inverse = 1.0 / (n + 2.0)
+    t = n * inverse
+    slope = t + val * (4.0 * grown * (1.0 + grown)) * (inverse * inverse)
+    return val * t, slope
+
+
+def dot_t(a, b):
+    return lax.dot_general(a, b, (((1,), (1,)), ((), ())), preferred_element_type=jnp.float32)
+
+
+def dot_rows(a, b):
+    return lax.dot_general(a, b, (((0,), (0,)), ((), ())), preferred_element_type=jnp.float32)
+
+
+def one_hot(condition):
+    return jnp.where(condition, 1.0, 0.0).astype(jnp.bfloat16)
+
+
+def first_kernel(dims, count_ref, ids_ref, scale_ref, shift_ref, w_ref, cot_ref, send_ref, pre_ref):
+    chips, reps, take, block = dims.chips, dims.reps, dims.take, dims.block
+    slots = dims.slots
+    count = count_ref[0]
+    resid = lax.rem(ids_ref[...], modulus)
+    high = lax.shift_right_logical(resid, 8).astype(jnp.float32)
+    low = lax.bitwise_and(resid, 255).astype(jnp.float32)
+    r = lax.broadcasted_iota(jnp.int32, (slots, slots), 0)
+    c = lax.broadcasted_iota(jnp.int32, (slots, slots), 1)
+    blank = jnp.zeros((6, slots), jnp.float32)
+    pieces = jnp.concatenate([high, low, blank], axis=0).astype(jnp.bfloat16)
+    columns = dot_t(one_hot(r == c), pieces)
+    id_column = (columns[:, 0:1] * 256.0 + columns[:, 1:2]).astype(jnp.int32)
+    codes = codes_of(id_column, scale_ref[...], shift_ref[...])
+    pre = jnp.dot(codes, w_ref[...], preferred_element_type=jnp.float32)
+    pre_ref[...] = pre
+    keep = lax.broadcasted_iota(jnp.int32, (slots, 1), 0) < count
+    sums = jnp.where(keep, pre, 0.0).sum(0, keepdims=True)
+    apart = jnp.where(keep, pre - sums / count.astype(jnp.float32), 0.0)
+    spread = (apart * apart).sum(0, keepdims=True)
+    stats = jnp.concatenate(split_pair(sums) + split_pair(spread), axis=0)
+    order = one_hot(c == (r % take) * chips + r // take)
+    moved = jnp.dot(order, cot_ref[...], preferred_element_type=jnp.float32).astype(jnp.bfloat16)
+    by_chip = dot_t(pieces, order)
+    lane_parts = slots // LANES
+    tail = [by_chip[i : i + 1, t * LANES : (t + 1) * LANES] for i in range(2) for t in range(lane_parts)]
+    tail.append(jnp.full((1, LANES), 1.0, jnp.float32) * count.astype(jnp.float32))
+    tail.append(jnp.zeros((dims.send_rows - take - dims.stat_rows - len(tail), LANES), jnp.float32))
+    tail = jnp.concatenate(tail, axis=0)
+    for rep in range(reps):
+        tiles = pick_blocks(stats, [k * reps + rep for k in range(chips)], block)
+        lower = jnp.concatenate(tiles + [tail], axis=0).astype(jnp.bfloat16)
+        for k in range(chips):
+            send_ref[k * reps + rep, :take, :] = moved[k * take : (k + 1) * take, :]
+            send_ref[k * reps + rep, take:, :] = lower
+
+
+def count_column(dims, recv):
+    row = dims.take + dims.stat_rows + 2 * (dims.slots // LANES)
+    return recv[:, row, :][:, 0:1]
+
+
+def id_table(dims, recv):
+    base = dims.take + dims.stat_rows
+    parts = dims.slots // LANES
+    rows = dims.devices * dims.take
+    spread = one_hot(
+        lax.broadcasted_iota(jnp.int32, (rows, dims.devices), 0) // dims.take
+        == lax.broadcasted_iota(jnp.int32, (rows, dims.devices), 1)
+    )
+    own_j = (
+        lax.broadcasted_iota(jnp.int32, (rows, dims.slots), 1) % dims.take
+        == lax.broadcasted_iota(jnp.int32, (rows, dims.slots), 0) % dims.take
+    )
+    fold = one_hot(
+        lax.broadcasted_iota(jnp.int32, (dims.slots, LANES), 0) // dims.take
+        == lax.broadcasted_iota(jnp.int32, (dims.slots, LANES), 1)
+    )
+    tables = []
+    for i in range(2):
+        flat = row_of([recv[:, base + i * parts + t, :] for t in range(parts)]).astype(jnp.bfloat16)
+        wide = jnp.dot(spread, flat, preferred_element_type=jnp.float32)
+        wide = jnp.where(own_j, wide, 0.0).astype(jnp.bfloat16)
+        tables.append(jnp.dot(wide, fold, preferred_element_type=jnp.float32).astype(jnp.bfloat16))
+    return tables
+
+
+def packing(dims, counts, chip):
+    lanes = dims.devices * dims.take
+    d = lax.broadcasted_iota(jnp.int32, (dims.devices, lanes), 0)
+    l = lax.broadcasted_iota(jnp.int32, (dims.devices, lanes), 1) // dims.take
+    j = (lax.broadcasted_iota(jnp.int32, (1, lanes), 1) % dims.take).astype(jnp.float32)
+    chip = chip.astype(jnp.float32) if hasattr(chip, "astype") else float(chip)
+    live = jnp.maximum(jnp.floor((counts - chip + (dims.chips - 1.0)) * (1.0 / dims.chips)), 0.0)
+    before = jnp.where(d < l, live, 0.0).sum(0, keepdims=True)
+    here = jnp.where(d == l, live, 0.0).sum(0, keepdims=True)
+    target = jnp.where(j < here, before + j, -1.0).astype(jnp.int32)
+    row = lax.broadcasted_iota(jnp.int32, (dims.rows, lanes), 0)
+    return one_hot(row == target), live.sum(0, keepdims=True)
+
+
+def middle_kernel(
+    dims, place_ref, recv_ref, w_ref, gain_ref, bias_ref, w_out_ref, scale_ref, shift_ref,
+    send_ref, stat_ref,
+):
+    take, block, rows = dims.take, dims.block, dims.rows
+    half, groups = dims.half, dims.groups
+    chip = place_ref[0]
+    recv = recv_ref[...].astype(jnp.float32)
+    counts = count_column(dims, recv)
+    total = counts.sum(0, keepdims=True)
+    means, variances = [], []
+    for t in range(half // LANES):
+        r = take + 4 * t
+        sums = recv[:, r, :] + recv[:, r + 1, :]
+        spread = recv[:, r + 2, :] + recv[:, r + 3, :]
+        mean = sums.sum(0, keepdims=True) / total
+        off = sums / counts - mean
+        means.append(mean)
+        variances.append((spread + counts * (off * off)).sum(0, keepdims=True) / total)
+    mean = row_of(means)
+    inv_std = lax.rsqrt(row_of(variances) + epsilon)
+    stat_ref[...] = jnp.concatenate([mean, inv_std, jnp.zeros((6, half), jnp.float32)], axis=0)
+
+    pack, _ = packing(dims, counts, chip)
+    cot = jnp.dot(
+        pack, recv_ref[:, :take, :].reshape(dims.devices * take, LANES),
+        preferred_element_type=jnp.float32,
+    )
+    high, low = id_table(dims, recv)
+    lane = lax.broadcasted_iota(jnp.int32, (rows, LANES), 1)
+    ids = jnp.dot(pack, high, preferred_element_type=jnp.float32) * 256.0 + jnp.dot(
+        pack, low, preferred_element_type=jnp.float32
+    )
+    id_column = jnp.where(lane == chip, ids, 0.0).sum(1, keepdims=True).astype(jnp.int32)
+    codes = codes_of(id_column, scale_ref[...], shift_ref[...])
+    pre = jnp.dot(codes, w_ref[...], preferred_element_type=jnp.float32)
+    normed = (pre - mean) * inv_std
+    act, slope = mish_of(normed * gain_ref[...] + bias_ref[...])
+    delta = (cot * lax.rsqrt(total)).astype(jnp.bfloat16)
+    dval = dot_t(delta, w_out_ref[...]) * slope
+    grad_out = dot_rows(act.astype(jnp.bfloat16), delta).astype(jnp.bfloat16)
+    gain_pair = split_pair((dval * normed).sum(0, keepdims=True))
+    bias_pair = split_pair(dval.sum(0, keepdims=True))
+    four = jnp.concatenate(gain_pair + bias_pair, axis=0)
+    four = jnp.concatenate(
+        [four[:, t * LANES : (t + 1) * LANES] for t in range(half // LANES)], axis=0
+    ).astype(jnp.bfloat16)
+    part = rows // groups
+    lane = lax.broadcasted_iota(jnp.int32, (part, LANES), 1) // block
+    for k in range(dims.chips):
+        start = k // groups * LANES
+        tile = None
+        for q in range(groups):
+            piece = dval[q * part : (q + 1) * part, start : start + LANES]
+            piece = place_block(piece, k % groups, q, block)
+            tile = piece if tile is None else jnp.where(lane == q, piece, tile)
+        send_ref[k, :part, :] = tile.astype(jnp.bfloat16)
+        send_ref[k, part : part + block, :] = grad_out[k * block : (k + 1) * block, :]
+        send_ref[k, part + block :, :] = four
+
+
+def embed_kernel(
+    dims, count_ref, total_ref, pre_ref, mean_ref, inv_ref, gain_ref, bias_ref, w_out_ref,
+    out_bias_ref, out_ref,
+):
+    normed = (pre_ref[...] - mean_ref[...]) * inv_ref[...]
+    act, _ = mish_of(normed * gain_ref[...] + bias_ref[...])
+    out = jnp.dot(act.astype(jnp.bfloat16), w_out_ref[...], preferred_element_type=jnp.float32)
+    keep = lax.broadcasted_iota(jnp.int32, (dims.slots, 1), 0) < count_ref[0]
+    out_ref[...] = jnp.where(keep, out + out_bias_ref[...], 0.0).astype(jnp.bfloat16)
+
+
+def owner_kernel(dims, recv_ref, w_ref, scale_ref, shift_ref, code_ref, pre_ref, live_ref):
+    recv = recv_ref[...].astype(jnp.float32)
+    counts = count_column(dims, recv)
+    part = dims.rows // dims.groups
+    tables = id_table(dims, recv)
+    both = row_of([table.astype(jnp.float32) for table in tables]).astype(jnp.bfloat16)
+    row = lax.broadcasted_iota(jnp.int32, (part, LANES), 0)
+    group = lax.broadcasted_iota(jnp.int32, (part, LANES), 1) // dims.block
+    for s in range(dims.chips):
+        pack, live = packing(dims, counts, s)
+        ids = jnp.dot(pack, both, preferred_element_type=jnp.float32)
+        id_column = (ids[:, s : s + 1] * 256.0 + ids[:, LANES + s : LANES + s + 1]).astype(jnp.int32)
+        codes = codes_of(id_column, scale_ref[...], shift_ref[...])
+        rows = pl.ds(s * part, part)
+        pre = None
+        for q in range(dims.groups):
+            chunk = codes[q * part : (q + 1) * part, :]
+            code_ref[q, rows, :] = chunk
+            term = jnp.dot(chunk, w_ref[q], preferred_element_type=jnp.float32)
+            pre = term if pre is None else pre + term
+        pre_ref[rows, :] = pre
+        live_ref[rows, :] = jnp.where(
+            (group * part + row).astype(jnp.float32) < live, 1.0, 0.0
+        )
+
+
+def spread_own(dims, x, chip):
+    groups, block = dims.groups, dims.block
+    lane = lax.broadcasted_iota(jnp.int32, (1, LANES), 1) // block
+    own = jnp.zeros((1, LANES), jnp.float32)
+    for t in range(dims.half // LANES):
+        own = own + jnp.where(
+            lane + t * groups == chip, x[:, t * LANES : (t + 1) * LANES], 0.0
+        )
+    out = own
+    for i in range(1, groups):
+        out = out + pltpu.roll(own, i * block, 1)
+    return out
+
+
+def last_kernel(
+    dims, place_ref, total_ref, recv_ref, code_ref, pre_ref, live_ref, stat_ref, gain_ref,
+    code_out_ref, out_out_ref, pair_ref,
+):
+    part, block, groups = dims.rows // dims.groups, dims.block, dims.groups
+    chip = place_ref[0]
+    total = total_ref[0].astype(jnp.float32)
+    four = recv_ref[:, part + block :, :].astype(jnp.float32).sum(0)
+    gains, biases = [], []
+    for t in range(dims.half // LANES):
+        gains.append(four[4 * t : 4 * t + 1, :] + four[4 * t + 1 : 4 * t + 2, :])
+        biases.append(four[4 * t + 2 : 4 * t + 3, :] + four[4 * t + 3 : 4 * t + 4, :])
+    gain, bias = row_of(gains), row_of(biases)
+    pair_ref[...] = jnp.concatenate([gain, bias, jnp.zeros((6, dims.half), jnp.float32)], axis=0)
+    out_out_ref[...] = recv_ref[:, part : part + block, :].astype(jnp.float32).sum(0)
+    mean = spread_own(dims, stat_ref[0:1, :], chip)
+    inv_std = spread_own(dims, stat_ref[1:2, :], chip)
+    scale = spread_own(dims, gain_ref[...], chip) * inv_std
+    shift = spread_own(dims, bias, chip) / total
+    tilt = spread_own(dims, gain, chip) / total
+    dval = recv_ref[:, :part, :].astype(jnp.float32).reshape(dims.chips * part, LANES)
+    normed = (pre_ref[...] - mean) * inv_std
+    dpre = scale * (dval - shift - normed * tilt)
+    dpre = jnp.where(live_ref[...] > 0.5, dpre, 0.0).astype(jnp.bfloat16)
+    out = None
+    for q in range(groups):
+        term = dot_rows(dpre, code_ref[q])[q * block : (q + 1) * block, :]
+        out = term if out is None else out + term
+    code_out_ref[...] = out
+
+
+class Dims:
+    def __init__(self, mesh, slots, codes, hidden, width):
+        self.chips, self.reps = mesh.shape["dp"], mesh.shape["rep"]
+        self.devices = self.chips * self.reps
+        self.slots, self.codes, self.hidden, self.width = slots, codes, hidden, width
+        self.block = hidden // self.devices
+        self.half = hidden // self.reps
+        self.groups = LANES // max(1, self.block)
+        self.take = slots // self.chips
+        bound = self.devices * slots // 4 // self.chips
+        bound += self.devices * (self.chips - 1) // self.chips
+        step = 8 * self.groups
+        self.rows = min(-(-bound // step) * step, self.devices * self.take)
+        self.stat_rows = 4 * self.half // LANES
+        self.send_rows = -(-(self.take + self.stat_rows + 2 * slots // LANES + 1) // 8) * 8
+        self.grad_rows = self.rows // self.groups + self.block + self.stat_rows
+        self.vmem = 48 << 20
+
+    def fits(self):
+        return (
+            self.width == LANES
+            and LANES % self.block == 0
+            and self.block % 8 == 0
+            and self.take % 8 == 0
+            and self.slots % LANES == 0
+            and self.half % LANES == 0
+            and self.codes % LANES == 0
+            and self.chips <= LANES
+            and self.slots <= 256
+            and self.rows % (8 * self.groups) == 0
+            and self.chips * self.rows * self.codes <= (1 << 22)
+        )
+
+
+def kernel_call(dims, body, outs, arguments, scalars, name, flops):
+    specs = [pl.BlockSpec(memory_space=pltpu.SMEM)] * scalars
+    specs += [pl.BlockSpec(memory_space=pltpu.VMEM)] * (len(arguments) - scalars)
+    return pl.pallas_call(
+        functools.partial(body, dims),
+        out_shape=[jax.ShapeDtypeStruct(shape, kind) for shape, kind in outs],
+        in_specs=specs,
+        out_specs=[pl.BlockSpec(memory_space=pltpu.VMEM)] * len(outs),
+        compiler_params=pltpu.CompilerParams(vmem_limit_bytes=dims.vmem),
+        cost_estimate=pl.CostEstimate(flops=flops, bytes_accessed=1 << 20, transcendentals=0),
+        name=name,
+    )(*arguments)
+
+
+def fast_device(
+    dims, ids, counts, hash_scale, hash_shift, w_code, norm_gain, norm_bias, w_out, out_bias,
+    cotangent,
+):
+    chips, reps, block, half = dims.chips, dims.reps, dims.block, dims.half
+    dp, rep = lax.axis_index("dp"), lax.axis_index("rep")
+    f32, bf16 = jnp.float32, jnp.bfloat16
+    scale_row, shift_row = hash_scale.reshape(1, -1), hash_shift.reshape(1, -1)
+    send, pre = kernel_call(
+        dims, first_kernel,
+        [((dims.devices, dims.send_rows, LANES), bf16), ((dims.slots, dims.hidden), f32)],
+        (counts, ids.reshape(1, -1), scale_row, shift_row, w_code, cotangent), 1, "first", 10**9,
+    )
+    recv = exchange(send)
+
+    def of_rep(x, axis):
+        shape = x.shape[:axis] + (chips, reps, block) + x.shape[axis + 1 :]
+        x = lax.dynamic_index_in_dim(x.reshape(shape), rep, axis + 1, keepdims=False)
+        return x.reshape(x.shape[:axis] + (half,) + x.shape[axis + 2 :])
+
+    place = dp.reshape(1).astype(jnp.int32)
+    w_half, w_out_half = of_rep(w_code, 1), of_rep(w_out, 0)
+    gain_half = of_rep(norm_gain, 0).reshape(1, -1)
+    bias_half = of_rep(norm_bias, 0).reshape(1, -1)
+    w_own = lax.dynamic_slice_in_dim(w_code, (dp * reps + rep) * block, block, 1)
+    w_own = jnp.stack(
+        [jnp.pad(w_own, ((0, 0), (q * block, LANES - (q + 1) * block))) for q in range(dims.groups)]
+    )
+    grads, stat = kernel_call(
+        dims, middle_kernel,
+        [((chips, dims.grad_rows, LANES), bf16), ((8, half), f32)],
+        (place, recv, w_half, gain_half, bias_half, w_out_half, scale_row, shift_row), 1,
+        "middle", 10**9,
+    )
+    share = lax.all_to_all(grads, "dp", split_axis=0, concat_axis=0, tiled=True)
+
+    def whole(x):
+        other = lax.ppermute(x, "rep", [(i, (i + 1) % reps) for i in range(reps)])
+        halves = jnp.where(rep == 0, jnp.stack([x, other]), jnp.stack([other, x]))
+        halves = halves.reshape(reps, 2, chips, block).transpose(1, 2, 0, 3)
+        return halves.reshape(2, dims.hidden)
+
+    total = recv[:, dims.send_rows - 8 :, :]
+    row = dims.take + dims.stat_rows + 2 * dims.slots // LANES - (dims.send_rows - 8)
+    total = total[:, row, 0].astype(jnp.float32).sum().astype(jnp.int32).reshape(1)
+    moments = whole(stat[:2])
+    (embedded,) = kernel_call(
+        dims, embed_kernel, [((dims.slots, dims.width), bf16)],
+        (
+            counts, total, pre, moments[0:1], moments[1:2], norm_gain.reshape(1, -1),
+            norm_bias.reshape(1, -1), w_out, out_bias.reshape(1, -1),
+        ),
+        2, "embed", 10**9,
+    )
+    packed = chips * dims.rows // dims.groups
+    code, own_pre, live = kernel_call(
+        dims, owner_kernel,
+        [((dims.groups, packed, dims.codes), bf16), ((packed, LANES), f32), ((packed, LANES), f32)],
+        (recv, w_own, scale_row, shift_row), 0, "owner", 4 * 10**9,
+    )
+    code_share, out_share, pair = kernel_call(
+        dims, last_kernel,
+        [((block, dims.codes), f32), ((block, dims.width), f32), ((8, half), f32)],
+        (place, total, share, code, own_pre, live, stat, gain_half), 2, "last", 10**9,
+    )
+    grad_pair = whole(pair[:2])
+    return embedded, code_share, out_share, grad_pair[0], grad_pair[1]
+
+
 def solution(mesh):
     rows = P(AXES)
+
+    def per_device(*arguments):
+        ids, w_code, w_out = arguments[0], arguments[4], arguments[7]
+        dims = Dims(mesh, ids.shape[0], w_code.shape[0], w_code.shape[1], w_out.shape[1])
+        if dims.reps == 2 and dims.fits():
+            return fast_device(dims, *arguments)
+        return general_device(*arguments)
+
     return jax.shard_map(
         per_device,
         mesh=mesh,

time: 97.1 us -> 51.2 us (0.53)
  matrix products: 31.3 us -> 0 us
  blocking collectives: 20.4 us -> 0 us
  waiting for transfers between devices: 24.7 us -> 8 us
  Pallas kernels: 0 us -> 14.2 us
  local copies, waits for them, and re-layouts: 5.56 us -> 14.4 us
  other arithmetic: 6.5 us -> 0.84 us
  starting transfers between devices: 5.69 us -> 11.1 us
    dot_general x6 -> x0, matrix products: 31.3 us -> none  [the longest x1 12.2 us: accumulate(): lax.dot_general(w_own, code, (((0,), (1,)), ((), ())), preferred_element_...]
    all_to_all x1 -> x0, blocking collectives: 20.4 us -> none  [exchange(): return lax.all_to_all(blocks, AXES, split_axis=0, concat_axis=0, tiled=True)]
    all_to_all x2 -> x1, waiting for transfers between devices: 24.7 us -> 6.72 us  [exchange(): return lax.all_to_all(blocks, AXES, split_axis=0, concat_axis=0, tiled=True)]
    pallas_call x0 -> x5, Pallas kernels: none -> 14.2 us  [kernel_call(): pl.pallas_call(functools.partial(body, dims), out_shape=[jax.ShapeDtypeSt...]
    unnamed x33 -> x29, local copies, waits for them, and re-layouts: 1.21 us -> 8.68 us
    all_to_all x0 -> x1, starting transfers between devices: none -> 3.73 us  [fast_device(): share = lax.all_to_all(grads, 'dp', split_axis=0, concat_axis=0, tiled=True)]
    convert_element_type x3 -> x0, other arithmetic: 2.49 us -> none  [the longest x1 1.08 us: per_device(): dval.astype(jnp.bfloat16).T.reshape(devices, share, slots)]
    dynamic_slice x1 -> x4, local copies, waits for them, and re-layouts: 0.08 us -> 2.1 us  [the longest x3 1.98 us: of_rep(): lax.dynamic_index_in_dim(x.reshape(shape), rep, axis + 1, keepdims=False)]
  transfers between devices with their start and end apart: 2 -> 4, of which waited for: 2 -> 2; matrix products, arithmetic and copies ran while one was open for 12% -> 13% of each run, Pallas kernels for 0% -> 16%
where the time goes in v2:
time: 51.2 us; the launch traced here: 50.6 us
  local copies, waits for them, and re-layouts  14.4 us (28%)
  Pallas kernels  14.2 us (28%)
  starting transfers between devices  11.1 us (22%)
  waiting for transfers between devices  8 us (16%)
  between operations  2.11 us (4%)
  other arithmetic  0.84 us (2%)
    pallas_call x5, Pallas kernels, kernel_call(): pl.pallas_call(functools.partial(body, dims), out_shape=[jax.ShapeDtypeSt...  14.2 us
    unnamed x29, local copies, waits for them, and re-layouts  8.68 us
    all_to_all x1, starting transfers between devices, exchange(): return lax.all_to_all(blocks, AXES, split_axis=0, concat_axis=0, tiled=True)  7.32 us
    all_to_all x1, waiting for transfers between devices, exchange(): return lax.all_to_all(blocks, AXES, split_axis=0, concat_axis=0, tiled=True)  6.72 us
    all_to_all x1, starting transfers between devices, fast_device(): share = lax.all_to_all(grads, 'dp', split_axis=0, concat_axis=0, tiled=True)  3.73 us
    dynamic_slice x3, local copies, waits for them, and re-layouts, of_rep(): lax.dynamic_index_in_dim(x.reshape(shape), rep, axis + 1, keepdims=False)  1.98 us
    squeeze x2, local copies, waits for them, and re-layouts, fast_device(): return (embedded, code_share, out_share, grad_pair[0], grad_pair[1])  1.35 us
    all_to_all x1, waiting for transfers between devices, fast_device(): share = lax.all_to_all(grads, 'dp', split_axis=0, concat_axis=0, tiled=True)  1.28 us
  transfers between devices with their start and end apart: 4, of which 2 were waited for; matrix products, arithmetic and copies ran while one was open for 13% of the time, Pallas kernels for 16%

profile of v2, /device:TPU:0, one launch (start us, length us, event | category | flops | bytes accessed | tf_op | source)
XLA Modules:
  0.0 50.6 jit_solution(7186633007239819263)
XLA Ops:
  1.3 1.2 %copy-done = bf16[512,1024]{1,0:T(8,128)(2,1)S(1)} copy-done((bf16[512,1024]{1,0:T(8,128)(2,1)S(1)}, bf16[512,1024]{1,0:T(8,128)(2,1)}, u32[]{:S(2)}) %copy-start) | copy-done | bytes 1048600
  2.5 0.8 %copy-done.5 = bf16[256,128]{1,0:T(8,128)(2,1)S(1)} copy-done((bf16[256,128]{1,0:T(8,128)(2,1)S(1)}, bf16[256,128]{1,0:T(8,128)(2,1)}, u32[]{:S(2)}) %copy-start.5) | copy-done | bytes 65560
  3.3 0.7 %copy-done.6 = s32[512]{0:T(512)S(1)} copy-done((s32[512]{0:T(512)S(1)}, s32[512]{0:T(512)}, u32[]{:S(2)}) %copy-start.6) | copy-done | bytes 2072
  4.0 0.7 %copy-done.8 = s32[512]{0:T(512)S(1)} copy-done((s32[512]{0:T(512)S(1)}, s32[512]{0:T(512)}, u32[]{:S(2)}) %copy-start.8) | copy-done | bytes 2072
  4.7 0.7 %copy-done.10 = s32[256]{0:T(256)S(1)} copy-done((s32[256]{0:T(256)S(1)}, s32[256]{0:T(256)}, u32[]{:S(2)}) %copy-start.10) | copy-done | bytes 1048
  5.4 1.9 %first.1 = (bf16[32,40,128]{2,1,0:T(8,128)(2,1)}, f32[256,1024]{1,0:T(8,128)S(1)}) custom-call(s32[1]{0:T(128)S(6)} %copy.31.count_ref, s32[1,256]{1,0:T(1,128)S(1)} %bitcast.40, s32[1,512]{1,0:T(1,128)S(1)} %bitcast.34, s32[1,512]{1,0:T(1,128)S(1)} %bitcast.37, bf16[512,1024]{1,0:T(8,128)(2,1)S(1)} %copy-done, bf16[256,128]{1,0:T(8,128)(2,1)S(1)} %copy-done.5), custom_call_target="tpu_custom_call" | custom-call | flops 1000000000 | bytes 1048576 | tf_op jit(solution)/shard_map/first/pallas_call | solution.py:455
  7.3 7.3 %all-to-all-start = ((bf16[32,40,128]{2,1,0:T(8,128)(2,1)}), bf16[32,40,128]{2,1,0:T(8,128)(2,1)S(1)}, u32[]{:S(2)}, u32[]{:S(2)}) async-start(bf16[32,40,128]{2,1,0:T(8,128)(2,1)} %get-tuple-element.15), calls=%async_computation | async-start | bytes 655360 | tf_op jit(solution)/shard_map/all_to_all | solution.py:30
  14.6 1.3 %copy.19 = bf16[512,1024]{0,1:T(8,128)(2,1)} copy(bf16[512,1024]{1,0:T(8,128)(2,1)S(1)} %copy-done.1) | data formatting | bytes 2097152 | tf_op args[4]
  16.0 0.1 reshape.90
  16.1 0.1 reshape.91
  16.2 0.1 reshape_reshape.7.bias_ref
  16.3 0.1 reshape_reshape.6.gain_ref
  16.4 1.9 %constant_dynamic-slice_fusion.2 = bf16[512,16,1,32]{0,3,2,1:T(8,128)(2,1)} fusion(bf16[512,16,2,32]{0,3,2,1:T(8,128)(2,1)} %bitcast.42, s32[]{:T(128)S(6)} %select_n.27), kind=kLoop, calls=%fused_computation.15 | loop fusion | bytes 1048580 | tf_op jit(solution)/shard_map/jit(dynamic_index_in_dim)/dynamic_slice | solution.py:483
  18.3 1.3 %copy.21.w_ref = bf16[512,512]{1,0:T(8,128)(2,1)S(1)} copy(bf16[512,512]{0,1:T(8,128)(2,1)} %bitcast.43) | data formatting | bytes 1048576 | tf_op jit(solution)/shard_map/reshape | solution.py:484
  19.5 0.1 constant_dynamic-slice_fusion
  19.7 0.2 pad_bitcast_fusion.3
  19.9 6.7 %all-to-all-done.recv_ref = bf16[32,40,128]{2,1,0:T(8,128)(2,1)S(1)} async-done(((bf16[32,40,128]{2,1,0:T(8,128)(2,1)}), bf16[32,40,128]{2,1,0:T(8,128)(2,1)S(1)}, u32[]{:S(2)}, u32[]{:S(2)}) %all-to-all-start) | async-done | bytes 327712 | tf_op jit(solution)/shard_map/all_to_all | solution.py:30
  26.7 2.6 %middle.1 = (bf16[16,88,128]{2,1,0:T(8,128)(2,1)}, f32[8,512]{1,0:T(8,128)S(1)}) custom-call(s32[1]{0:T(128)} %bitcast.4.place_ref, bf16[32,40,128]{2,1,0:T(8,128)(2,1)S(1)} %all-to-all-done.recv_ref, bf16[512,512]{1,0:T(8,128)(2,1)S(1)} %copy.21.w_ref, f32[1,512]{1,0:T(1,128)S(1)} %reshape_reshape.6.gain_ref, f32[1,512]{1,0:T(1,128)S(1)} %reshape_reshape.7.bias_ref, ...), custom_call_target="tpu_custom_call" | custom-call | flops 1000000000 | bytes 1048576 | tf_op jit(solution)/shard_map/middle/pallas_call | solution.py:455
  29.2 3.7 %all-to-all-start.1 = ((bf16[16,88,128]{2,1,0:T(8,128)(2,1)}), bf16[16,88,128]{2,1,0:T(8,128)(2,1)S(1)}, u32[]{:S(2)}, u32[]{:S(2)}) async-start(bf16[16,88,128]{2,1,0:T(8,128)(2,1)} %get-tuple-element.18), calls=%async_computation.1 | async-start | bytes 720896 | tf_op jit(solution)/shard_map/all_to_all | solution.py:500
  33.1 7.1 %owner.1 = (bf16[4,640,512]{2,1,0:T(8,128)(2,1)S(1)}, f32[640,128]{1,0:T(8,128)S(1)}, f32[640,128]{1,0:T(8,128)S(1)}) custom-call(bf16[32,40,128]{2,1,0:T(8,128)(2,1)S(1)} %all-to-all-done.recv_ref, bf16[4,512,128]{2,1,0:T(8,128)(2,1)S(1)} %pad_maximum_fusion.w_ref, s32[1,512]{1,0:T(1,128)S(1)} %bitcast.36, s32[1,512]{1,0:T(1,128)S(1)} %bitcast.39), custom_call_target="tpu_custom_call" | custom-call | flops 4000000000 | bytes 1048576 | tf_op jit(solution)/shard_map/owner/pallas_call | solution.py:455
  40.1 1.5 %copy-done.12 = bf16[4,640,512]{2,1,0:T(8,128)(2,1)} copy-done((bf16[4,640,512]{2,1,0:T(8,128)(2,1)}, bf16[4,640,512]{2,1,0:T(8,128)(2,1)S(1)}, u32[]{:S(2)}) %copy-start.12) | copy-done | bytes 2621464
  41.6 0.6 %fusion.2 = f32[]{:T(128)} fusion(bf16[32,40,128]{2,1,0:T(8,128)(2,1)S(1)} %all-to-all-done.recv_ref), kind=kLoop, calls=%fused_computation.10 | loop fusion | flops 63 | bytes 68 | tf_op jit(solution)/shard_map/reduce_sum | solution.py:510
  43.0 0.1 stack.44
  43.2 0.1 slice.36.inv_ref
  43.3 0.1 slice.34.mean_ref
  43.4 1.3 %all-to-all-done.1.recv_ref = bf16[16,88,128]{2,1,0:T(8,128)(2,1)S(1)} async-done(((bf16[16,88,128]{2,1,0:T(8,128)(2,1)}), bf16[16,88,128]{2,1,0:T(8,128)(2,1)S(1)}, u32[]{:S(2)}, u32[]{:S(2)}) %all-to-all-start.1) | async-done | bytes 360480 | tf_op jit(solution)/shard_map/all_to_all | solution.py:500
  44.6 1.7 %copy-done.13 = bf16[4,640,512]{2,1,0:T(8,128)(2,1)S(1)} copy-done((bf16[4,640,512]{2,1,0:T(8,128)(2,1)S(1)}, bf16[4,640,512]{2,1,0:T(8,128)(2,1)}, u32[]{:S(2)}) %copy-start.13) | copy-done | bytes 2621464
  46.4 1.4 %last.1 = (f32[32,512]{1,0:T(8,128)}, f32[32,128]{1,0:T(8,128)}, f32[8,512]{1,0:T(8,128)S(1)}) custom-call(s32[1]{0:T(128)} %bitcast.4.place_ref, s32[1]{0:T(128)} %bitcast.3.total_ref, bf16[16,88,128]{2,1,0:T(8,128)(2,1)S(1)} %all-to-all-done.1.recv_ref, bf16[4,640,512]{2,1,0:T(8,128)(2,1)S(1)} %copy-done.13, f32[640,128]{1,0:T(8,128)S(1)} %get-tuple-element.20.pre_ref, ...), custom_call_target="tpu_custom_call" | custom-call | flops 1000000000 | bytes 1048576 | tf_op jit(solution)/shard_map/last/pallas_call | solution.py:455
  47.8 1.3 %embed.1 = bf16[256,128]{1,0:T(8,128)(2,1)} custom-call(s32[1]{0:T(128)S(6)} %copy.31.count_ref, s32[1]{0:T(128)} %bitcast.3.total_ref, f32[256,1024]{1,0:T(8,128)S(1)} %get-tuple-element.16.pre_ref, f32[1,1024]{1,0:T(1,128)S(1)} %slice.34.mean_ref, f32[1,1024]{1,0:T(1,128)S(1)} %slice.36.inv_ref, f32[1,1024]{1,0:T(1,128)S(1)} %bitcast.33, ...), custom_call_target="tpu_custom_call" | custom-call | flops 1000000000 | bytes 1048576 | tf_op jit(solution)/shard_map/embed/pallas_call | solution.py:455
  49.1 0.1 stack.53
  49.3 0.7 %squeeze.15 = f32[1024]{0:T(1024)} reshape(f32[1,16,2,32]{3,2,1,0:T(2,128)S(1)} %get-tuple-element.29) | data formatting | bytes 8192 | tf_op jit(solution)/shard_map/squeeze | solution.py:532
  50.0 0.7 %squeeze.14 = f32[1024]{0:T(1024)} reshape(f32[1,16,2,32]{3,2,1,0:T(2,128)S(1)} %get-tuple-element.30) | data formatting | bytes 8192 | tf_op jit(solution)/shard_map/squeeze | solution.py:532
  (36 shorter events, 0.6 us)
Async XLA Ops:
  1.3 1.2 %copy-start = (bf16[512,1024]{1,0:T(8,128)(2,1)S(1)}, bf16[512,1024]{1,0:T(8,128)(2,1)}, u32[]{:S(2)}) copy-start(bf16[512,1024]{1,0:T(8,128)(2,1)} %w_ref.1) | copy-start | bytes 3145732
  2.5 0.8 %copy-start.5 = (bf16[256,128]{1,0:T(8,128)(2,1)S(1)}, bf16[256,128]{1,0:T(8,128)(2,1)}, u32[]{:S(2)}) copy-start(bf16[256,128]{1,0:T(8,128)(2,1)} %cot_ref.1) | copy-start | bytes 196612
  3.3 0.7 %copy-start.6 = (s32[512]{0:T(512)S(1)}, s32[512]{0:T(512)}, u32[]{:S(2)}) copy-start(s32[512]{0:T(512)} %param.12) | copy-start | bytes 6148
  4.0 0.7 %copy-start.8 = (s32[512]{0:T(512)S(1)}, s32[512]{0:T(512)}, u32[]{:S(2)}) copy-start(s32[512]{0:T(512)} %param.13) | copy-start | bytes 6148
  4.7 0.7 %copy-start.10 = (s32[256]{0:T(256)S(1)}, s32[256]{0:T(256)}, u32[]{:S(2)}) copy-start(s32[256]{0:T(256)} %param.10) | copy-start | bytes 3076
  5.4 9.2 %copy-start.1 = (bf16[512,1024]{1,0:T(8,128)(2,1)S(1)}, bf16[512,1024]{1,0:T(8,128)(2,1)}, u32[]{:S(2)}) copy-start(bf16[512,1024]{1,0:T(8,128)(2,1)} %w_ref.1) | copy-start | bytes 3145732
  5.4 10.6 %copy-start.4 = (f32[1024]{0:T(1024)S(1)}, f32[1024]{0:T(1024)}, u32[]{:S(2)}) copy-start(f32[1024]{0:T(1024)} %param.15) | copy-start | bytes 12292
  5.4 10.7 %copy-start.3 = (f32[1024]{0:T(1024)S(1)}, f32[1024]{0:T(1024)}, u32[]{:S(2)}) copy-start(f32[1024]{0:T(1024)} %param.16) | copy-start | bytes 12292
  7.3 12.4 %copy-start.2 = (bf16[1024,128]{1,0:T(8,128)(2,1)S(1)}, bf16[1024,128]{1,0:T(8,128)(2,1)}, u32[]{:S(2)}) copy-start(bf16[1024,128]{1,0:T(8,128)(2,1)} %w_out_ref.1) | copy-start | bytes 786436
  7.3 19.4 %all-to-all-start = ((bf16[32,40,128]{2,1,0:T(8,128)(2,1)}), bf16[32,40,128]{2,1,0:T(8,128)(2,1)S(1)}, u32[]{:S(2)}, u32[]{:S(2)}) async-start(bf16[32,40,128]{2,1,0:T(8,128)(2,1)} %get-tuple-element.15), calls=%async_computation | async-start | bytes 655360 | tf_op jit(solution)/shard_map/all_to_all | solution.py:30
  16.0 10.7 %copy-start.7 = (s32[512]{0:T(512)S(1)}, s32[512]{0:T(512)}, u32[]{:S(2)}) copy-start(s32[512]{0:T(512)} %param.12) | copy-start | bytes 6148
  16.0 10.7 %copy-start.9 = (s32[512]{0:T(512)S(1)}, s32[512]{0:T(512)}, u32[]{:S(2)}) copy-start(s32[512]{0:T(512)} %param.13) | copy-start | bytes 6148
  29.2 15.4 %all-to-all-start.1 = ((bf16[16,88,128]{2,1,0:T(8,128)(2,1)}), bf16[16,88,128]{2,1,0:T(8,128)(2,1)S(1)}, u32[]{:S(2)}, u32[]{:S(2)}) async-start(bf16[16,88,128]{2,1,0:T(8,128)(2,1)} %get-tuple-element.18), calls=%async_computation.1 | async-start | bytes 720896 | tf_op jit(solution)/shard_map/all_to_all | solution.py:500
  33.0 10.0 %collective-permute-start = (f32[2,512]{1,0:T(2,128)S(1)}, f32[2,512]{1,0:T(2,128)S(1)}, u32[]{:S(2)}, u32[]{:S(2)}) collective-permute-start(f32[2,512]{1,0:T(2,128)S(1)} %slice.32), channel_id=1, source_target_pairs={{0,1},{1,0},{2,3},{3,2},{4,5},{5,4},{6,7},{7,6},{8,9},{9,8},{10,11... | collective-permute-start | bytes 12296 | tf_op jit(solution)/shard_map/ppermute | solution.py:503
  40.1 1.5 %copy-start.12 = (bf16[4,640,512]{2,1,0:T(8,128)(2,1)}, bf16[4,640,512]{2,1,0:T(8,128)(2,1)S(1)}, u32[]{:S(2)}) copy-start(bf16[4,640,512]{2,1,0:T(8,128)(2,1)S(1)} %get-tuple-element.19.code_ref) | copy-start | bytes 7864324
  41.6 6.1 %copy-start.11 = (f32[128]{0:T(128)S(1)}, f32[128]{0:T(128)}, u32[]{:S(2)}) copy-start(f32[128]{0:T(128)} %param.18) | copy-start | bytes 1540
  44.6 1.7 %copy-start.13 = (bf16[4,640,512]{2,1,0:T(8,128)(2,1)S(1)}, bf16[4,640,512]{2,1,0:T(8,128)(2,1)}, u32[]{:S(2)}) copy-start(bf16[4,640,512]{2,1,0:T(8,128)(2,1)} %copy-done.12) | copy-start | bytes 7864324
  47.8 1.4 %collective-permute-start.1 = (f32[2,512]{1,0:T(2,128)S(1)}, f32[2,512]{1,0:T(2,128)S(1)}, u32[]{:S(2)}, u32[]{:S(2)}) collective-permute-start(f32[2,512]{1,0:T(2,128)S(1)} %slice.37), channel_id=1, source_target_pairs={{0,1},{1,0},{2,3},{3,2},{4,5},{5,4},{6,7},{7,6},{8,9},{9,8},{10,11... | collective-permute-start | bytes 12296 | tf_op jit(solution)/shard_map/ppermute | solution.py:503

commit v3 on v2

v3 whole, which is shorter than its diff:
```python
import functools
import math

import jax
import jax.numpy as jnp
from jax import lax
from jax.experimental import pallas as pl
from jax.experimental.pallas import tpu as pltpu
from jax.sharding import PartitionSpec as P

LANES = 128
modulus = 65521
epsilon = 1e-05
AXES = ("dp", "rep")


def hashed(ident, hash_scale, hash_shift):
    resid = ident % modulus
    bucket = (hash_scale[None, :] * resid[:, None] + hash_shift[None, :]) % modulus
    return (bucket.astype(jnp.float32) * (2.0 / (modulus - 1)) - 1.0).astype(jnp.bfloat16)


def mish_parts(gated):
    softer = jax.nn.softplus(gated)
    tangent = jnp.tanh(softer)
    return (gated * tangent, tangent + gated * (1.0 - tangent * tangent) * jax.nn.sigmoid(gated))


def exchange(blocks):
    return lax.all_to_all(blocks, AXES, split_axis=0, concat_axis=0, tiled=True)


def lane_rows(flat):
    pad = -flat.shape[-1] % (8 * LANES)
    flat = jnp.pad(flat, [(0, 0)] * (flat.ndim - 1) + [(0, pad)])
    return flat.reshape(flat.shape[:-1] + (-1, LANES))


def general_device(
    ids, counts, hash_scale, hash_shift, w_code, norm_gain, norm_bias, w_out, out_bias, cotangent
):
    devices = lax.axis_size("dp") * lax.axis_size("rep")
    me = lax.axis_index("dp") * lax.axis_size("rep") + lax.axis_index("rep")
    slots = ids.shape[0]
    codes, hidden = w_code.shape
    width = w_out.shape[1]
    share = hidden // devices
    keep = (jnp.arange(slots, dtype=jnp.int32) < counts[0])[:, None]

    preact = jnp.dot(
        hashed(ids, hash_scale, hash_shift), w_code, preferred_element_type=jnp.float32
    )
    masked = jnp.where(keep, preact, 0.0)
    row = lane_rows(
        jnp.concatenate(
            [
                masked.sum(0),
                (masked * masked).sum(0),
                ids.astype(jnp.float32),
                counts.astype(jnp.float32),
            ]
        )
    )
    table = exchange(jnp.broadcast_to(row, (devices,) + row.shape)).reshape(devices, -1)
    sums = table[:, : 2 * hidden].sum(0)
    all_ids = table[:, 2 * hidden : 2 * hidden + slots].astype(jnp.int32)
    all_counts = table[:, 2 * hidden + slots].astype(jnp.int32)
    total = all_counts.sum().astype(jnp.float32)
    mean = sums[:hidden] / total
    inv_std = lax.rsqrt(sums[hidden:] / total - mean * mean + epsilon)

    normed = (preact - mean) * inv_std
    act_full, slope = mish_parts(normed * norm_gain + norm_bias)
    act = act_full.astype(jnp.bfloat16)
    delta = jnp.where(keep, cotangent.astype(jnp.float32) * lax.rsqrt(total), 0.0).astype(
        jnp.bfloat16
    )
    dval = (
        lax.dot_general(delta, w_out, (((1,), (1,)), ((), ())), preferred_element_type=jnp.float32)
        * slope
    )
    grad_out = lax.dot_general(
        act, delta, (((0,), (0,)), ((), ())), preferred_element_type=jnp.float32
    )
    columns = exchange(dval.astype(jnp.bfloat16).T.reshape(devices, share, slots))
    pair = jnp.concatenate([(dval * normed).sum(0), dval.sum(0)])
    grads = exchange(
        lane_rows(
            jnp.concatenate(
                [
                    grad_out.reshape(devices, share * width),
                    jnp.broadcast_to(pair, (devices, 2 * hidden)),
                ],
                axis=1,
            )
        )
    )
    grads = grads.reshape(devices, -1)[:, : share * width + 2 * hidden].sum(0)
    out_share = grads[: share * width].reshape(share, width)
    grad_gain = grads[share * width : share * width + hidden]
    grad_bias = grads[share * width + hidden :]

    embedded = jnp.dot(act, w_out, preferred_element_type=jnp.float32) + out_bias
    embedded = jnp.where(keep, embedded, 0.0).astype(jnp.bfloat16)

    def own(vector):
        return lax.dynamic_slice_in_dim(vector, me * share, share, vector.ndim - 1)

    w_own = own(w_code)
    mean_own, inv_own = own(mean), own(inv_std)
    shift_own, tilt_own = own(grad_bias) / total, own(grad_gain) / total
    scale_own = own(norm_gain) * inv_own
    group = math.gcd(devices, max(1, 8192 // slots))

    def accumulate(index, grad_rows):
        start = index * group
        block_ids = lax.dynamic_slice_in_dim(all_ids, start, group, 0).reshape(-1)
        block_counts = lax.dynamic_slice_in_dim(all_counts, start, group, 0)
        block = lax.dynamic_slice_in_dim(columns, start, group, 0)
        code = hashed(block_ids, hash_scale, hash_shift)
        pre = lax.dot_general(
            w_own, code, (((0,), (1,)), ((), ())), preferred_element_type=jnp.float32
        )
        seen = (pre - mean_own[:, None]) * inv_own[:, None]
        dval_own = block.transpose(1, 0, 2).reshape(share, -1).astype(jnp.float32)
        dpre = scale_own[:, None] * (dval_own - shift_own[:, None] - seen * tilt_own[:, None])
        live = jnp.arange(slots, dtype=jnp.int32)[None, :] < block_counts[:, None]
        dpre = jnp.where(live.reshape(1, -1), dpre, 0.0).astype(jnp.bfloat16)
        return grad_rows + jnp.dot(dpre, code, preferred_element_type=jnp.float32)

    code_share = lax.fori_loop(
        0, devices // group, accumulate, jnp.zeros((share, codes), jnp.float32)
    )
    return embedded, code_share, out_share, grad_gain, grad_bias


def row_of(tiles):
    return jnp.concatenate(tiles, axis=1)


def place_block(tile, source, target, block):
    shift = ((target - source) * block) % LANES
    return pltpu.roll(tile, shift, 1) if shift else tile


def pick_blocks(x, chosen, block):
    per_tile = LANES // block
    lane = lax.broadcasted_iota(jnp.int32, (x.shape[0], LANES), 1) // block
    tiles = []
    for first in range(0, len(chosen), per_tile):
        tile = None
        for place, b in enumerate(chosen[first : first + per_tile]):
            start = b // per_tile * LANES
            piece = place_block(x[:, start : start + LANES], b % per_tile, place, block)
            tile = piece if tile is None else jnp.where(lane == place, piece, tile)
        tiles.append(tile)
    return tiles


def split_pair(x):
    high = x.astype(jnp.bfloat16).astype(jnp.float32)
    return high, (x - high).astype(jnp.bfloat16).astype(jnp.float32)


def codes_of(id_column, scale_row, shift_row):
    raw = scale_row * id_column + shift_row
    once = (raw - lax.shift_right_logical(raw, 16) * modulus).astype(jnp.float32)
    quotient = jnp.floor((once + 0.5) * (1.0 / modulus))
    bucket = once - quotient * float(modulus)
    return (bucket * (2.0 / (modulus - 1)) - 1.0).astype(jnp.bfloat16)


def mish_of(val):
    grown = jnp.exp(jnp.minimum(val, 20.0))
    n = grown * (grown + 2.0)
    inverse = 1.0 / (n + 2.0)
    t = n * inverse
    slope = t + val * (4.0 * grown * (1.0 + grown)) * (inverse * inverse)
    return val * t, slope


def dot_t(a, b):
    return lax.dot_general(a, b, (((1,), (1,)), ((), ())), preferred_element_type=jnp.float32)


def dot_rows(a, b):
    return lax.dot_general(a, b, (((0,), (0,)), ((), ())), preferred_element_type=jnp.float32)


def one_hot(condition):
    return jnp.where(condition, 1.0, 0.0).astype(jnp.bfloat16)


def id_bytes(ids_row):
    resid = lax.rem(ids_row, modulus)
    high = lax.shift_right_logical(resid, 8).astype(jnp.float32)
    low = lax.bitwise_and(resid, 255).astype(jnp.float32)
    return high, low, jnp.zeros((6, ids_row.shape[1]), jnp.float32)


def slot_codes(high, low, blank, scale_row, shift_row):
    slots = high.shape[1]
    same = one_hot(
        lax.broadcasted_iota(jnp.int32, (slots, slots), 0)
        == lax.broadcasted_iota(jnp.int32, (slots, slots), 1)
    )
    pieces = jnp.concatenate([high, low, blank], axis=0).astype(jnp.bfloat16)
    columns = dot_t(same, pieces)
    id_column = (columns[:, 0:1] * 256.0 + columns[:, 1:2]).astype(jnp.int32)
    return codes_of(id_column, scale_row, shift_row)


def first_kernel(
    dims, count_ref, ids_hbm, scale_hbm, shift_hbm, w_hbm, cot_hbm, send_ref,
    ids_ref, scale_ref, shift_ref, w_ref, cot_ref, sems,
):
    chips, reps, take, block = dims.chips, dims.reps, dims.take, dims.block
    slots = dims.slots
    copies = [
        pltpu.make_async_copy(source, target, sems.at[i])
        for i, (source, target) in enumerate(
            [
                (ids_hbm, ids_ref),
                (scale_hbm, scale_ref),
                (shift_hbm, shift_ref),
                (w_hbm, w_ref),
                (cot_hbm, cot_ref),
            ]
        )
    ]
    for copy in copies:
        copy.start()
    count = count_ref[0]
    r = lax.broadcasted_iota(jnp.int32, (slots, slots), 0)
    c = lax.broadcasted_iota(jnp.int32, (slots, slots), 1)
    order = one_hot(c == (r % take) * chips + r // take)
    for copy in copies[:3]:
        copy.wait()
    high, low, blank = id_bytes(ids_ref[...])
    codes = slot_codes(high, low, blank, scale_ref[...], shift_ref[...])
    live = lax.broadcasted_iota(jnp.int32, (1, slots), 1) < count
    marked = jnp.concatenate([jnp.where(live, high, 256.0), low, blank], axis=0)
    by_chip = dot_t(marked.astype(jnp.bfloat16), order)
    tail = [
        by_chip[i : i + 1, t * LANES : (t + 1) * LANES]
        for i in range(2)
        for t in range(slots // LANES)
    ]
    for copy in copies[3:]:
        copy.wait()
    pre = jnp.dot(codes, w_ref[...], preferred_element_type=jnp.float32)
    moved = jnp.dot(order, cot_ref[...], preferred_element_type=jnp.float32).astype(jnp.bfloat16)
    keep = lax.broadcasted_iota(jnp.int32, (slots, 1), 0) < count
    sums = jnp.where(keep, pre, 0.0).sum(0, keepdims=True)
    apart = jnp.where(keep, pre - sums / count.astype(jnp.float32), 0.0)
    spread = (apart * apart).sum(0, keepdims=True)
    stats = jnp.concatenate(split_pair(sums) + (spread,), axis=0)
    for rep in range(reps):
        tiles = pick_blocks(stats, [k * reps + rep for k in range(chips)], block)
        lower = jnp.concatenate(tiles + tail, axis=0).astype(jnp.bfloat16)
        for k in range(chips):
            send_ref[k * reps + rep, :take, :] = moved[k * take : (k + 1) * take, :]
            send_ref[k * reps + rep, take:, :] = lower


def id_rows(dims, recv):
    base = dims.take + dims.stat_rows
    parts = dims.slots // LANES
    rows = dims.devices * dims.take
    spread = one_hot(
        lax.broadcasted_iota(jnp.int32, (rows, dims.devices), 0) // dims.take
        == lax.broadcasted_iota(jnp.int32, (rows, dims.devices), 1)
    )
    own_j = (
        lax.broadcasted_iota(jnp.int32, (rows, dims.slots), 1) % dims.take
        == lax.broadcasted_iota(jnp.int32, (rows, dims.slots), 0) % dims.take
    )
    fold = one_hot(
        lax.broadcasted_iota(jnp.int32, (dims.chips, dims.slots), 1) // dims.take
        == lax.broadcasted_iota(jnp.int32, (dims.chips, dims.slots), 0)
    )
    flats = [
        row_of([recv[:, base + i * parts + t, :] for t in range(parts)]) for i in range(2)
    ]
    counts = jnp.where(flats[0] < 255.5, 1.0, 0.0).sum(1, keepdims=True)
    tables = []
    for flat in flats:
        wide = jnp.dot(spread, flat.astype(jnp.bfloat16), preferred_element_type=jnp.float32)
        tables.append(dot_t(fold, jnp.where(own_j, wide, 0.0).astype(jnp.bfloat16)))
    return counts, tables[0] * 256.0 + tables[1]


def packing(dims, counts, chip):
    lanes = dims.devices * dims.take
    d = lax.broadcasted_iota(jnp.int32, (dims.devices, lanes), 0)
    l = lax.broadcasted_iota(jnp.int32, (dims.devices, lanes), 1) // dims.take
    j = (lax.broadcasted_iota(jnp.int32, (1, lanes), 1) % dims.take).astype(jnp.float32)
    live = jnp.maximum(jnp.floor((counts - chip + (dims.chips - 1.0)) * (1.0 / dims.chips)), 0.0)
    before = jnp.where(d < l, live, 0.0).sum(0, keepdims=True)
    here = jnp.where(d == l, live, 0.0).sum(0, keepdims=True)
    target = jnp.where(j < here, before + j, -1.0).astype(jnp.int32)
    return target, live.sum(0, keepdims=True)


def middle_kernel(
    dims, place_ref, recv_ref, w_ref, gain_ref, bias_ref, w_out_ref, scale_ref, shift_ref, _,
    send_ref, stat_ref,
):
    take, block, rows = dims.take, dims.block, dims.rows
    half, groups = dims.half, dims.groups
    chip = place_ref[0]
    recv = recv_ref[:, take:, :].astype(jnp.float32)
    recv_all = jnp.concatenate([jnp.zeros((dims.devices, take, LANES), jnp.float32), recv], axis=1)
    counts, ids = id_rows(dims, recv_all)
    total = counts.sum(0, keepdims=True)
    target, _ = packing(dims, counts, chip.astype(jnp.float32))
    hit = lax.broadcasted_iota(jnp.int32, (rows, dims.devices * take), 0) == target
    own = lax.broadcasted_iota(jnp.int32, (dims.chips, 1), 0) == chip
    own_ids = jnp.where(own, ids, 0.0).sum(0, keepdims=True)
    id_column = jnp.where(hit, own_ids, 0.0).sum(1, keepdims=True).astype(jnp.int32)
    codes = codes_of(id_column, scale_ref[...], shift_ref[...])
    pre = jnp.dot(codes, w_ref[...], preferred_element_type=jnp.float32)
    cot = jnp.dot(
        one_hot(hit), recv_ref[:, :take, :].reshape(dims.devices * take, LANES),
        preferred_element_type=jnp.float32,
    )
    means, variances = [], []
    for t in range(half // LANES):
        r = 3 * t
        sums = recv[:, r, :] + recv[:, r + 1, :]
        mean = sums.sum(0, keepdims=True) / total
        off = sums / counts - mean
        means.append(mean)
        variances.append((recv[:, r + 2, :] + counts * (off * off)).sum(0, keepdims=True) / total)
    mean = row_of(means)
    inv_std = lax.rsqrt(row_of(variances) + epsilon)
    stat_ref[...] = jnp.concatenate(
        [mean, inv_std, jnp.zeros((6, half), jnp.float32) + total], axis=0
    )
    normed = (pre - mean) * inv_std
    act, slope = mish_of(normed * gain_ref[...] + bias_ref[...])
    delta = (cot * lax.rsqrt(total)).astype(jnp.bfloat16)
    dval = dot_t(delta, w_out_ref[...]) * slope
    grad_out = dot_rows(act.astype(jnp.bfloat16), delta).astype(jnp.bfloat16)
    pair = [(dval * normed).sum(0, keepdims=True), dval.sum(0, keepdims=True)]
    pair = jnp.concatenate(
        [x[:, t * LANES : (t + 1) * LANES] for x in pair for t in range(half // LANES)], axis=0
    ).astype(jnp.bfloat16)
    part = rows // groups
    lane = lax.broadcasted_iota(jnp.int32, (part, LANES), 1) // block
    for k in range(dims.chips):
        start = k // groups * LANES
        tile = None
        for q in range(groups):
            piece = dval[q * part : (q + 1) * part, start : start + LANES]
            piece = place_block(piece, k % groups, q, block)
            tile = piece if tile is None else jnp.where(lane == q, piece, tile)
        send_ref[k, :part, :] = tile.astype(jnp.bfloat16)
        send_ref[k, part : part + block, :] = grad_out[k * block : (k + 1) * block, :]
        send_ref[k, part + block :, :] = pair


def natural(dims, mine, other, rep):
    groups, reps, block = dims.groups, dims.reps, dims.block
    halves = [jnp.where(rep == 0, mine, other), jnp.where(rep == 0, other, mine)]
    lane = lax.broadcasted_iota(jnp.int32, (mine.shape[0], LANES), 1) // block
    tiles = []
    for first in range(0, dims.chips * reps, groups):
        tile = None
        for place in range(groups):
            k, p = (first + place) // reps, (first + place) % reps
            start = k // groups * LANES
            piece = place_block(halves[p][:, start : start + LANES], k % groups, place, block)
            tile = piece if tile is None else jnp.where(lane == place, piece, tile)
        tiles.append(tile)
    return row_of(tiles)


def embed_kernel(
    dims, count_ref, rep_ref, ids_ref, scale_ref, shift_ref, w_ref, mine_ref, other_ref, gain_ref,
    bias_ref, w_out_ref, out_bias_ref, out_ref, token_ref,
):
    codes = slot_codes(*id_bytes(ids_ref[...]), scale_ref[...], shift_ref[...])
    pre = jnp.dot(codes, w_ref[...], preferred_element_type=jnp.float32)
    moments = natural(dims, mine_ref[...], other_ref[...], rep_ref[0])
    normed = (pre - moments[0:1, :]) * moments[1:2, :]
    act, _ = mish_of(normed * gain_ref[...] + bias_ref[...])
    out = jnp.dot(act.astype(jnp.bfloat16), w_out_ref[...], preferred_element_type=jnp.float32)
    keep = lax.broadcasted_iota(jnp.int32, (dims.slots, 1), 0) < count_ref[0]
    out_ref[...] = jnp.where(keep, out + out_bias_ref[...], 0.0).astype(jnp.bfloat16)
    token_ref[...] = jnp.zeros((8, LANES), jnp.float32)


def spread_own(dims, x, chip):
    groups, block = dims.groups, dims.block
    lane = lax.broadcasted_iota(jnp.int32, (1, LANES), 1) // block
    own = jnp.zeros((1, LANES), jnp.float32)
    for t in range(dims.half // LANES):
        own = own + jnp.where(
            lane + t * groups == chip, x[:, t * LANES : (t + 1) * LANES], 0.0
        )
    out = own
    for i in range(1, groups):
        out = out + pltpu.roll(own, i * block, 1)
    return out


def owner_kernel(
    dims, place_ref, recv_ref, w_ref, scale_ref, shift_ref, stat_ref, _, fixed_ref, *code_refs
):
    counts, ids = id_rows(dims, recv_ref[...].astype(jnp.float32))
    part, block, groups = dims.rows // dims.groups, dims.block, dims.groups
    chip = place_ref[0]
    mean = spread_own(dims, stat_ref[0:1, :], chip)
    inv_std = spread_own(dims, stat_ref[1:2, :], chip)
    group = lax.broadcasted_iota(jnp.int32, (part, LANES), 1) // block
    row = lax.broadcasted_iota(jnp.int32, (part, LANES), 0)
    wide = lax.broadcasted_iota(jnp.int32, (dims.rows, dims.devices * dims.take), 0)
    pieces = [[] for _ in range(groups)]
    for s in range(dims.chips):
        target, live = packing(dims, counts, float(s))
        id_column = jnp.where(wide == target, ids[s : s + 1, :], 0.0).sum(1, keepdims=True)
        codes = codes_of(id_column.astype(jnp.int32), scale_ref[...], shift_ref[...])
        pre = jnp.dot(codes, w_ref[...], preferred_element_type=jnp.float32)
        for q in range(groups):
            code_refs[q][s * part : (s + 1) * part, :] = codes[q * part : (q + 1) * part, :]
            normed = (pre[q * part : (q + 1) * part, :] - mean) * inv_std
            piece = jnp.where(group == q, normed, jnp.where(group == (q + 1) % groups, 1.0, 0.0))
            piece = jnp.where((q * part + row).astype(jnp.float32) < live, piece, 0.0)
            pieces[q].append(piece)
    moved, plain = None, None
    for q in range(groups):
        term = dot_rows(
            jnp.concatenate(pieces[q], axis=0).astype(jnp.bfloat16), code_refs[q][...]
        )
        after = (q + 1) % groups
        own, ones = term[q * block : (q + 1) * block, :], term[after * block : (after + 1) * block, :]
        moved = own if moved is None else moved + own
        plain = ones if plain is None else plain + ones
    fixed_ref[:block, :] = moved
    fixed_ref[block:, :] = plain


def sums_kernel(dims, recv_ref, out_out_ref, pair_ref):
    part, block = dims.rows // dims.groups, dims.block
    pair = recv_ref[:, part + block :, :].astype(jnp.float32).sum(0)
    tiles = dims.half // LANES
    pair_ref[...] = jnp.concatenate(
        [row_of([pair[i * tiles + t : i * tiles + t + 1, :] for t in range(tiles)]) for i in range(2)]
        + [jnp.zeros((6, dims.half), jnp.float32)],
        axis=0,
    )
    out_out_ref[...] = recv_ref[:, part : part + block, :].astype(jnp.float32).sum(0)


def own_column(dims, x, chip):
    own = spread_own(dims, x, chip)
    spot = lax.broadcasted_iota(jnp.int32, (dims.block, LANES), 1)
    same = spot == lax.broadcasted_iota(jnp.int32, (dims.block, LANES), 0)
    return jnp.where(same, own, 0.0).sum(1, keepdims=True)


def last_kernel(
    dims, place_ref, recv_ref, fixed_ref, stat_ref, gain_ref, pair_ref, *refs
):
    part, block, groups = dims.rows // dims.groups, dims.block, dims.groups
    code_refs, code_out_ref, held, sems = list(refs[:groups]), refs[groups], refs[-2], refs[-1]
    copies = [
        pltpu.make_async_copy(code_refs[dims.near + i], held.at[i], sems.at[i])
        for i in range(groups - dims.near)
    ]
    for copy in copies:
        copy.start()
    chip = place_ref[0]
    total = stat_ref[2:3, :1]
    scale = own_column(dims, gain_ref[...] * stat_ref[1:2, :], chip)
    tilt = own_column(dims, pair_ref[0:1, :], chip) / total
    shift = own_column(dims, pair_ref[1:2, :], chip) / total
    dval = recv_ref[:, :part, :].reshape(dims.chips * part, LANES)
    out = -(shift * fixed_ref[block:, :] + tilt * fixed_ref[:block, :])
    for q in range(groups):
        if q >= dims.near:
            copies[q - dims.near].wait()
        code = code_refs[q][...] if q < dims.near else held[q - dims.near]
        out = out + dot_rows(dval, code)[q * block : (q + 1) * block, :]
    code_out_ref[...] = scale * out


def join_kernel(dims, rep_ref, mine_ref, other_ref, gain_ref, bias_ref):
    pair = natural(dims, mine_ref[...], other_ref[...], rep_ref[0])
    gain_ref[...] = pair[0:1, :]
    bias_ref[...] = pair[1:2, :]


class Dims:
    def __init__(self, mesh, slots, codes, hidden, width):
        self.chips, self.reps = mesh.shape["dp"], mesh.shape["rep"]
        self.devices = self.chips * self.reps
        self.slots, self.codes, self.hidden, self.width = slots, codes, hidden, width
        self.block = hidden // self.devices
        self.half = hidden // self.reps
        self.groups = LANES // max(1, self.block)
        self.near = self.groups // 2
        self.take = slots // self.chips
        bound = self.devices * slots // 4 // self.chips
        bound += self.devices * (self.chips - 1) // self.chips
        step = 8 * self.groups
        self.rows = min(-(-bound // step) * step, self.devices * self.take)
        self.stat_rows = 3 * self.half // LANES
        self.send_rows = self.take + self.stat_rows + 2 * slots // LANES
        self.grad_rows = self.rows // self.groups + self.block + 2 * self.half // LANES

    def fits(self):
        return (
            self.width == LANES
            and LANES % self.block == 0
            and self.block % 8 == 0
            and self.groups >= 2
            and self.take % 8 == 0
            and self.slots % LANES == 0
            and self.half % LANES == 0
            and self.codes % LANES == 0
            and self.chips <= LANES
            and self.slots <= 256
            and self.rows % (8 * self.groups) == 0
            and self.chips * self.rows * self.codes <= (1 << 22)
        )


def kernel_call(dims, body, outs, arguments, scalars, name, flops, hbm=(), scratch=(), vmem=16):
    specs = [pl.BlockSpec(memory_space=pltpu.SMEM)] * scalars
    for i in range(scalars, len(arguments)):
        specs.append(pl.BlockSpec(memory_space=pltpu.HBM if i in hbm else pltpu.VMEM))
    return pl.pallas_call(
        functools.partial(body, dims),
        out_shape=[jax.ShapeDtypeStruct(shape, kind) for shape, kind in outs],
        in_specs=specs,
        out_specs=[pl.BlockSpec(memory_space=pltpu.VMEM)] * len(outs),
        scratch_shapes=list(scratch),
        compiler_params=pltpu.CompilerParams(vmem_limit_bytes=vmem << 20),
        cost_estimate=pl.CostEstimate(flops=flops, bytes_accessed=1 << 20, transcendentals=0),
        name=name,
    )(*arguments)


def fast_device(
    dims, ids, counts, hash_scale, hash_shift, w_code, norm_gain, norm_bias, w_out, out_bias,
    cotangent,
):
    chips, reps, block, half = dims.chips, dims.reps, dims.block, dims.half
    dp, rep = lax.axis_index("dp"), lax.axis_index("rep")
    f32, bf16 = jnp.float32, jnp.bfloat16
    ids = ids.reshape(1, -1)
    scale_row, shift_row = hash_scale.reshape(1, -1), hash_shift.reshape(1, -1)
    loaded = (ids, scale_row, shift_row, w_code, cotangent)
    (send,) = kernel_call(
        dims, first_kernel,
        [((dims.devices, dims.send_rows, LANES), bf16)],
        (counts,) + loaded, 1, "first", 10**9, hbm=(1, 2, 3, 4, 5),
        scratch=[pltpu.VMEM(x.shape, x.dtype) for x in loaded]
        + [pltpu.SemaphoreType.DMA((len(loaded),))], vmem=60,
    )
    recv = exchange(send)

    def of_rep(x, axis):
        shape = x.shape[:axis] + (chips, reps, block) + x.shape[axis + 1 :]
        x = lax.dynamic_index_in_dim(x.reshape(shape), rep, axis + 1, keepdims=False)
        return x.reshape(x.shape[:axis] + (half,) + x.shape[axis + 2 :])

    place, side = dp.reshape(1).astype(jnp.int32), rep.reshape(1).astype(jnp.int32)
    w_half, w_out_half = of_rep(w_code, 1), of_rep(w_out, 0)
    gain_half = of_rep(norm_gain, 0).reshape(1, -1)
    bias_half = of_rep(norm_bias, 0).reshape(1, -1)
    w_own = lax.dynamic_slice_in_dim(w_code, (dp * reps + rep) * block, block, 1)
    w_own = jnp.concatenate([w_own] * dims.groups, axis=1)
    grads, stat = kernel_call(
        dims, middle_kernel,
        [((chips, dims.grad_rows, LANES), bf16), ((8, half), f32)],
        (place, recv, w_half, gain_half, bias_half, w_out_half, scale_row, shift_row, w_own), 1,
        "middle", 10**9,
    )
    share = lax.all_to_all(grads, "dp", split_axis=0, concat_axis=0, tiled=True)

    def partner(x):
        return lax.ppermute(x, "rep", [(i, (i + 1) % reps) for i in range(reps)])

    packed = chips * dims.rows // dims.groups
    embedded, token = kernel_call(
        dims, embed_kernel, [((dims.slots, dims.width), bf16), ((8, LANES), f32)],
        (
            counts, side, ids, scale_row, shift_row, w_code, stat, partner(stat), norm_gain.reshape(1, -1),
            norm_bias.reshape(1, -1), w_out, out_bias.reshape(1, -1),
        ),
        2, "embed", 10**9,
    )
    fixed, *code = kernel_call(
        dims, owner_kernel,
        [((2 * block, dims.codes), f32)] + [((packed, dims.codes), bf16)] * dims.groups,
        (place, recv, w_own, scale_row, shift_row, stat, token), 1, "owner", 4 * 10**9,
    )
    out_share, pair = kernel_call(
        dims, sums_kernel, [((block, dims.width), f32), ((8, half), f32)],
        (share,), 0, "sums", 10**8,
    )
    other = partner(pair)
    (code_share,) = kernel_call(
        dims, last_kernel, [((block, dims.codes), f32)],
        (
            place, share, fixed, stat, gain_half, pair, *code[: dims.near],
            *[pltpu.with_memory_space_constraint(x, pltpu.HBM) for x in code[dims.near :]],
        ),
        1, "last", 10**9, hbm=range(6 + dims.near, 6 + dims.groups),
        scratch=[
            pltpu.VMEM((dims.groups - dims.near, packed, dims.codes), bf16),
            pltpu.SemaphoreType.DMA((dims.groups - dims.near,)),
        ],
    )
    gain, bias = kernel_call(
        dims, join_kernel, [((1, dims.hidden), f32)] * 2, (side, pair, other), 1, "join", 10**6
    )
    return embedded, code_share, out_share, gain.reshape(-1), bias.reshape(-1)


def solution(mesh):
    rows = P(AXES)

    def per_device(*arguments):
        ids, w_code, w_out = arguments[0], arguments[4], arguments[7]
        dims = Dims(mesh, ids.shape[0], w_code.shape[0], w_code.shape[1], w_out.shape[1])
        if dims.reps == 2 and dims.fits():
            return fast_device(dims, *arguments)
        return general_device(*arguments)

    return jax.shard_map(
        per_device,
        mesh=mesh,
        in_specs=(rows, rows, P(), P(), P(), P(), P(), P(), P(), P(AXES, None)),
        out_specs=(P(AXES, None), P(AXES, None), P(AXES, None), P(), P()),
        check_vma=False,
    )
```

time: 51.2 us -> 43.6 us (0.85)
  local copies, waits for them, and re-layouts: 14.4 us -> 4.77 us
  waiting for transfers between devices: 8 us -> 10.4 us
  Pallas kernels: 14.2 us -> 15.4 us
  other arithmetic: 0.84 us -> 0.17 us
  between operations: 2.11 us -> 1.46 us
    unnamed x29 -> x21, local copies, waits for them, and re-layouts: 8.68 us -> 4.01 us
    dynamic_slice x3, local copies, waits for them, and re-layouts: 1.98 us -> 0.12 us  [of_rep(): lax.dynamic_index_in_dim(x.reshape(shape), rep, axis + 1, keepdims=False)]
    squeeze x2 -> x0, local copies, waits for them, and re-layouts: 1.35 us -> none  [fast_device(): return (embedded, code_share, out_share, grad_pair[0], grad_pair[1])]
    pallas_call x5 -> x7, Pallas kernels: 14.2 us -> 15.4 us  [kernel_call(): pl.pallas_call(functools.partial(body, dims), out_shape=[jax.ShapeDtypeSt...]
    all_to_all x1, waiting for transfers between devices: 6.72 us -> 7.92 us  [exchange(): return lax.all_to_all(blocks, AXES, split_axis=0, concat_axis=0, tiled=True)]
    ppermute x2, waiting for transfers between devices: 0.01 us -> 1.17 us  [partner(): return lax.ppermute(x, 'rep', [(i, (i + 1) % reps) for i in range(reps)])]
    reshape x1, local copies, waits for them, and re-layouts: 1.25 us -> 0.21 us  [of_rep(): return x.reshape(x.shape[:axis] + (half,) + x.shape[axis + 2:])]
    reduce_sum x1 -> x0, other arithmetic: 0.63 us -> none  [fast_device(): total[:, row, 0].astype(jnp.float32).sum().astype(jnp.int32).reshape(1)]
  transfers between devices with their start and end apart: 4 -> 4, of which waited for: 2 -> 3; matrix products, arithmetic and copies ran while one was open for 13% -> 3% of each run, Pallas kernels for 16% -> 21%
where the time goes in v3:
time: 43.6 us; the launch traced here: 43.2 us
  Pallas kernels  15.4 us (35%)
  starting transfers between devices  10.9 us (25%)
  waiting for transfers between devices  10.4 us (24%)
  local copies, waits for them, and re-layouts  4.77 us (11%)
  between operations  1.46 us (3%)
    pallas_call x7, Pallas kernels, kernel_call(): pl.pallas_call(functools.partial(body, dims), out_shape=[jax.ShapeDtypeSt...  15.4 us
    all_to_all x1, waiting for transfers between devices, exchange(): return lax.all_to_all(blocks, AXES, split_axis=0, concat_axis=0, tiled=True)  7.92 us
    all_to_all x1, starting transfers between devices, exchange(): return lax.all_to_all(blocks, AXES, split_axis=0, concat_axis=0, tiled=True)  7.33 us
    unnamed x21, local copies, waits for them, and re-layouts  4.01 us
    all_to_all x1, starting transfers between devices, fast_device(): share = lax.all_to_all(grads, 'dp', split_axis=0, concat_axis=0, tiled=True)  3.54 us
    all_to_all x1, waiting for transfers between devices, fast_device(): share = lax.all_to_all(grads, 'dp', split_axis=0, concat_axis=0, tiled=True)  1.34 us
    ppermute x2, waiting for transfers between devices, partner(): return lax.ppermute(x, 'rep', [(i, (i + 1) % reps) for i in range(reps)])  1.17 us
  transfers between devices with their start and end apart: 4, of which 3 were waited for; matrix products, arithmetic and copies ran while one was open for 3% of the time, Pallas kernels for 21%

profile of v3, /device:TPU:0, one launch (start us, length us, event | category | flops | bytes accessed | tf_op | source)
XLA Modules:
  0.0 43.2 jit_solution(13430195561653155390)
XLA Ops:
  1.3 2.8 %first.1 = bf16[32,32,128]{2,1,0:T(8,128)(2,1)} custom-call(s32[1]{0:T(128)S(6)} %copy.21.count_ref, s32[1,256]{1,0:T(1,128)} %bitcast.28, s32[1,512]{1,0:T(1,128)} %bitcast.20, s32[1,512]{1,0:T(1,128)} %bitcast.24, bf16[512,1024]{1,0:T(8,128)(2,1)} %w_ref.1, bf16[256,128]{1,0:T(8,128)(2,1)} %cot_hbm.1), custom_call_target="tpu_custom_call" | custom-call | flops 1000000000 | bytes 1048576 | tf_op jit(solution)/shard_map/first/pallas_call | solution.py:534
  4.0 7.3 %all-to-all-start = ((bf16[32,32,128]{2,1,0:T(8,128)(2,1)}), bf16[32,32,128]{2,1,0:T(8,128)(2,1)S(1)}, u32[]{:S(2)}, u32[]{:S(2)}) async-start(bf16[32,32,128]{2,1,0:T(8,128)(2,1)} %first.1), calls=%async_computation | async-start | bytes 524288 | tf_op jit(solution)/shard_map/all_to_all | solution.py:30
  11.4 0.5 %copy.17 = bf16[512,1024]{0,1:T(8,128)(2,1)S(1)} copy(bf16[512,1024]{1,0:T(8,128)(2,1)S(1)} %copy-done) | data formatting | bytes 2097152 | tf_op args[4]
  12.0 0.0 copy-start.2
  12.0 0.0 copy-start.1
  12.0 0.2 copy.19.w_ref
  12.3 0.4 %copy-done.2 = f32[1024]{0:T(1024)S(1)} copy-done((f32[1024]{0:T(1024)S(1)}, f32[1024]{0:T(1024)}, u32[]{:S(2)}) %copy-start.2) | copy-done | bytes 4120
  12.7 0.1 reshape.70
  12.8 0.6 %copy-done.3 = f32[1024]{0:T(1024)S(1)} copy-done((f32[1024]{0:T(1024)S(1)}, f32[1024]{0:T(1024)}, u32[]{:S(2)}) %copy-start.3) | copy-done | bytes 4120
  13.4 0.1 reshape.69
  13.5 0.1 dynamic-slice_reduce_fusion
  13.5 0.1 reshape_reshape.6.gain_ref
  13.6 0.1 reshape_reshape.7.bias_ref
  13.7 0.1 constant_dynamic-slice_fusion
  13.8 0.0 copy-start.5
  13.8 0.2 pad_maximum_fusion._.w_ref
  14.0 0.0 copy-start.4
  14.0 7.9 %all-to-all-done.recv_ref = bf16[32,32,128]{2,1,0:T(8,128)(2,1)S(1)} async-done(((bf16[32,32,128]{2,1,0:T(8,128)(2,1)}), bf16[32,32,128]{2,1,0:T(8,128)(2,1)S(1)}, u32[]{:S(2)}, u32[]{:S(2)}) %all-to-all-start) | async-done | bytes 262176 | tf_op jit(solution)/shard_map/all_to_all | solution.py:30
  22.0 2.2 %middle.1 = (bf16[16,80,128]{2,1,0:T(8,128)(2,1)}, f32[8,512]{1,0:T(8,128)S(1)}) custom-call(s32[1]{0:T(128)} %bitcast.4.place_ref, bf16[32,32,128]{2,1,0:T(8,128)(2,1)S(1)} %all-to-all-done.recv_ref, bf16[512,512]{1,0:T(8,128)(2,1)S(1)} %copy.19.w_ref, f32[1,512]{1,0:T(1,128)S(1)} %reshape_reshape.6.gain_ref, f32[1,512]{1,0:T(1,128)S(1)} %reshape_reshape.7.bias_ref, ...), custom_call_target="tpu_custom_call" | custom-call | flops 1000000000 | bytes 1048576 | tf_op jit(solution)/shard_map/middle/pallas_call | solution.py:534
  24.1 3.5 %all-to-all-start.1 = ((bf16[16,80,128]{2,1,0:T(8,128)(2,1)}), bf16[16,80,128]{2,1,0:T(8,128)(2,1)S(1)}, u32[]{:S(2)}, u32[]{:S(2)}) async-start(bf16[16,80,128]{2,1,0:T(8,128)(2,1)} %get-tuple-element.20), calls=%async_computation.1 | async-start | bytes 655360 | tf_op jit(solution)/shard_map/all_to_all | solution.py:582
  27.7 0.1 collective-permute-start
  27.8 1.2 %collective-permute-done.other_ref = f32[8,512]{1,0:T(8,128)S(1)} collective-permute-done((f32[8,512]{1,0:T(8,128)S(1)}, f32[8,512]{1,0:T(8,128)S(1)}, u32[]{:S(2)}, u32[]{:S(2)}) %collective-permute-start) | collective-permute-done | bytes 16416 | tf_op jit(solution)/shard_map/ppermute | solution.py:585
  28.9 0.7 %copy-done.6 = s32[256]{0:T(256)S(1)} copy-done((s32[256]{0:T(256)S(1)}, s32[256]{0:T(256)}, u32[]{:S(2)}) %copy-start.6) | copy-done | bytes 1048
  29.6 1.9 %embed.1 = (bf16[256,128]{1,0:T(8,128)(2,1)}, f32[8,128]{1,0:T(8,128)S(1)}) custom-call(s32[1]{0:T(128)S(6)} %copy.21.count_ref, s32[1]{0:T(128)} %bitcast.rep_ref, s32[1,256]{1,0:T(1,128)S(1)} %bitcast.29, s32[1,512]{1,0:T(1,128)S(1)} %bitcast.22, s32[1,512]{1,0:T(1,128)S(1)} %bitcast.26, bf16[512,1024]{1,0:T(8,128)(2,1)S(1)} %copy-done, ...), custom_call_target="tpu_custom_call" | custom-call | flops 1000000000 | bytes 1048576 | tf_op jit(solution)/shard_map/embed/pallas_call | solution.py:534
  31.5 4.7 %owner.1 = (f32[64,512]{1,0:T(8,128)S(1)}, bf16[640,512]{1,0:T(8,128)(2,1)S(1)}, bf16[640,512]{1,0:T(8,128)(2,1)S(1)}, bf16[640,512]{1,0:T(8,128)(2,1)S(1)}, bf16[640,512]{1,0:T(8,128)(2,1)S(1)}) custom-call(s32[1]{0:T(128)} %bitcast.4.place_ref, bf16[32,32,128]{2,1,0:T(8,128)(2,1)S(1)} %all-to-all-done.recv_ref, ...), custom_call_target="tpu_custom_call" | custom-call | flops 4000000000 | bytes 1048576 | tf_op jit(solution)/shard_map/owner/pallas_call | solution.py:534
  36.3 0.8 %copy-done.8 = bf16[640,512]{1,0:T(8,128)(2,1)} copy-done((bf16[640,512]{1,0:T(8,128)(2,1)}, bf16[640,512]{1,0:T(8,128)(2,1)S(1)}, u32[]{:S(2)}) %copy-start.8) | copy-done | bytes 655384
  37.1 0.9 %copy-done.9 = bf16[640,512]{1,0:T(8,128)(2,1)} copy-done((bf16[640,512]{1,0:T(8,128)(2,1)}, bf16[640,512]{1,0:T(8,128)(2,1)S(1)}, u32[]{:S(2)}) %copy-start.9) | copy-done | bytes 655384
  38.0 1.3 %all-to-all-done.1.recv_ref = bf16[16,80,128]{2,1,0:T(8,128)(2,1)S(1)} async-done(((bf16[16,80,128]{2,1,0:T(8,128)(2,1)}), bf16[16,80,128]{2,1,0:T(8,128)(2,1)S(1)}, u32[]{:S(2)}, u32[]{:S(2)}) %all-to-all-start.1) | async-done | bytes 327712 | tf_op jit(solution)/shard_map/all_to_all | solution.py:582
  39.3 0.6 %sums.1 = (f32[32,128]{1,0:T(8,128)}, f32[8,512]{1,0:T(8,128)S(1)}) custom-call(bf16[16,80,128]{2,1,0:T(8,128)(2,1)S(1)} %all-to-all-done.1.recv_ref), custom_call_target="tpu_custom_call" | custom-call | flops 100000000 | bytes 1048576 | tf_op jit(solution)/shard_map/sums/pallas_call | solution.py:534
  39.9 0.0 collective-permute-start.1
  39.9 2.5 %last.1 = f32[32,512]{1,0:T(8,128)} custom-call(s32[1]{0:T(128)} %bitcast.4.place_ref, bf16[16,80,128]{2,1,0:T(8,128)(2,1)S(1)} %all-to-all-done.1.recv_ref, f32[64,512]{1,0:T(8,128)S(1)} %get-tuple-element.22.fixed_ref, f32[8,512]{1,0:T(8,128)S(1)} %get-tuple-element.18.mine_ref.stat_ref, f32[1,512]{1,0:T(1,128)S(1)} %reshape_reshape.6.gain_ref, ...), custom_call_target="tpu_custom_call" | custom-call | flops 1000000000 | bytes 1048576 | tf_op jit(solution)/shard_map/last/pallas_call | solution.py:534
  42.5 0.7 %join.1 = (f32[1,1024]{1,0:T(1,128)}, f32[1,1024]{1,0:T(1,128)}) custom-call(s32[1]{0:T(128)} %bitcast.rep_ref, f32[8,512]{1,0:T(8,128)S(1)} %get-tuple-element.23.pair_ref.mine_ref, f32[8,512]{1,0:T(8,128)S(1)} %collective-permute-done.1.other_ref), custom_call_target="tpu_custom_call" | custom-call | flops 1000000 | bytes 1048576 | tf_op jit(solution)/shard_map/join/pallas_call | solution.py:534
  (14 shorter events, 0.1 us)
Async XLA Ops:
  1.3 10.1 %copy-start = (bf16[512,1024]{1,0:T(8,128)(2,1)S(1)}, bf16[512,1024]{1,0:T(8,128)(2,1)}, u32[]{:S(2)}) copy-start(bf16[512,1024]{1,0:T(8,128)(2,1)} %w_ref.1) | copy-start | bytes 3145732
  4.0 17.9 %all-to-all-start = ((bf16[32,32,128]{2,1,0:T(8,128)(2,1)}), bf16[32,32,128]{2,1,0:T(8,128)(2,1)S(1)}, u32[]{:S(2)}, u32[]{:S(2)}) async-start(bf16[32,32,128]{2,1,0:T(8,128)(2,1)} %first.1), calls=%async_computation | async-start | bytes 524288 | tf_op jit(solution)/shard_map/all_to_all | solution.py:30
  12.0 0.7 %copy-start.2 = (f32[1024]{0:T(1024)S(1)}, f32[1024]{0:T(1024)}, u32[]{:S(2)}) copy-start(f32[1024]{0:T(1024)} %param.16) | copy-start | bytes 12292
  12.0 1.7 %copy-start.1 = (bf16[1024,128]{1,0:T(8,128)(2,1)S(1)}, bf16[1024,128]{1,0:T(8,128)(2,1)}, u32[]{:S(2)}) copy-start(bf16[1024,128]{1,0:T(8,128)(2,1)} %w_out_ref.1) | copy-start | bytes 786436
  12.7 0.7 %copy-start.3 = (f32[1024]{0:T(1024)S(1)}, f32[1024]{0:T(1024)}, u32[]{:S(2)}) copy-start(f32[1024]{0:T(1024)} %param.15) | copy-start | bytes 12292
  13.8 8.1 %copy-start.5 = (s32[512]{0:T(512)S(1)}, s32[512]{0:T(512)}, u32[]{:S(2)}) copy-start(s32[512]{0:T(512)} %param.13) | copy-start | bytes 6148
  14.0 7.9 %copy-start.4 = (s32[512]{0:T(512)S(1)}, s32[512]{0:T(512)}, u32[]{:S(2)}) copy-start(s32[512]{0:T(512)} %param.12) | copy-start | bytes 6148
  24.1 15.2 %all-to-all-start.1 = ((bf16[16,80,128]{2,1,0:T(8,128)(2,1)}), bf16[16,80,128]{2,1,0:T(8,128)(2,1)S(1)}, u32[]{:S(2)}, u32[]{:S(2)}) async-start(bf16[16,80,128]{2,1,0:T(8,128)(2,1)} %get-tuple-element.20), calls=%async_computation.1 | async-start | bytes 655360 | tf_op jit(solution)/shard_map/all_to_all | solution.py:582
  27.7 1.2 %collective-permute-start = (f32[8,512]{1,0:T(8,128)S(1)}, f32[8,512]{1,0:T(8,128)S(1)}, u32[]{:S(2)}, u32[]{:S(2)}) collective-permute-start(f32[8,512]{1,0:T(8,128)S(1)} %get-tuple-element.18.mine_ref.stat_ref), channel_id=1, source_target_pairs={{0,1},{1,0},{2,3},{3,2},{4,5},{5,4},{6,7},{7,6},{8,9},{9,8},{10,11... | collective-permute-start | bytes 49160 | tf_op jit(solution)/shard_map/ppermute | solution.py:585
  28.9 0.7 %copy-start.6 = (s32[256]{0:T(256)S(1)}, s32[256]{0:T(256)}, u32[]{:S(2)}) copy-start(s32[256]{0:T(256)} %param.10) | copy-start | bytes 3076
  28.9 0.7 %copy-start.7 = (f32[128]{0:T(128)S(1)}, f32[128]{0:T(128)}, u32[]{:S(2)}) copy-start(f32[128]{0:T(128)} %param.18) | copy-start | bytes 1540
  36.3 0.8 %copy-start.8 = (bf16[640,512]{1,0:T(8,128)(2,1)}, bf16[640,512]{1,0:T(8,128)(2,1)S(1)}, u32[]{:S(2)}) copy-start(bf16[640,512]{1,0:T(8,128)(2,1)S(1)} %get-tuple-element.26.refs_2_) | copy-start | bytes 1966084
  37.1 0.9 %copy-start.9 = (bf16[640,512]{1,0:T(8,128)(2,1)}, bf16[640,512]{1,0:T(8,128)(2,1)S(1)}, u32[]{:S(2)}) copy-start(bf16[640,512]{1,0:T(8,128)(2,1)S(1)} %get-tuple-element.27.refs_3_) | copy-start | bytes 1966084
  39.9 2.5 %collective-permute-start.1 = (f32[8,512]{1,0:T(8,128)S(1)}, f32[8,512]{1,0:T(8,128)S(1)}, u32[]{:S(2)}, u32[]{:S(2)}) collective-permute-start(f32[8,512]{1,0:T(8,128)S(1)} %get-tuple-element.23.pair_ref.mine_ref), channel_id=1, source_target_pairs={{0,1},{1,0},{2,3},{3,2},{4,5},{5,4},{6,7},{7,6},{8,9},{9,8},{10,11... | collective-permute-start | bytes 49160 | tf_op jit(solution)/shard_map/ppermute | solution.py:585

commit v4 on v3

--- a/solution.py
+++ b/solution.py
@@ -9,6 +9,7 @@
 from jax.sharding import PartitionSpec as P
 
 LANES = 128
+PARTS = 4
 modulus = 65521
 epsilon = 1e-05
 AXES = ("dp", "rep")
@@ -304,7 +305,7 @@
 
 def middle_kernel(
     dims, place_ref, recv_ref, w_ref, gain_ref, bias_ref, w_out_ref, scale_ref, shift_ref, _,
-    send_ref, stat_ref,
+    send_ref, stat_ref, ids_ref, counts_ref,
 ):
     take, block, rows = dims.take, dims.block, dims.rows
     half, groups = dims.half, dims.groups
@@ -312,6 +313,8 @@
     recv = recv_ref[:, take:, :].astype(jnp.float32)
     recv_all = jnp.concatenate([jnp.zeros((dims.devices, take, LANES), jnp.float32), recv], axis=1)
     counts, ids = id_rows(dims, recv_all)
+    ids_ref[...] = ids
+    counts_ref[...] = jnp.zeros((dims.devices, LANES), jnp.float32) + counts
     total = counts.sum(0, keepdims=True)
     target, _ = packing(dims, counts, chip.astype(jnp.float32))
     hit = lax.broadcasted_iota(jnp.int32, (rows, dims.devices * take), 0) == target
@@ -377,11 +380,25 @@
 
 
 def embed_kernel(
-    dims, count_ref, rep_ref, ids_ref, scale_ref, shift_ref, w_ref, mine_ref, other_ref, gain_ref,
-    bias_ref, w_out_ref, out_bias_ref, out_ref, token_ref,
+    dims, count_ref, rep_ref, ids_ref, scale_ref, shift_ref, w_hbm, mine_ref, other_ref, gain_ref,
+    bias_ref, w_out_hbm, out_bias_ref, out_ref, token_ref, w_ref, w_out_ref, sems,
 ):
+    cut = dims.codes // 2
+    copies = [
+        pltpu.make_async_copy(
+            w_hbm.at[pl.ds(i * cut, cut)], w_ref.at[pl.ds(i * cut, cut)], sems.at[i]
+        )
+        for i in range(2)
+    ]
+    copies.append(pltpu.make_async_copy(w_out_hbm, w_out_ref, sems.at[2]))
+    for copy in copies:
+        copy.start()
     codes = slot_codes(*id_bytes(ids_ref[...]), scale_ref[...], shift_ref[...])
-    pre = jnp.dot(codes, w_ref[...], preferred_element_type=jnp.float32)
+    copies[0].wait()
+    pre = jnp.dot(codes[:, :cut], w_ref[:cut, :], preferred_element_type=jnp.float32)
+    copies[1].wait()
+    pre = pre + jnp.dot(codes[:, cut:], w_ref[cut:, :], preferred_element_type=jnp.float32)
+    copies[2].wait()
     moments = natural(dims, mine_ref[...], other_ref[...], rep_ref[0])
     normed = (pre - moments[0:1, :]) * moments[1:2, :]
     act, _ = mish_of(normed * gain_ref[...] + bias_ref[...])
@@ -405,10 +422,17 @@
     return out
 
 
+def codes_of_group(dims, code_refs, q):
+    return jnp.concatenate(
+        [ref[...] for ref in code_refs[q * dims.parts : (q + 1) * dims.parts]], axis=0
+    )
+
+
 def owner_kernel(
-    dims, place_ref, recv_ref, w_ref, scale_ref, shift_ref, stat_ref, _, fixed_ref, *code_refs
+    dims, place_ref, ids_ref, counts_ref, w_ref, scale_ref, shift_ref, stat_ref, _, fixed_ref,
+    *code_refs,
 ):
-    counts, ids = id_rows(dims, recv_ref[...].astype(jnp.float32))
+    counts = counts_ref[:, 0:1]
     part, block, groups = dims.rows // dims.groups, dims.block, dims.groups
     chip = place_ref[0]
     mean = spread_own(dims, stat_ref[0:1, :], chip)
@@ -419,11 +443,14 @@
     pieces = [[] for _ in range(groups)]
     for s in range(dims.chips):
         target, live = packing(dims, counts, float(s))
-        id_column = jnp.where(wide == target, ids[s : s + 1, :], 0.0).sum(1, keepdims=True)
+        id_column = jnp.where(wide == target, ids_ref[s : s + 1, :], 0.0).sum(1, keepdims=True)
         codes = codes_of(id_column.astype(jnp.int32), scale_ref[...], shift_ref[...])
         pre = jnp.dot(codes, w_ref[...], preferred_element_type=jnp.float32)
         for q in range(groups):
-            code_refs[q][s * part : (s + 1) * part, :] = codes[q * part : (q + 1) * part, :]
+            start = s * part
+            code_refs[q * dims.parts + start // dims.piece][
+                start % dims.piece : start % dims.piece + part, :
+            ] = codes[q * part : (q + 1) * part, :]
             normed = (pre[q * part : (q + 1) * part, :] - mean) * inv_std
             piece = jnp.where(group == q, normed, jnp.where(group == (q + 1) % groups, 1.0, 0.0))
             piece = jnp.where((q * part + row).astype(jnp.float32) < live, piece, 0.0)
@@ -431,26 +458,22 @@
     moved, plain = None, None
     for q in range(groups):
         term = dot_rows(
-            jnp.concatenate(pieces[q], axis=0).astype(jnp.bfloat16), code_refs[q][...]
+            jnp.concatenate(pieces[q], axis=0).astype(jnp.bfloat16), codes_of_group(dims, code_refs, q)
         )
         after = (q + 1) % groups
         own, ones = term[q * block : (q + 1) * block, :], term[after * block : (after + 1) * block, :]
         moved = own if moved is None else moved + own
         plain = ones if plain is None else plain + ones
     fixed_ref[:block, :] = moved
-    fixed_ref[block:, :] = plain
-
-
-def sums_kernel(dims, recv_ref, out_out_ref, pair_ref):
-    part, block = dims.rows // dims.groups, dims.block
-    pair = recv_ref[:, part + block :, :].astype(jnp.float32).sum(0)
+    fixed_ref[block:, :] = plain[:8, :]
+
+
+def pair_sums(dims, rows):
+    pair = rows.astype(jnp.float32).sum(0)
     tiles = dims.half // LANES
-    pair_ref[...] = jnp.concatenate(
-        [row_of([pair[i * tiles + t : i * tiles + t + 1, :] for t in range(tiles)]) for i in range(2)]
-        + [jnp.zeros((6, dims.half), jnp.float32)],
-        axis=0,
-    )
-    out_out_ref[...] = recv_ref[:, part : part + block, :].astype(jnp.float32).sum(0)
+    return [
+        row_of([pair[i * tiles + t : i * tiles + t + 1, :] for t in range(tiles)]) for i in range(2)
+    ]
 
 
 def own_column(dims, x, chip):
@@ -461,33 +484,30 @@
 
 
 def last_kernel(
-    dims, place_ref, recv_ref, fixed_ref, stat_ref, gain_ref, pair_ref, *refs
+    dims, place_ref, recv_ref, fixed_ref, stat_ref, gain_ref, *refs
 ):
     part, block, groups = dims.rows // dims.groups, dims.block, dims.groups
-    code_refs, code_out_ref, held, sems = list(refs[:groups]), refs[groups], refs[-2], refs[-1]
-    copies = [
-        pltpu.make_async_copy(code_refs[dims.near + i], held.at[i], sems.at[i])
-        for i in range(groups - dims.near)
-    ]
-    for copy in copies:
-        copy.start()
+    code_refs, (code_out_ref, out_out_ref) = refs[:-2], refs[-2:]
     chip = place_ref[0]
     total = stat_ref[2:3, :1]
     scale = own_column(dims, gain_ref[...] * stat_ref[1:2, :], chip)
-    tilt = own_column(dims, pair_ref[0:1, :], chip) / total
-    shift = own_column(dims, pair_ref[1:2, :], chip) / total
+    gain, bias = pair_sums(dims, recv_ref[:, part + block :, :])
+    tilt = own_column(dims, gain, chip) / total
+    shift = own_column(dims, bias, chip) / total
+    out_out_ref[...] = recv_ref[:, part : part + block, :].astype(jnp.float32).sum(0)
     dval = recv_ref[:, :part, :].reshape(dims.chips * part, LANES)
-    out = -(shift * fixed_ref[block:, :] + tilt * fixed_ref[:block, :])
+    out = -(shift * fixed_ref[block : block + 1, :] + tilt * fixed_ref[:block, :])
     for q in range(groups):
-        if q >= dims.near:
-            copies[q - dims.near].wait()
-        code = code_refs[q][...] if q < dims.near else held[q - dims.near]
-        out = out + dot_rows(dval, code)[q * block : (q + 1) * block, :]
+        out = out + dot_rows(dval, codes_of_group(dims, code_refs, q))[q * block : (q + 1) * block, :]
     code_out_ref[...] = scale * out
 
 
 def join_kernel(dims, rep_ref, mine_ref, other_ref, gain_ref, bias_ref):
-    pair = natural(dims, mine_ref[...], other_ref[...], rep_ref[0])
+    blank = jnp.zeros((6, dims.half), jnp.float32)
+    mine, other = (
+        jnp.concatenate(pair_sums(dims, ref[...]) + [blank], axis=0) for ref in (mine_ref, other_ref)
+    )
+    pair = natural(dims, mine, other, rep_ref[0])
     gain_ref[...] = pair[0:1, :]
     bias_ref[...] = pair[1:2, :]
 
@@ -500,12 +520,13 @@
         self.block = hidden // self.devices
         self.half = hidden // self.reps
         self.groups = LANES // max(1, self.block)
-        self.near = self.groups // 2
         self.take = slots // self.chips
+        self.parts = PARTS
         bound = self.devices * slots // 4 // self.chips
         bound += self.devices * (self.chips - 1) // self.chips
         step = 8 * self.groups
         self.rows = min(-(-bound // step) * step, self.devices * self.take)
+        self.piece = self.chips * self.rows // self.groups // self.parts
         self.stat_rows = 3 * self.half // LANES
         self.send_rows = self.take + self.stat_rows + 2 * slots // LANES
         self.grad_rows = self.rows // self.groups + self.block + 2 * self.half // LANES
@@ -515,7 +536,7 @@
             self.width == LANES
             and LANES % self.block == 0
             and self.block % 8 == 0
-            and self.groups >= 2
+            and self.chips % self.parts == 0
             and self.take % 8 == 0
             and self.slots % LANES == 0
             and self.half % LANES == 0
@@ -573,9 +594,14 @@
     bias_half = of_rep(norm_bias, 0).reshape(1, -1)
     w_own = lax.dynamic_slice_in_dim(w_code, (dp * reps + rep) * block, block, 1)
     w_own = jnp.concatenate([w_own] * dims.groups, axis=1)
-    grads, stat = kernel_call(
+    grads, stat, all_ids, all_counts = kernel_call(
         dims, middle_kernel,
-        [((chips, dims.grad_rows, LANES), bf16), ((8, half), f32)],
+        [
+            ((chips, dims.grad_rows, LANES), bf16),
+            ((8, half), f32),
+            ((chips, dims.devices * dims.take), f32),
+            ((dims.devices, LANES), f32),
+        ],
         (place, recv, w_half, gain_half, bias_half, w_out_half, scale_row, shift_row, w_own), 1,
         "middle", 10**9,
     )
@@ -588,32 +614,28 @@
     embedded, token = kernel_call(
         dims, embed_kernel, [((dims.slots, dims.width), bf16), ((8, LANES), f32)],
         (
-            counts, side, ids, scale_row, shift_row, w_code, stat, partner(stat), norm_gain.reshape(1, -1),
-            norm_bias.reshape(1, -1), w_out, out_bias.reshape(1, -1),
+            counts, side, ids, scale_row, shift_row,
+            pltpu.with_memory_space_constraint(w_code, pltpu.HBM), stat, partner(stat),
+            norm_gain.reshape(1, -1), norm_bias.reshape(1, -1),
+            pltpu.with_memory_space_constraint(w_out, pltpu.HBM), out_bias.reshape(1, -1),
         ),
-        2, "embed", 10**9,
+        2, "embed", 10**9, hbm=(5, 10),
+        scratch=[
+            pltpu.VMEM(w_code.shape, bf16), pltpu.VMEM(w_out.shape, bf16),
+            pltpu.SemaphoreType.DMA((3,)),
+        ],
     )
     fixed, *code = kernel_call(
         dims, owner_kernel,
-        [((2 * block, dims.codes), f32)] + [((packed, dims.codes), bf16)] * dims.groups,
-        (place, recv, w_own, scale_row, shift_row, stat, token), 1, "owner", 4 * 10**9,
-    )
-    out_share, pair = kernel_call(
-        dims, sums_kernel, [((block, dims.width), f32), ((8, half), f32)],
-        (share,), 0, "sums", 10**8,
-    )
+        [((block + 8, dims.codes), f32)] + [((dims.piece, dims.codes), bf16)] * (dims.groups * dims.parts),
+        (place, all_ids, all_counts, w_own, scale_row, shift_row, stat, token), 1,
+        "owner", 4 * 10**9,
+    )
+    pair = share[:, dims.rows // dims.groups + block :, :]
     other = partner(pair)
-    (code_share,) = kernel_call(
-        dims, last_kernel, [((block, dims.codes), f32)],
-        (
-            place, share, fixed, stat, gain_half, pair, *code[: dims.near],
-            *[pltpu.with_memory_space_constraint(x, pltpu.HBM) for x in code[dims.near :]],
-        ),
-        1, "last", 10**9, hbm=range(6 + dims.near, 6 + dims.groups),
-        scratch=[
-            pltpu.VMEM((dims.groups - dims.near, packed, dims.codes), bf16),
-            pltpu.SemaphoreType.DMA((dims.groups - dims.near,)),
-        ],
+    code_share, out_share = kernel_call(
+        dims, last_kernel, [((block, dims.codes), f32), ((block, dims.width), f32)],
+        (place, share, fixed, stat, gain_half, *code), 1, "last", 10**9,
     )
     gain, bias = kernel_call(
         dims, join_kernel, [((1, dims.hidden), f32)] * 2, (side, pair, other), 1, "join", 10**6

time: 43.6 us -> 41.7 us (0.956)
  local copies, waits for them, and re-layouts: 4.77 us -> 3.07 us
  Pallas kernels: 15.4 us -> 14.3 us
  waiting for transfers between devices: 10.4 us -> 11.3 us
    unnamed x21 -> x17, local copies, waits for them, and re-layouts: 4.01 us -> 2.31 us
    pallas_call x7 -> x6, Pallas kernels: 15.4 us -> 14.3 us  [kernel_call(): pl.pallas_call(functools.partial(body, dims), out_shape=[jax.ShapeDtypeSt...]
    all_to_all x1, waiting for transfers between devices: 1.34 us -> 2.22 us  [fast_device(): share = lax.all_to_all(grads, 'dp', split_axis=0, concat_axis=0, tiled=True)]
  transfers between devices with their start and end apart: 4 -> 4, of which waited for: 3 -> 3; matrix products, arithmetic and copies ran while one was open for 3% -> 4% of each run, Pallas kernels for 21% -> 21%
where the time goes in v4:
time: 41.7 us; the launch traced here: 41.3 us
  Pallas kernels  14.3 us (34%)
  waiting for transfers between devices  11.3 us (27%)
  starting transfers between devices  10.9 us (26%)
  local copies, waits for them, and re-layouts  3.07 us (7%)
  between operations  1.44 us (3%)
    pallas_call x6, Pallas kernels, kernel_call(): pl.pallas_call(functools.partial(body, dims), out_shape=[jax.ShapeDtypeSt...  14.3 us
    all_to_all x1, waiting for transfers between devices, exchange(): return lax.all_to_all(blocks, AXES, split_axis=0, concat_axis=0, tiled=True)  7.92 us
    all_to_all x1, starting transfers between devices, exchange(): return lax.all_to_all(blocks, AXES, split_axis=0, concat_axis=0, tiled=True)  7.33 us
    all_to_all x1, starting transfers between devices, fast_device(): share = lax.all_to_all(grads, 'dp', split_axis=0, concat_axis=0, tiled=True)  3.54 us
    unnamed x17, local copies, waits for them, and re-layouts  2.31 us
    all_to_all x1, waiting for transfers between devices, fast_device(): share = lax.all_to_all(grads, 'dp', split_axis=0, concat_axis=0, tiled=True)  2.22 us
    ppermute x2, waiting for transfers between devices, partner(): return lax.ppermute(x, 'rep', [(i, (i + 1) % reps) for i in range(reps)])  1.17 us
  transfers between devices with their start and end apart: 4, of which 3 were waited for; matrix products, arithmetic and copies ran while one was open for 4% of the time, Pallas kernels for 21%

profile of v4, /device:TPU:0, one launch (start us, length us, event | category | flops | bytes accessed | tf_op | source)
XLA Modules:
  0.0 41.3 jit_solution(12606550077621376607)
XLA Ops:
  1.3 0.0 copy-start.6
  1.3 2.8 %first.1 = bf16[32,32,128]{2,1,0:T(8,128)(2,1)} custom-call(s32[1]{0:T(128)S(6)} %copy.21.count_ref, s32[1,256]{1,0:T(1,128)} %bitcast.27, s32[1,512]{1,0:T(1,128)} %bitcast.19, s32[1,512]{1,0:T(1,128)} %bitcast.23, bf16[512,1024]{1,0:T(8,128)(2,1)} %w_hbm.3, bf16[256,128]{1,0:T(8,128)(2,1)} %cot_hbm.1), custom_call_target="tpu_custom_call" | custom-call | flops 1000000000 | bytes 1048576 | tf_op jit(solution)/shard_map/first/pallas_call | solution.py:555
  4.1 7.3 %all-to-all-start = ((bf16[32,32,128]{2,1,0:T(8,128)(2,1)}), bf16[32,32,128]{2,1,0:T(8,128)(2,1)S(1)}, u32[]{:S(2)}, u32[]{:S(2)}) async-start(bf16[32,32,128]{2,1,0:T(8,128)(2,1)} %first.1), calls=%async_computation | async-start | bytes 524288 | tf_op jit(solution)/shard_map/all_to_all | solution.py:31
  11.4 0.5 %copy.17 = bf16[512,1024]{0,1:T(8,128)(2,1)S(1)} copy(bf16[512,1024]{1,0:T(8,128)(2,1)S(1)} %copy-done.6) | data formatting | bytes 2097152 | tf_op args[4]
  12.0 0.0 copy-start
  12.0 0.0 copy-start.7
  12.1 0.2 copy.19.w_ref
  12.3 0.4 %copy-done = f32[1024]{0:T(1024)S(1)} copy-done((f32[1024]{0:T(1024)S(1)}, f32[1024]{0:T(1024)}, u32[]{:S(2)}) %copy-start) | copy-done | bytes 4120
  12.7 0.1 reshape.70
  12.8 0.6 %copy-done.1 = f32[1024]{0:T(1024)S(1)} copy-done((f32[1024]{0:T(1024)S(1)}, f32[1024]{0:T(1024)}, u32[]{:S(2)}) %copy-start.1) | copy-done | bytes 4120
  13.4 0.1 reshape.69
  13.5 0.1 dynamic-slice_reduce_fusion
  13.6 0.1 reshape_reshape.6.gain_ref
  13.6 0.1 reshape_reshape.7.bias_ref
  13.7 0.1 constant_dynamic-slice_fusion
  13.8 0.0 copy-start.3
  13.9 0.2 pad_maximum_fusion._.w_ref
  14.0 0.0 copy-start.2
  14.1 7.9 %all-to-all-done.recv_ref = bf16[32,32,128]{2,1,0:T(8,128)(2,1)S(1)} async-done(((bf16[32,32,128]{2,1,0:T(8,128)(2,1)}), bf16[32,32,128]{2,1,0:T(8,128)(2,1)S(1)}, u32[]{:S(2)}, u32[]{:S(2)}) %all-to-all-start) | async-done | bytes 262176 | tf_op jit(solution)/shard_map/all_to_all | solution.py:31
  22.0 2.2 %middle.1 = (bf16[16,80,128]{2,1,0:T(8,128)(2,1)}, f32[8,512]{1,0:T(8,128)S(1)}, f32[16,512]{1,0:T(8,128)S(1)}, f32[32,128]{1,0:T(8,128)S(1)}) custom-call(s32[1]{0:T(128)} %bitcast.4.place_ref, bf16[32,32,128]{2,1,0:T(8,128)(2,1)S(1)} %all-to-all-done.recv_ref, bf16[512,512]{1,0:T(8,128)(2,1)S(1)} %copy.19.w_ref, f32[1,512]{1,0:T(1,128)S(1)} %reshape_reshape.6.gain_ref, ...), custom_call_target="tpu_custom_call" | custom-call | flops 1000000000 | bytes 1048576 | tf_op jit(solution)/shard_map/middle/pallas_call | solution.py:555
  24.2 3.5 %all-to-all-start.1 = ((bf16[16,80,128]{2,1,0:T(8,128)(2,1)}), bf16[16,80,128]{2,1,0:T(8,128)(2,1)S(1)}, u32[]{:S(2)}, u32[]{:S(2)}) async-start(bf16[16,80,128]{2,1,0:T(8,128)(2,1)} %get-tuple-element.34), calls=%async_computation.1 | async-start | bytes 655360 | tf_op jit(solution)/shard_map/all_to_all | solution.py:608
  27.7 0.1 collective-permute-start
  27.8 1.2 %collective-permute-done.other_ref = f32[8,512]{1,0:T(8,128)S(1)} collective-permute-done((f32[8,512]{1,0:T(8,128)S(1)}, f32[8,512]{1,0:T(8,128)S(1)}, u32[]{:S(2)}, u32[]{:S(2)}) %collective-permute-start) | collective-permute-done | bytes 16416 | tf_op jit(solution)/shard_map/ppermute | solution.py:611
  29.0 0.7 %copy-done.4 = s32[256]{0:T(256)S(1)} copy-done((s32[256]{0:T(256)S(1)}, s32[256]{0:T(256)}, u32[]{:S(2)}) %copy-start.4) | copy-done | bytes 1048
  29.6 0.0 copy-done.5
  29.6 3.0 %embed.1 = (bf16[256,128]{1,0:T(8,128)(2,1)}, f32[8,128]{1,0:T(8,128)S(1)}) custom-call(s32[1]{0:T(128)S(6)} %copy.21.count_ref, s32[1]{0:T(128)} %bitcast.rep_ref, s32[1,256]{1,0:T(1,128)S(1)} %bitcast.28, s32[1,512]{1,0:T(1,128)S(1)} %bitcast.21, s32[1,512]{1,0:T(1,128)S(1)} %bitcast.25, bf16[512,1024]{1,0:T(8,128)(2,1)} %w_hbm.3, ...), custom_call_target="tpu_custom_call" | custom-call | flops 1000000000 | bytes 1048576 | tf_op jit(solution)/shard_map/embed/pallas_call | solution.py:555
  32.6 4.5 %owner.1 = (f32[40,512]{1,0:T(8,128)S(1)}, bf16[160,512]{1,0:T(8,128)(2,1)S(1)}, bf16[160,512]{1,0:T(8,128)(2,1)S(1)}, bf16[160,512]{1,0:T(8,128)(2,1)S(1)}, bf1...) custom-call(s32[1]{0:T(128)} %bitcast.4.place_ref, ...), custom_call_target="tpu_custom_call" | custom-call | flops 4000000000 | bytes 1048576 | tf_op jit(solution)/shard_map/owner/pallas_call | solution.py:555
  37.1 2.2 %all-to-all-done.1.recv_ref = bf16[16,80,128]{2,1,0:T(8,128)(2,1)S(1)} async-done(((bf16[16,80,128]{2,1,0:T(8,128)(2,1)}), bf16[16,80,128]{2,1,0:T(8,128)(2,1)S(1)}, u32[]{:S(2)}, u32[]{:S(2)}) %all-to-all-start.1) | async-done | bytes 327712 | tf_op jit(solution)/shard_map/all_to_all | solution.py:608
  39.3 0.0 collective-permute-start.1
  39.3 1.2 %last.1 = (f32[32,512]{1,0:T(8,128)}, f32[32,128]{1,0:T(8,128)}) custom-call(s32[1]{0:T(128)} %bitcast.4.place_ref, bf16[16,80,128]{2,1,0:T(8,128)(2,1)S(1)} %all-to-all-done.1.recv_ref, f32[40,512]{1,0:T(8,128)S(1)} %get-tuple-element.38.fixed_ref, f32[8,512]{1,0:T(8,128)S(1)} %get-tuple-element.32.mine_ref.stat_ref, f32[1,512]{1,0:T(1,128)S(1)} %reshape_reshape.6.gain_ref, ...), custom_call_target="tpu_custom_call" | custom-call | flops 1000000000 | bytes 1048576 | tf_op jit(solution)/shard_map/last/pallas_call | solution.py:555
  40.6 0.0 collective-permute-done.1.other_ref
  40.6 0.7 %join.1 = (f32[1,1024]{1,0:T(1,128)}, f32[1,1024]{1,0:T(1,128)}) custom-call(s32[1]{0:T(128)} %bitcast.rep_ref, bf16[16,8,128]{2,1,0:T(8,128)(2,1)S(1)} %slice.4.mine_ref, bf16[16,8,128]{2,1,0:T(8,128)(2,1)S(1)} %collective-permute-done.1.other_ref), custom_call_target="tpu_custom_call" | custom-call | flops 1000000 | bytes 1048576 | tf_op jit(solution)/shard_map/join/pallas_call | solution.py:555
  (10 shorter events, 0.1 us)
Async XLA Ops:
  1.3 10.1 %copy-start.6 = (bf16[512,1024]{1,0:T(8,128)(2,1)S(1)}, bf16[512,1024]{1,0:T(8,128)(2,1)}, u32[]{:S(2)}) copy-start(bf16[512,1024]{1,0:T(8,128)(2,1)} %w_hbm.3) | copy-start | bytes 3145732
  4.1 17.9 %all-to-all-start = ((bf16[32,32,128]{2,1,0:T(8,128)(2,1)}), bf16[32,32,128]{2,1,0:T(8,128)(2,1)S(1)}, u32[]{:S(2)}, u32[]{:S(2)}) async-start(bf16[32,32,128]{2,1,0:T(8,128)(2,1)} %first.1), calls=%async_computation | async-start | bytes 524288 | tf_op jit(solution)/shard_map/all_to_all | solution.py:31
  12.0 0.7 %copy-start = (f32[1024]{0:T(1024)S(1)}, f32[1024]{0:T(1024)}, u32[]{:S(2)}) copy-start(f32[1024]{0:T(1024)} %param.16) | copy-start | bytes 12292
  12.0 1.7 %copy-start.7 = (bf16[1024,128]{1,0:T(8,128)(2,1)S(1)}, bf16[1024,128]{1,0:T(8,128)(2,1)}, u32[]{:S(2)}) copy-start(bf16[1024,128]{1,0:T(8,128)(2,1)} %w_out_hbm.1) | copy-start | bytes 786436
  12.7 0.7 %copy-start.1 = (f32[1024]{0:T(1024)S(1)}, f32[1024]{0:T(1024)}, u32[]{:S(2)}) copy-start(f32[1024]{0:T(1024)} %param.15) | copy-start | bytes 12292
  13.8 8.1 %copy-start.3 = (s32[512]{0:T(512)S(1)}, s32[512]{0:T(512)}, u32[]{:S(2)}) copy-start(s32[512]{0:T(512)} %param.13) | copy-start | bytes 6148
  14.0 7.9 %copy-start.2 = (s32[512]{0:T(512)S(1)}, s32[512]{0:T(512)}, u32[]{:S(2)}) copy-start(s32[512]{0:T(512)} %param.12) | copy-start | bytes 6148
  24.2 15.2 %all-to-all-start.1 = ((bf16[16,80,128]{2,1,0:T(8,128)(2,1)}), bf16[16,80,128]{2,1,0:T(8,128)(2,1)S(1)}, u32[]{:S(2)}, u32[]{:S(2)}) async-start(bf16[16,80,128]{2,1,0:T(8,128)(2,1)} %get-tuple-element.34), calls=%async_computation.1 | async-start | bytes 655360 | tf_op jit(solution)/shard_map/all_to_all | solution.py:608
  27.7 1.2 %collective-permute-start = (f32[8,512]{1,0:T(8,128)S(1)}, f32[8,512]{1,0:T(8,128)S(1)}, u32[]{:S(2)}, u32[]{:S(2)}) collective-permute-start(f32[8,512]{1,0:T(8,128)S(1)} %get-tuple-element.32.mine_ref.stat_ref), channel_id=1, source_target_pairs={{0,1},{1,0},{2,3},{3,2},{4,5},{5,4},{6,7},{7,6},{8,9},{9,8},{10,11... | collective-permute-start | bytes 49160 | tf_op jit(solution)/shard_map/ppermute | solution.py:611
  29.0 0.7 %copy-start.4 = (s32[256]{0:T(256)S(1)}, s32[256]{0:T(256)}, u32[]{:S(2)}) copy-start(s32[256]{0:T(256)} %param.10) | copy-start | bytes 3076
  29.0 0.7 %copy-start.5 = (f32[128]{0:T(128)S(1)}, f32[128]{0:T(128)}, u32[]{:S(2)}) copy-start(f32[128]{0:T(128)} %param.18) | copy-start | bytes 1540
  39.3 1.2 %collective-permute-start.1 = (bf16[16,8,128]{2,1,0:T(8,128)(2,1)S(1)}, bf16[16,8,128]{2,1,0:T(8,128)(2,1)S(1)}, u32[]{:S(2)}, u32[]{:S(2)}) collective-permute-start(bf16[16,8,128]{2,1,0:T(8,128)(2,1)S(1)} %slice.4.mine_ref), channel_id=1, source_target_pairs={{0,1},{1,0},{2,3},{3,2},{4,5},{5,4},{6,7},{7,6},{8,9},{9,8},{10,11... | collective-permute-start | bytes 98312 | tf_op jit(solution)/shard_map/ppermute | solution.py:611

commit v5 on v4

--- a/solution.py
+++ b/solution.py
@@ -212,8 +212,9 @@
 
 
 def first_kernel(
-    dims, count_ref, ids_hbm, scale_hbm, shift_hbm, w_hbm, cot_hbm, send_ref,
-    ids_ref, scale_ref, shift_ref, w_ref, cot_ref, sems,
+    dims, count_ref, _, __, ids_hbm, scale_hbm, shift_hbm, w_hbm, cot_hbm, gain_hbm, bias_hbm,
+    w_out_hbm, send_ref, scale_ref, shift_ref, w_ref, gain_ref, bias_ref, w_out_ref,
+    ids_ref, cot_ref, sems,
 ):
     chips, reps, take, block = dims.chips, dims.reps, dims.take, dims.block
     slots = dims.slots
@@ -226,6 +227,9 @@
                 (shift_hbm, shift_ref),
                 (w_hbm, w_ref),
                 (cot_hbm, cot_ref),
+                (gain_hbm, gain_ref),
+                (bias_hbm, bias_ref),
+                (w_out_hbm, w_out_ref),
             ]
         )
     ]
@@ -247,7 +251,7 @@
         for i in range(2)
         for t in range(slots // LANES)
     ]
-    for copy in copies[3:]:
+    for copy in copies[3:5]:
         copy.wait()
     pre = jnp.dot(codes, w_ref[...], preferred_element_type=jnp.float32)
     moved = jnp.dot(order, cot_ref[...], preferred_element_type=jnp.float32).astype(jnp.bfloat16)
@@ -262,6 +266,8 @@
         for k in range(chips):
             send_ref[k * reps + rep, :take, :] = moved[k * take : (k + 1) * take, :]
             send_ref[k * reps + rep, take:, :] = lower
+    for copy in copies[5:]:
+        copy.wait()
 
 
 def id_rows(dims, recv):
@@ -303,13 +309,19 @@
     return target, live.sum(0, keepdims=True)
 
 
+def half_of(dims, x, rep):
+    tiles = [x[:, t : t + LANES] for t in range(0, dims.hidden, LANES)]
+    moved = [jnp.where(rep == 0, t, pltpu.roll(t, LANES - dims.block, 1)) for t in tiles]
+    return row_of(pick_blocks(row_of(moved), [k * dims.reps for k in range(dims.chips)], dims.block))
+
+
 def middle_kernel(
-    dims, place_ref, recv_ref, w_ref, gain_ref, bias_ref, w_out_ref, scale_ref, shift_ref, _,
+    dims, place_ref, side_ref, recv_ref, w_ref, gain_ref, bias_ref, w_out_ref, scale_ref, shift_ref,
     send_ref, stat_ref, ids_ref, counts_ref,
 ):
     take, block, rows = dims.take, dims.block, dims.rows
     half, groups = dims.half, dims.groups
-    chip = place_ref[0]
+    chip, rep = place_ref[0], side_ref[0]
     recv = recv_ref[:, take:, :].astype(jnp.float32)
     recv_all = jnp.concatenate([jnp.zeros((dims.devices, take, LANES), jnp.float32), recv], axis=1)
     counts, ids = id_rows(dims, recv_all)
@@ -322,7 +334,7 @@
     own_ids = jnp.where(own, ids, 0.0).sum(0, keepdims=True)
     id_column = jnp.where(hit, own_ids, 0.0).sum(1, keepdims=True).astype(jnp.int32)
     codes = codes_of(id_column, scale_ref[...], shift_ref[...])
-    pre = jnp.dot(codes, w_ref[...], preferred_element_type=jnp.float32)
+    pre = half_of(dims, jnp.dot(codes, w_ref[...], preferred_element_type=jnp.float32), rep)
     cot = jnp.dot(
         one_hot(hit), recv_ref[:, :take, :].reshape(dims.devices * take, LANES),
         preferred_element_type=jnp.float32,
@@ -337,13 +349,22 @@
         variances.append((recv[:, r + 2, :] + counts * (off * off)).sum(0, keepdims=True) / total)
     mean = row_of(means)
     inv_std = lax.rsqrt(row_of(variances) + epsilon)
+    gain = half_of(dims, gain_ref[...], rep)
+    bias = half_of(dims, bias_ref[...], rep)
     stat_ref[...] = jnp.concatenate(
-        [mean, inv_std, jnp.zeros((6, half), jnp.float32) + total], axis=0
+        [mean, inv_std, gain, jnp.zeros((5, half), jnp.float32) + total], axis=0
+    )
+    w_out = jnp.concatenate(
+        [
+            w_out_ref[pl.ds(pl.multiple_of((k * dims.reps + rep) * block, block), block), :]
+            for k in range(dims.chips)
+        ],
+        axis=0,
     )
     normed = (pre - mean) * inv_std
-    act, slope = mish_of(normed * gain_ref[...] + bias_ref[...])
+    act, slope = mish_of(normed * gain + bias)
     delta = (cot * lax.rsqrt(total)).astype(jnp.bfloat16)
-    dval = dot_t(delta, w_out_ref[...]) * slope
+    dval = dot_t(delta, w_out) * slope
     grad_out = dot_rows(act.astype(jnp.bfloat16), delta).astype(jnp.bfloat16)
     pair = [(dval * normed).sum(0, keepdims=True), dval.sum(0, keepdims=True)]
     pair = jnp.concatenate(
@@ -484,13 +505,13 @@
 
 
 def last_kernel(
-    dims, place_ref, recv_ref, fixed_ref, stat_ref, gain_ref, *refs
+    dims, place_ref, recv_ref, fixed_ref, stat_ref, *refs
 ):
     part, block, groups = dims.rows // dims.groups, dims.block, dims.groups
     code_refs, (code_out_ref, out_out_ref) = refs[:-2], refs[-2:]
     chip = place_ref[0]
-    total = stat_ref[2:3, :1]
-    scale = own_column(dims, gain_ref[...] * stat_ref[1:2, :], chip)
+    total = stat_ref[3:4, :1]
+    scale = own_column(dims, stat_ref[2:3, :] * stat_ref[1:2, :], chip)
     gain, bias = pair_sums(dims, recv_ref[:, part + block :, :])
     tilt = own_column(dims, gain, chip) / total
     shift = own_column(dims, bias, chip) / total
@@ -571,29 +592,23 @@
     chips, reps, block, half = dims.chips, dims.reps, dims.block, dims.half
     dp, rep = lax.axis_index("dp"), lax.axis_index("rep")
     f32, bf16 = jnp.float32, jnp.bfloat16
+    place, side = dp.reshape(1).astype(jnp.int32), rep.reshape(1).astype(jnp.int32)
     ids = ids.reshape(1, -1)
     scale_row, shift_row = hash_scale.reshape(1, -1), hash_shift.reshape(1, -1)
-    loaded = (ids, scale_row, shift_row, w_code, cotangent)
-    (send,) = kernel_call(
+    gain_row, bias_row = norm_gain.reshape(1, -1), norm_bias.reshape(1, -1)
+    kept = (scale_row, shift_row, w_code, gain_row, bias_row, w_out)
+    loaded = (ids, scale_row, shift_row, w_code, cotangent, gain_row, bias_row, w_out)
+    send, scale_row, shift_row, w_near, gain_row, bias_row, w_out_near = kernel_call(
         dims, first_kernel,
-        [((dims.devices, dims.send_rows, LANES), bf16)],
-        (counts,) + loaded, 1, "first", 10**9, hbm=(1, 2, 3, 4, 5),
-        scratch=[pltpu.VMEM(x.shape, x.dtype) for x in loaded]
-        + [pltpu.SemaphoreType.DMA((len(loaded),))], vmem=60,
+        [((dims.devices, dims.send_rows, LANES), bf16)]
+        + [(x.shape, x.dtype) for x in kept],
+        (counts, place, side) + tuple(pltpu.with_memory_space_constraint(x, pltpu.HBM) for x in loaded),
+        3, "first", 10**9, hbm=range(3, 3 + len(loaded)),
+        scratch=[pltpu.VMEM(x.shape, x.dtype) for x in (ids, cotangent)]
+        + [pltpu.SemaphoreType.DMA((len(loaded),))],
     )
     recv = exchange(send)
 
-    def of_rep(x, axis):
-        shape = x.shape[:axis] + (chips, reps, block) + x.shape[axis + 1 :]
-        x = lax.dynamic_index_in_dim(x.reshape(shape), rep, axis + 1, keepdims=False)
-        return x.reshape(x.shape[:axis] + (half,) + x.shape[axis + 2 :])
-
-    place, side = dp.reshape(1).astype(jnp.int32), rep.reshape(1).astype(jnp.int32)
-    w_half, w_out_half = of_rep(w_code, 1), of_rep(w_out, 0)
-    gain_half = of_rep(norm_gain, 0).reshape(1, -1)
-    bias_half = of_rep(norm_bias, 0).reshape(1, -1)
-    w_own = lax.dynamic_slice_in_dim(w_code, (dp * reps + rep) * block, block, 1)
-    w_own = jnp.concatenate([w_own] * dims.groups, axis=1)
     grads, stat, all_ids, all_counts = kernel_call(
         dims, middle_kernel,
         [
@@ -602,7 +617,10 @@
             ((chips, dims.devices * dims.take), f32),
             ((dims.devices, LANES), f32),
         ],
-        (place, recv, w_half, gain_half, bias_half, w_out_half, scale_row, shift_row, w_own), 1,
+        (
+            place, side, recv, w_near, gain_row, bias_row, w_out_near, scale_row, shift_row,
+        ),
+        2,
         "middle", 10**9,
     )
     share = lax.all_to_all(grads, "dp", split_axis=0, concat_axis=0, tiled=True)
@@ -610,13 +628,16 @@
     def partner(x):
         return lax.ppermute(x, "rep", [(i, (i + 1) % reps) for i in range(reps)])
 
+    w_own, stat, at, of = lax.optimization_barrier((w_code, stat, place, side))
+    w_own = lax.dynamic_slice_in_dim(w_own, (at[0] * reps + of[0]) * block, block, 1)
+    w_own = jnp.concatenate([w_own] * dims.groups, axis=1)
     packed = chips * dims.rows // dims.groups
     embedded, token = kernel_call(
         dims, embed_kernel, [((dims.slots, dims.width), bf16), ((8, LANES), f32)],
         (
             counts, side, ids, scale_row, shift_row,
             pltpu.with_memory_space_constraint(w_code, pltpu.HBM), stat, partner(stat),
-            norm_gain.reshape(1, -1), norm_bias.reshape(1, -1),
+            gain_row, bias_row,
             pltpu.with_memory_space_constraint(w_out, pltpu.HBM), out_bias.reshape(1, -1),
         ),
         2, "embed", 10**9, hbm=(5, 10),
@@ -635,7 +656,7 @@
     other = partner(pair)
     code_share, out_share = kernel_call(
         dims, last_kernel, [((block, dims.codes), f32), ((block, dims.width), f32)],
-        (place, share, fixed, stat, gain_half, *code), 1, "last", 10**9,
+        (place, share, fixed, stat, *code), 1, "last", 10**9,
     )
     gain, bias = kernel_call(
         dims, join_kernel, [((1, dims.hidden), f32)] * 2, (side, pair, other), 1, "join", 10**6

time: 41.7 us -> 41.1 us (0.986)
  blocking collectives: 0 us -> 17.7 us
  waiting for transfers between devices: 11.3 us -> 2.48 us
  starting transfers between devices: 10.9 us -> 3.55 us
  local copies, waits for them, and re-layouts: 3.07 us -> 1.67 us
  Pallas kernels: 14.3 us -> 13.8 us
    all_to_all x0 -> x1, blocking collectives: none -> 17.7 us  [exchange(): return lax.all_to_all(blocks, AXES, split_axis=0, concat_axis=0, tiled=True)]
    all_to_all x1 -> x0, waiting for transfers between devices: 7.92 us -> none  [exchange(): return lax.all_to_all(blocks, AXES, split_axis=0, concat_axis=0, tiled=True)]
    all_to_all x1 -> x0, starting transfers between devices: 7.33 us -> none  [exchange(): return lax.all_to_all(blocks, AXES, split_axis=0, concat_axis=0, tiled=True)]
    unnamed x17 -> x4, local copies, waits for them, and re-layouts: 2.31 us -> 0.66 us
    ppermute x2, waiting for transfers between devices: 1.17 us -> 0.01 us  [partner(): return lax.ppermute(x, 'rep', [(i, (i + 1) % reps) for i in range(reps)])]
    dynamic_slice x4 -> x1, local copies, waits for them, and re-layouts: 0.23 us -> 1.01 us  [fast_device(): lax.dynamic_slice_in_dim(w_own, (at[0] * reps + of[0]) * block, block, 1)]
    pallas_call x6, Pallas kernels: 14.3 us -> 13.8 us  [kernel_call(): pl.pallas_call(functools.partial(body, dims), out_shape=[jax.ShapeDtypeSt...]
  transfers between devices with their start and end apart: 4 -> 3, of which waited for: 3 -> 1; matrix products, arithmetic and copies ran while one was open for 4% -> 3% of each run, Pallas kernels for 21% -> 21%
where the time goes in v5:
time: 41.1 us; the launch traced here: 40.8 us
  blocking collectives  17.7 us (43%)
  Pallas kernels  13.8 us (34%)
  starting transfers between devices  3.55 us (9%)
  waiting for transfers between devices  2.48 us (6%)
  local copies, waits for them, and re-layouts  1.67 us (4%)
  between operations  1.37 us (3%)
    all_to_all x1, blocking collectives, exchange(): return lax.all_to_all(blocks, AXES, split_axis=0, concat_axis=0, tiled=True)  17.7 us
    pallas_call x6, Pallas kernels, kernel_call(): pl.pallas_call(functools.partial(body, dims), out_shape=[jax.ShapeDtypeSt...  13.8 us
    all_to_all x1, starting transfers between devices, fast_device(): share = lax.all_to_all(grads, 'dp', split_axis=0, concat_axis=0, tiled=True)  3.54 us
    all_to_all x1, waiting for transfers between devices, fast_device(): share = lax.all_to_all(grads, 'dp', split_axis=0, concat_axis=0, tiled=True)  2.47 us
    dynamic_slice x1, local copies, waits for them, and re-layouts, fast_device(): lax.dynamic_slice_in_dim(w_own, (at[0] * reps + of[0]) * block, block, 1)  1.01 us
  transfers between devices with their start and end apart: 3, of which 1 were waited for; matrix products, arithmetic and copies ran while one was open for 3% of the time, Pallas kernels for 21%

profile of v5, /device:TPU:0, one launch (start us, length us, event | category | flops | bytes accessed | tf_op | source)
XLA Modules:
  0.0 40.8 jit_solution(7054989759982625979)
XLA Ops:
  1.3 2.0 %first.1 = (bf16[32,32,128]{2,1,0:T(8,128)(2,1)S(1)}, s32[1,512]{1,0:T(1,128)S(1)}, s32[1,512]{1,0:T(1,128)S(1)}, bf16[512,1024]{1,0:T(8,128)(2,1)S(1)}, f32[1,1...) custom-call(s32[1]{0:T(128)S(6)} %copy.15.count_ref, s32[1]{0:T(128)} %bitcast.2._.place_ref, ...), custom_call_target="tpu_custom_call" | custom-call | flops 1000000000 | bytes 1048576 | tf_op jit(solution)/shard_map/first/pallas_call | solution.py:576
  3.3 17.7 %all_to_all.10.recv_ref = bf16[32,32,128]{2,1,0:T(8,128)(2,1)S(1)} all-to-all(bf16[32,32,128]{2,1,0:T(8,128)(2,1)S(1)} %get-tuple-element.45), channel_id=1, replica_groups=mesh['dp'=16,'rep'=2] {'dp','rep'}, dimensions={0} | all-to-all | bytes 524288 | tf_op jit(solution)/shard_map/all_to_all | solution.py:31
  21.0 2.5 %middle.1 = (bf16[16,80,128]{2,1,0:T(8,128)(2,1)}, f32[8,512]{1,0:T(8,128)S(1)}, f32[16,512]{1,0:T(8,128)S(1)}, f32[32,128]{1,0:T(8,128)S(1)}) custom-call(s32[1]{0:T(128)} %bitcast.2._.place_ref, s32[1]{0:T(128)} %bitcast.__.side_ref.rep_ref, bf16[32,32,128]{2,1,0:T(8,128)(2,1)S(1)} %all_to_all.10.recv_ref, bf16[512,1024]{1,0:T(8,128)(2,1)S(1)} %get-tuple-element.46.w_ref, ...), custom_call_target="tpu_custom_call" | custom-call | flops 1000000000 | bytes 1048576 | tf_op jit(solution)/shard_map/middle/pallas_call | solution.py:576
  23.5 0.0 collective-permute-start
  23.5 3.5 %all-to-all-start.1 = ((bf16[16,80,128]{2,1,0:T(8,128)(2,1)}), bf16[16,80,128]{2,1,0:T(8,128)(2,1)S(1)}, u32[]{:S(2)}, u32[]{:S(2)}) async-start(bf16[16,80,128]{2,1,0:T(8,128)(2,1)} %get-tuple-element.53), calls=%async_computation.1 | async-start | bytes 655360 | tf_op jit(solution)/shard_map/all_to_all | solution.py:626
  27.0 1.0 %constant_dynamic-slice_fusion = bf16[512,32]{1,0:T(8,128)(2,1)S(1)} fusion(bf16[512,1024]{1,0:T(8,128)(2,1)} %w_hbm.3, s32[]{:T(128)S(6)} %select_n.3), kind=kLoop, calls=%fused_computation.1 | loop fusion | bytes 65540 | tf_op jit(solution)/shard_map/dynamic_slice | solution.py:632
  28.1 0.2 pad_maximum_fusion.w_ref
  28.2 0.0 copy-start
  28.3 0.0 copy-start.1
  28.3 0.0 collective-permute-done.other_ref
  28.3 0.6 %copy-done = s32[256]{0:T(256)S(1)} copy-done((s32[256]{0:T(256)S(1)}, s32[256]{0:T(256)}, u32[]{:S(2)}) %copy-start) | copy-done | bytes 1048
  28.9 0.0 copy-done.1
  28.9 3.0 %embed.1 = (bf16[256,128]{1,0:T(8,128)(2,1)}, f32[8,128]{1,0:T(8,128)S(1)}) custom-call(s32[1]{0:T(128)S(6)} %copy.15.count_ref, s32[1]{0:T(128)} %bitcast.__.side_ref.rep_ref, s32[1,256]{1,0:T(1,128)S(1)} %bitcast.12, s32[1,512]{1,0:T(1,128)S(1)} %get-tuple-element.43.scale_ref, s32[1,512]{1,0:T(1,128)S(1)} %get-tuple-element.44.shift_ref, ...), custom_call_target="tpu_custom_call" | custom-call | flops 1000000000 | bytes 1048576 | tf_op jit(solution)/shard_map/embed/pallas_call | solution.py:576
  31.9 4.4 %owner.1 = (f32[40,512]{1,0:T(8,128)S(1)}, bf16[160,512]{1,0:T(8,128)(2,1)S(1)}, bf16[160,512]{1,0:T(8,128)(2,1)S(1)}, bf16[160,512]{1,0:T(8,128)(2,1)S(1)}, bf1...) custom-call(s32[1]{0:T(128)} %bitcast.2._.place_ref, ...), custom_call_target="tpu_custom_call" | custom-call | flops 4000000000 | bytes 1048576 | tf_op jit(solution)/shard_map/owner/pallas_call | solution.py:576
  36.4 2.5 %all-to-all-done.1.recv_ref = bf16[16,80,128]{2,1,0:T(8,128)(2,1)S(1)} async-done(((bf16[16,80,128]{2,1,0:T(8,128)(2,1)}), bf16[16,80,128]{2,1,0:T(8,128)(2,1)S(1)}, u32[]{:S(2)}, u32[]{:S(2)}) %all-to-all-start.1) | async-done | bytes 327712 | tf_op jit(solution)/shard_map/all_to_all | solution.py:626
  38.8 0.0 collective-permute-start.1
  38.8 1.2 %last.1 = (f32[32,512]{1,0:T(8,128)}, f32[32,128]{1,0:T(8,128)}) custom-call(s32[1]{0:T(128)} %bitcast.2._.place_ref, bf16[16,80,128]{2,1,0:T(8,128)(2,1)S(1)} %all-to-all-done.1.recv_ref, f32[40,512]{1,0:T(8,128)S(1)} %get-tuple-element.60.fixed_ref, f32[8,512]{1,0:T(8,128)S(1)} %get-tuple-element.51.mine_ref.stat_ref, ...), custom_call_target="tpu_custom_call" | custom-call | flops 1000000000 | bytes 1048576 | tf_op jit(solution)/shard_map/last/pallas_call | solution.py:576
  40.1 0.0 collective-permute-done.1.other_ref
  40.1 0.7 %join.1 = (f32[1,1024]{1,0:T(1,128)}, f32[1,1024]{1,0:T(1,128)}) custom-call(s32[1]{0:T(128)} %bitcast.__.side_ref.rep_ref, bf16[16,8,128]{2,1,0:T(8,128)(2,1)S(1)} %slice.4.mine_ref, bf16[16,8,128]{2,1,0:T(8,128)(2,1)S(1)} %collective-permute-done.1.other_ref), custom_call_target="tpu_custom_call" | custom-call | flops 1000000 | bytes 1048576 | tf_op jit(solution)/shard_map/join/pallas_call | solution.py:576
  (1 shorter events, 0.0 us)
Async XLA Ops:
  23.5 4.8 %collective-permute-start = (f32[8,512]{1,0:T(8,128)S(1)}, f32[8,512]{1,0:T(8,128)S(1)}, u32[]{:S(2)}, u32[]{:S(2)}) collective-permute-start(f32[8,512]{1,0:T(8,128)S(1)} %get-tuple-element.51.mine_ref.stat_ref), channel_id=1, source_target_pairs={{0,1},{1,0},{2,3},{3,2},{4,5},{5,4},{6,7},{7,6},{8,9},{9,8},{10,11... | collective-permute-start | bytes 49160 | tf_op jit(solution)/shard_map/ppermute | solution.py:629
  23.5 15.3 %all-to-all-start.1 = ((bf16[16,80,128]{2,1,0:T(8,128)(2,1)}), bf16[16,80,128]{2,1,0:T(8,128)(2,1)S(1)}, u32[]{:S(2)}, u32[]{:S(2)}) async-start(bf16[16,80,128]{2,1,0:T(8,128)(2,1)} %get-tuple-element.53), calls=%async_computation.1 | async-start | bytes 655360 | tf_op jit(solution)/shard_map/all_to_all | solution.py:626
  28.2 0.7 %copy-start = (s32[256]{0:T(256)S(1)}, s32[256]{0:T(256)}, u32[]{:S(2)}) copy-start(s32[256]{0:T(256)} %param.10) | copy-start | bytes 3076
  28.3 0.7 %copy-start.1 = (f32[128]{0:T(128)S(1)}, f32[128]{0:T(128)}, u32[]{:S(2)}) copy-start(f32[128]{0:T(128)} %param.18) | copy-start | bytes 1540
  38.8 1.2 %collective-permute-start.1 = (bf16[16,8,128]{2,1,0:T(8,128)(2,1)S(1)}, bf16[16,8,128]{2,1,0:T(8,128)(2,1)S(1)}, u32[]{:S(2)}, u32[]{:S(2)}) collective-permute-start(bf16[16,8,128]{2,1,0:T(8,128)(2,1)S(1)} %slice.4.mine_ref), channel_id=1, source_target_pairs={{0,1},{1,0},{2,3},{3,2},{4,5},{5,4},{6,7},{7,6},{8,9},{9,8},{10,11... | collective-permute-start | bytes 98312 | tf_op jit(solution)/shard_map/ppermute | solution.py:629

commit v6 on v5

--- a/solution.py
+++ b/solution.py
@@ -310,9 +310,19 @@
 
 
 def half_of(dims, x, rep):
-    tiles = [x[:, t : t + LANES] for t in range(0, dims.hidden, LANES)]
-    moved = [jnp.where(rep == 0, t, pltpu.roll(t, LANES - dims.block, 1)) for t in tiles]
-    return row_of(pick_blocks(row_of(moved), [k * dims.reps for k in range(dims.chips)], dims.block))
+    groups, block = dims.groups, dims.block
+    lane = lax.broadcasted_iota(jnp.int32, (x.shape[0], LANES), 1) // block
+    tiles = []
+    for first in range(0, dims.chips, groups):
+        tile = None
+        for place in range(groups):
+            b = (first + place) * dims.reps
+            start = b // groups * LANES
+            shift = lax.rem((place - b % groups - rep) * block + 2 * LANES, LANES)
+            piece = pltpu.roll(x[:, start : start + LANES], shift, 1)
+            tile = piece if tile is None else jnp.where(lane == place, piece, tile)
+        tiles.append(tile)
+    return row_of(tiles)
 
 
 def middle_kernel(

time: 41.1 us -> 41.1 us (level)
  no operation moved by 1% of the time
where the time goes in v6:
time: 41.1 us; the launch traced here: 40.7 us
  blocking collectives  17.7 us (43%)
  Pallas kernels  13.8 us (34%)
  starting transfers between devices  3.55 us (9%)
  waiting for transfers between devices  2.49 us (6%)
  local copies, waits for them, and re-layouts  1.67 us (4%)
  between operations  1.37 us (3%)
    all_to_all x1, blocking collectives, exchange(): return lax.all_to_all(blocks, AXES, split_axis=0, concat_axis=0, tiled=True)  17.7 us
    pallas_call x6, Pallas kernels, kernel_call(): pl.pallas_call(functools.partial(body, dims), out_shape=[jax.ShapeDtypeSt...  13.8 us
    all_to_all x1, starting transfers between devices, fast_device(): share = lax.all_to_all(grads, 'dp', split_axis=0, concat_axis=0, tiled=True)  3.54 us
    all_to_all x1, waiting for transfers between devices, fast_device(): share = lax.all_to_all(grads, 'dp', split_axis=0, concat_axis=0, tiled=True)  2.48 us
    dynamic_slice x1, local copies, waits for them, and re-layouts, fast_device(): lax.dynamic_slice_in_dim(w_own, (at[0] * reps + of[0]) * block, block, 1)  1.01 us
  transfers between devices with their start and end apart: 3, of which 1 were waited for; matrix products, arithmetic and copies ran while one was open for 3% of the time, Pallas kernels for 21%

profile of v6, /device:TPU:0, one launch (start us, length us, event | category | flops | bytes accessed | tf_op | source)
XLA Modules:
  0.0 40.7 jit_solution(5453759951515900026)
XLA Ops:
  1.3 2.0 %first.1 = (bf16[32,32,128]{2,1,0:T(8,128)(2,1)S(1)}, s32[1,512]{1,0:T(1,128)S(1)}, s32[1,512]{1,0:T(1,128)S(1)}, bf16[512,1024]{1,0:T(8,128)(2,1)S(1)}, f32[1,1...) custom-call(s32[1]{0:T(128)S(6)} %copy.15.count_ref, s32[1]{0:T(128)} %bitcast.2._.place_ref, ...), custom_call_target="tpu_custom_call" | custom-call | flops 1000000000 | bytes 1048576 | tf_op jit(solution)/shard_map/first/pallas_call | solution.py:586
  3.3 17.7 %all_to_all.10.recv_ref = bf16[32,32,128]{2,1,0:T(8,128)(2,1)S(1)} all-to-all(bf16[32,32,128]{2,1,0:T(8,128)(2,1)S(1)} %get-tuple-element.45), channel_id=1, replica_groups=mesh['dp'=16,'rep'=2] {'dp','rep'}, dimensions={0} | all-to-all | bytes 524288 | tf_op jit(solution)/shard_map/all_to_all | solution.py:31
  21.0 2.4 %middle.1 = (bf16[16,80,128]{2,1,0:T(8,128)(2,1)}, f32[8,512]{1,0:T(8,128)S(1)}, f32[16,512]{1,0:T(8,128)S(1)}, f32[32,128]{1,0:T(8,128)S(1)}) custom-call(s32[1]{0:T(128)} %bitcast.2._.place_ref, s32[1]{0:T(128)} %bitcast.__.side_ref.rep_ref, bf16[32,32,128]{2,1,0:T(8,128)(2,1)S(1)} %all_to_all.10.recv_ref, bf16[512,1024]{1,0:T(8,128)(2,1)S(1)} %get-tuple-element.46.w_ref, ...), custom_call_target="tpu_custom_call" | custom-call | flops 1000000000 | bytes 1048576 | tf_op jit(solution)/shard_map/middle/pallas_call | solution.py:586
  23.4 0.0 collective-permute-start
  23.4 3.5 %all-to-all-start.1 = ((bf16[16,80,128]{2,1,0:T(8,128)(2,1)}), bf16[16,80,128]{2,1,0:T(8,128)(2,1)S(1)}, u32[]{:S(2)}, u32[]{:S(2)}) async-start(bf16[16,80,128]{2,1,0:T(8,128)(2,1)} %get-tuple-element.53), calls=%async_computation.1 | async-start | bytes 655360 | tf_op jit(solution)/shard_map/all_to_all | solution.py:636
  27.0 1.0 %constant_dynamic-slice_fusion = bf16[512,32]{1,0:T(8,128)(2,1)S(1)} fusion(bf16[512,1024]{1,0:T(8,128)(2,1)} %w_hbm.3, s32[]{:T(128)S(6)} %select_n.3), kind=kLoop, calls=%fused_computation.1 | loop fusion | bytes 65540 | tf_op jit(solution)/shard_map/dynamic_slice | solution.py:642
  28.0 0.2 pad_maximum_fusion.w_ref
  28.2 0.0 copy-start
  28.2 0.0 copy-start.1
  28.2 0.0 collective-permute-done.other_ref
  28.2 0.6 %copy-done = s32[256]{0:T(256)S(1)} copy-done((s32[256]{0:T(256)S(1)}, s32[256]{0:T(256)}, u32[]{:S(2)}) %copy-start) | copy-done | bytes 1048
  28.9 0.0 copy-done.1
  28.9 3.0 %embed.1 = (bf16[256,128]{1,0:T(8,128)(2,1)}, f32[8,128]{1,0:T(8,128)S(1)}) custom-call(s32[1]{0:T(128)S(6)} %copy.15.count_ref, s32[1]{0:T(128)} %bitcast.__.side_ref.rep_ref, s32[1,256]{1,0:T(1,128)S(1)} %bitcast.12, s32[1,512]{1,0:T(1,128)S(1)} %get-tuple-element.43.scale_ref, s32[1,512]{1,0:T(1,128)S(1)} %get-tuple-element.44.shift_ref, ...), custom_call_target="tpu_custom_call" | custom-call | flops 1000000000 | bytes 1048576 | tf_op jit(solution)/shard_map/embed/pallas_call | solution.py:586
  31.8 4.4 %owner.1 = (f32[40,512]{1,0:T(8,128)S(1)}, bf16[160,512]{1,0:T(8,128)(2,1)S(1)}, bf16[160,512]{1,0:T(8,128)(2,1)S(1)}, bf16[160,512]{1,0:T(8,128)(2,1)S(1)}, bf1...) custom-call(s32[1]{0:T(128)} %bitcast.2._.place_ref, ...), custom_call_target="tpu_custom_call" | custom-call | flops 4000000000 | bytes 1048576 | tf_op jit(solution)/shard_map/owner/pallas_call | solution.py:586
  36.3 2.5 %all-to-all-done.1.recv_ref = bf16[16,80,128]{2,1,0:T(8,128)(2,1)S(1)} async-done(((bf16[16,80,128]{2,1,0:T(8,128)(2,1)}), bf16[16,80,128]{2,1,0:T(8,128)(2,1)S(1)}, u32[]{:S(2)}, u32[]{:S(2)}) %all-to-all-start.1) | async-done | bytes 327712 | tf_op jit(solution)/shard_map/all_to_all | solution.py:636
  38.8 0.0 collective-permute-start.1
  38.8 1.2 %last.1 = (f32[32,512]{1,0:T(8,128)}, f32[32,128]{1,0:T(8,128)}) custom-call(s32[1]{0:T(128)} %bitcast.2._.place_ref, bf16[16,80,128]{2,1,0:T(8,128)(2,1)S(1)} %all-to-all-done.1.recv_ref, f32[40,512]{1,0:T(8,128)S(1)} %get-tuple-element.60.fixed_ref, f32[8,512]{1,0:T(8,128)S(1)} %get-tuple-element.51.mine_ref.stat_ref, ...), custom_call_target="tpu_custom_call" | custom-call | flops 1000000000 | bytes 1048576 | tf_op jit(solution)/shard_map/last/pallas_call | solution.py:586
  40.0 0.0 collective-permute-done.1.other_ref
  40.0 0.7 %join.1 = (f32[1,1024]{1,0:T(1,128)}, f32[1,1024]{1,0:T(1,128)}) custom-call(s32[1]{0:T(128)} %bitcast.__.side_ref.rep_ref, bf16[16,8,128]{2,1,0:T(8,128)(2,1)S(1)} %slice.4.mine_ref, bf16[16,8,128]{2,1,0:T(8,128)(2,1)S(1)} %collective-permute-done.1.other_ref), custom_call_target="tpu_custom_call" | custom-call | flops 1000000 | bytes 1048576 | tf_op jit(solution)/shard_map/join/pallas_call | solution.py:586
  (1 shorter events, 0.0 us)
Async XLA Ops:
  23.4 4.8 %collective-permute-start = (f32[8,512]{1,0:T(8,128)S(1)}, f32[8,512]{1,0:T(8,128)S(1)}, u32[]{:S(2)}, u32[]{:S(2)}) collective-permute-start(f32[8,512]{1,0:T(8,128)S(1)} %get-tuple-element.51.mine_ref.stat_ref), channel_id=1, source_target_pairs={{0,1},{1,0},{2,3},{3,2},{4,5},{5,4},{6,7},{7,6},{8,9},{9,8},{10,11... | collective-permute-start | bytes 49160 | tf_op jit(solution)/shard_map/ppermute | solution.py:639
  23.4 15.3 %all-to-all-start.1 = ((bf16[16,80,128]{2,1,0:T(8,128)(2,1)}), bf16[16,80,128]{2,1,0:T(8,128)(2,1)S(1)}, u32[]{:S(2)}, u32[]{:S(2)}) async-start(bf16[16,80,128]{2,1,0:T(8,128)(2,1)} %get-tuple-element.53), calls=%async_computation.1 | async-start | bytes 655360 | tf_op jit(solution)/shard_map/all_to_all | solution.py:636
  28.2 0.7 %copy-start = (s32[256]{0:T(256)S(1)}, s32[256]{0:T(256)}, u32[]{:S(2)}) copy-start(s32[256]{0:T(256)} %param.10) | copy-start | bytes 3076
  28.2 0.7 %copy-start.1 = (f32[128]{0:T(128)S(1)}, f32[128]{0:T(128)}, u32[]{:S(2)}) copy-start(f32[128]{0:T(128)} %param.18) | copy-start | bytes 1540
  38.8 1.2 %collective-permute-start.1 = (bf16[16,8,128]{2,1,0:T(8,128)(2,1)S(1)}, bf16[16,8,128]{2,1,0:T(8,128)(2,1)S(1)}, u32[]{:S(2)}, u32[]{:S(2)}) collective-permute-start(bf16[16,8,128]{2,1,0:T(8,128)(2,1)S(1)} %slice.4.mine_ref), channel_id=1, source_target_pairs={{0,1},{1,0},{2,3},{3,2},{4,5},{5,4},{6,7},{7,6},{8,9},{9,8},{10,11... | collective-permute-start | bytes 98312 | tf_op jit(solution)/shard_map/ppermute | solution.py:639
